TPU v7x, 8 devices: a whole 2x2x1 slice. The times are simulated.
8 devices in a mesh: sp: 8 (over z, y, x, core).
Axes of the slice: x: 2, y: 2, z: 1, core: 2. Of those that a mesh axis runs over, the one named last changes fastest.
Arguments:
- hidden_in: bfloat16 [32, 512, 1024], P(None, 'sp')
- grad_out: bfloat16 [32, 512, 1024], P(None, 'sp')
- positions: int32 [32, 512], P(None, 'sp')
- w_q: bfloat16 [1024, 2048], replicated
- w_k: bfloat16 [1024, 1024], replicated
- w_v: bfloat16 [1024, 1024], replicated
- w_o: bfloat16 [2048, 1024], replicated
- g_in: bfloat16 [1024], replicated
- q_norm: bfloat16 [128], replicated
- k_norm: bfloat16 [128], replicated
Outputs:
- output 1: bfloat16 [32, 512, 1024], P(None, 'sp')
- output 2: bfloat16 [32, 512, 1024], P(None, 'sp')
- output 3: float32 [1024, 2048], replicated
- output 4: float32 [1024, 1024], replicated
- output 5: float32 [1024, 1024], replicated
- output 6: float32 [2048, 1024], replicated
- output 7: float32 [1024], replicated
- output 8: float32 [128], replicated
- output 9: float32 [128], replicated
All inputs are finite; a program needn't handle non-finite values.
Results may differ from a plain program's by a relative error of at most 0.0140917.
Values are sent between devices in bfloat16 or wider.
A program may use at most 1 GiB of HBM per device.

v0:
```python
import functools
import jax
import jax.numpy as jnp
from jax import lax
from jax.sharding import PartitionSpec as P

EPSILON = 1e-6
ROPE_THETA = 1000000.0
NEG_LARGE = -1e30
ROW_CONTRACT = (((0,), (0,)), ((), ()))
COL_CONTRACT = (((1,), (1,)), ((), ()))


def rope_tables(positions, head_dim):
    exponents = jnp.arange(0, head_dim, 2).astype(jnp.float32) / head_dim
    inv_freq = jnp.power(ROPE_THETA, -exponents)
    angles = positions.astype(jnp.float32)[:, :, None] * inv_freq
    return jnp.cos(angles)[:, :, None, :], jnp.sin(angles)[:, :, None, :]


def rotate_half(values, rope_cos, rope_sin):
    half = values.shape[-1] // 2
    first = values[..., :half]
    second = values[..., half:]
    return jnp.concatenate([first * rope_cos - second * rope_sin, second * rope_cos + first * rope_sin], axis=-1)


def rms_scale(values):
    return values * lax.rsqrt(jnp.mean(values * values, axis=-1, keepdims=True) + EPSILON)


def input_norm(tokens_f32, gain):
    return rms_scale(tokens_f32) * gain


def norm_rotate(projected, gain, rope_cos, rope_sin):
    return rotate_half(rms_scale(projected) * gain, rope_cos, rope_sin)


def spread_heads(values, copies):
    if copies == 1:
        return values
    batch, seq_dev, kv_heads, head_dim = values.shape
    wide = jnp.broadcast_to(values[:, :, :, None, :], (batch, seq_dev, kv_heads, copies, head_dim))
    return wide.reshape(batch, seq_dev, kv_heads * copies, head_dim)


def merge_heads(values, copies):
    batch, seq_dev, wide_heads, head_dim = values.shape
    return values.astype(jnp.float32).reshape(batch, seq_dev, wide_heads // copies, copies, head_dim).sum(axis=3)


def attend(q_grp, k_att, v_att, scale):
    seq_len = q_grp.shape[1]
    causal = jnp.arange(seq_len)[:, None] >= jnp.arange(seq_len)[None, :]
    scores = jnp.einsum('bqgrd,bkgd->bgrqk', q_grp, k_att, preferred_element_type=jnp.float32) * scale
    scores = jnp.where(causal, scores, NEG_LARGE)
    weights = jnp.exp(scores - jnp.max(scores, axis=-1, keepdims=True))
    prob_f32 = weights / jnp.sum(weights, axis=-1, keepdims=True)
    prob_bf16 = prob_f32.astype(jnp.bfloat16)
    attended = jnp.einsum('bgrqk,bkgd->bqgrd', prob_bf16, v_att, preferred_element_type=jnp.float32)
    return prob_f32, prob_bf16, attended.astype(jnp.bfloat16)


def attend_back(d_grp, q_grp, k_att, v_att, prob_f32, prob_bf16, scale):
    grad_v = jnp.einsum('bgrqk,bqgrd->bkgd', prob_bf16, d_grp, preferred_element_type=jnp.float32)
    grad_prob = jnp.einsum('bqgrd,bkgd->bgrqk', d_grp, v_att, preferred_element_type=jnp.float32)
    grad_scores = prob_f32 * (grad_prob - jnp.sum(prob_f32 * grad_prob, axis=-1, keepdims=True)) * scale
    scores_bf16 = grad_scores.astype(jnp.bfloat16)
    grad_q = jnp.einsum('bgrqk,bkgd->bqgrd', scores_bf16, k_att, preferred_element_type=jnp.float32)
    grad_k = jnp.einsum('bgrqk,bqgrd->bkgd', scores_bf16, q_grp, preferred_element_type=jnp.float32)
    return grad_q, grad_k, grad_v


def solution(mesh):
    group_size = mesh.shape['sp']
    seq_spec = P(None, 'sp', None)
    replicated = P()

    def shard_body(hidden_in, grad_out, positions, w_q, w_k, w_v, w_o, g_in, q_norm, k_norm):
        batch, seq_dev, model_dim = hidden_in.shape
        head_dim = q_norm.shape[0]
        heads = w_o.shape[0] // head_dim
        kv_heads = w_k.shape[1] // head_dim
        copies = max(1, group_size // kv_heads)
        heads_dev = heads // group_size
        kv_dev = kv_heads * copies // group_size
        per_kv = heads_dev // kv_dev
        seq_len = seq_dev * group_size
        tokens = batch * seq_dev
        scale = head_dim ** -0.5
        rope_cos, rope_sin = rope_tables(positions, head_dim)
        head_rope = functools.partial(norm_rotate, rope_cos=rope_cos, rope_sin=rope_sin)

        x_f32 = hidden_in.astype(jnp.float32)
        normed, norm_pull = jax.vjp(input_norm, x_f32, g_in.astype(jnp.float32))
        hidden = normed.astype(jnp.bfloat16).reshape(tokens, model_dim)
        q_proj = jnp.dot(hidden, w_q, preferred_element_type=jnp.float32).reshape(batch, seq_dev, heads, head_dim)
        k_proj = jnp.dot(hidden, w_k, preferred_element_type=jnp.float32).reshape(batch, seq_dev, kv_heads, head_dim)
        v_proj = jnp.dot(hidden, w_v, preferred_element_type=jnp.float32).astype(jnp.bfloat16).reshape(batch, seq_dev, kv_heads, head_dim)
        q_rot, q_pull = jax.vjp(head_rope, q_proj, q_norm.astype(jnp.float32))
        k_rot, k_pull = jax.vjp(head_rope, k_proj, k_norm.astype(jnp.float32))

        q_att = lax.all_to_all(q_rot.astype(jnp.bfloat16), 'sp', 2, 1, tiled=True)
        k_att = lax.all_to_all(spread_heads(k_rot.astype(jnp.bfloat16), copies), 'sp', 2, 1, tiled=True)
        v_att = lax.all_to_all(spread_heads(v_proj, copies), 'sp', 2, 1, tiled=True)
        q_grp = q_att.reshape(batch, seq_len, kv_dev, per_kv, head_dim)
        prob_f32, prob_bf16, attended = attend(q_grp, k_att, v_att, scale)
        attn_loc = lax.all_to_all(attended.reshape(batch, seq_len, heads_dev, head_dim), 'sp', 1, 2, tiled=True)
        attn_flat = attn_loc.reshape(tokens, heads * head_dim)
        mixed = jnp.dot(attn_flat, w_o, preferred_element_type=jnp.float32).reshape(batch, seq_dev, model_dim)
        hidden_out = (x_f32 + mixed).astype(jnp.bfloat16)

        dy_flat = grad_out.reshape(tokens, model_dim)
        grad_wo = lax.dot_general(attn_flat, dy_flat, ROW_CONTRACT, preferred_element_type=jnp.float32)
        d_attn = lax.dot_general(dy_flat, w_o, COL_CONTRACT, preferred_element_type=jnp.float32).astype(jnp.bfloat16)
        d_att = lax.all_to_all(d_attn.reshape(batch, seq_dev, heads, head_dim), 'sp', 2, 1, tiled=True)
        d_grp = d_att.reshape(batch, seq_len, kv_dev, per_kv, head_dim)
        grad_q, grad_k, grad_v = attend_back(d_grp, q_grp, k_att, v_att, prob_f32, prob_bf16, scale)
        dq_loc = lax.all_to_all(grad_q.astype(jnp.bfloat16).reshape(batch, seq_len, heads_dev, head_dim), 'sp', 1, 2, tiled=True)
        dk_loc = merge_heads(lax.all_to_all(grad_k.astype(jnp.bfloat16), 'sp', 1, 2, tiled=True), copies)
        dv_loc = merge_heads(lax.all_to_all(grad_v.astype(jnp.bfloat16), 'sp', 1, 2, tiled=True), copies)
        dq_proj, grad_qn = q_pull(dq_loc.astype(jnp.float32))
        dk_proj, grad_kn = k_pull(dk_loc)
        dq_flat = dq_proj.astype(jnp.bfloat16).reshape(tokens, heads * head_dim)
        dk_flat = dk_proj.astype(jnp.bfloat16).reshape(tokens, kv_heads * head_dim)
        dv_flat = dv_loc.astype(jnp.bfloat16).reshape(tokens, kv_heads * head_dim)
        grad_wq = lax.dot_general(hidden, dq_flat, ROW_CONTRACT, preferred_element_type=jnp.float32)
        grad_wk = lax.dot_general(hidden, dk_flat, ROW_CONTRACT, preferred_element_type=jnp.float32)
        grad_wv = lax.dot_general(hidden, dv_flat, ROW_CONTRACT, preferred_element_type=jnp.float32)
        d_hidden = (lax.dot_general(dq_flat, w_q, COL_CONTRACT, preferred_element_type=jnp.float32)
                    + lax.dot_general(dk_flat, w_k, COL_CONTRACT, preferred_element_type=jnp.float32)
                    + lax.dot_general(dv_flat, w_v, COL_CONTRACT, preferred_element_type=jnp.float32))
        norm_grad, grad_gin = norm_pull(d_hidden.reshape(batch, seq_dev, model_dim))
        grad_in = (grad_out.astype(jnp.float32) + norm_grad).astype(jnp.bfloat16)
        summed = lax.psum((grad_wq, grad_wk, grad_wv, grad_wo, grad_gin, grad_qn, grad_kn), 'sp')
        return (hidden_out, grad_in) + tuple(summed)

    return jax.shard_map(shard_body, mesh=mesh,
                         in_specs=(seq_spec, seq_spec, P(None, 'sp'), replicated, replicated, replicated, replicated, replicated, replicated, replicated),
                         out_specs=(seq_spec, seq_spec, replicated, replicated, replicated, replicated, replicated, replicated, replicated),
                         check_vma=False)
```

profile of v0, /device:TPU:0, one launch (start us, length us, event | category | flops | bytes accessed | tf_op | source)
XLA Modules:
  0.0 1301.3 jit_solution(1400990223245042825)
XLA Ops:
  77.3 16.3 %all-to-all-done.1 = bf16[32,64,8,128]{3,1,0,2:T(8,128)(2,1)} async-done(((bf16[32,64,8,128]{3,1,0,2:T(8,128)(2,1)}), bf16[32,64,8,128]{3,1,0,2:T(8,128)(2,1)}, u32[]{:S(2)}, u32[]{:S(2)}) %all-to-all-start.1) | async-done | bytes 4194336 | tf_op jit(solution)/shard_map/all_to_all | solution.py:105
  192.5 61.1 %all-to-all-done.2 = bf16[32,64,16,128]{3,1,0,2:T(8,128)(2,1)} async-done(((bf16[32,64,16,128]{3,1,0,2:T(8,128)(2,1)}), bf16[32,64,16,128]{3,1,0,2:T(8,128)(2,1)}, u32[]{:S(2)}, u32[]{:S(2)}) %all-to-all-start.2) | async-done | bytes 8388640 | tf_op jit(solution)/shard_map/all_to_all | solution.py:104
  278.8 72.9 %all-to-all-done.4 = bf16[32,64,16,128]{3,1,0,2:T(8,128)(2,1)} async-done(((bf16[32,64,16,128]{3,1,0,2:T(8,128)(2,1)}), bf16[32,64,16,128]{3,1,0,2:T(8,128)(2,1)}, u32[]{:S(2)}, u32[]{:S(2)}) %all-to-all-start.4) | async-done | bytes 8388640 | tf_op jit(solution)/shard_map/all_to_all | solution.py:117
  361.5 27.7 %fusion.6 = (f32[32,2,512]{2,1,0:T(2,128)S(1)}, f32[32,512,512,2]{2,1,3,0:T(8,128)}) fusion(pred[512,512]{0,1:T(8,128)(4,1)S(1)} %iota_compare_fusion, bf16[32,512,128,1]{2,1,3,0:T(8,128)(2,1)} %bitcast.218, bf16[32,512,2,128]{3,1,2,0:T(8,128)(2,1)} %bitcast.214), kind=kOutput, calls=%fused_computation.10 | convolution fusion | flops 4345266176 | bytes 80084992 | tf_op jit(solution)/shard_map/bqgrd,bkgd->bgrqk/dot_general | solution.py:56
  389.2 21.7 %fusion.5 = f32[32,2,512]{2,1,0:T(2,128)S(1)} fusion(f32[32,512,512,2]{2,1,3,0:T(8,128)} %get-tuple-element.37, f32[32,2,512]{2,1,0:T(2,128)S(1)} %get-tuple-element.36, pred[512,512]{0,1:T(8,128)(4,1)S(1)} %iota_compare_fusion), kind=kLoop, calls=%fused_computation.9 | loop fusion | flops 67076096 | bytes 67633152 | tf_op jit(solution)/shard_map/reduce_sum | solution.py:59
  410.9 49.3 %fusion = (f32[32,2,512]{2,1,0:T(2,128)S(1)}, f32[32,512,512,2]{2,1,3,0:T(8,128)}) fusion(f32[32,2,512]{2,1,0:T(2,128)S(1)} %fusion.5, f32[32,2,512]{2,1,0:T(2,128)S(1)} %get-tuple-element.36, f32[32,512,512,2]{2,1,3,0:T(8,128)} %get-tuple-element.37, pred[512,512]{0,1:T(8,128)(4,1)S(1)} %iota_compare_fusion, bf16[32,512,128,1]{2,1,3,0:T(8,128)(2,1)} %bitcast.236, ...), kind=kOutput, calls=%fused_computation.3 | convolution fusion | flops 4395597824 | bytes 147456000 | tf_op jit(solution)/shard_map/bqgrd,bkgd->bgrqk/dot_general | solution.py:67
  460.1 53.6 %fusion.7 = bf16[32,2,512,512]{2,3,1,0:T(8,128)(2,1)} fusion(f32[32,512,512,2]{2,1,3,0:T(8,128)} %get-tuple-element.39, f32[32,2,512]{2,1,0:T(2,128)S(1)} %get-tuple-element.38, f32[32,2,512]{2,1,0:T(2,128)S(1)} %fusion.5, f32[32,2,512]{2,1,0:T(2,128)S(1)} %get-tuple-element.36, f32[32,512,512,2]{2,1,3,0:T(8,128)} %get-tuple-element.37, ...), kind=kLoop, calls=%fused_computation.11 | loop fusion | flops 134217728 | bytes 168427520 | tf_op jit(solution)/shard_map/reshape.16
  513.7 19.8 %fusion.32 = bf16[32,512,1,128]{1,3,0,2:T(8,128)(2,1)} fusion(bf16[32,512,2,128]{3,1,2,0:T(8,128)(2,1)} %bitcast.215, bf16[32,2,512,512]{2,3,1,0:T(8,128)(2,1)} %fusion.7), kind=kOutput, calls=%fused_computation.68 | convolution fusion | flops 4297064448 | bytes 46137344 | tf_op jit(solution)/shard_map/bgrqk,bqgrd->bkgd/dot_general | solution.py:71
  544.6 30.7 %fusion.33 = bf16[32,512,1,128]{1,3,0,2:T(8,128)(2,1)} fusion(bf16[32,512,2,128]{3,1,2,0:T(8,128)(2,1)} %bitcast.230, f32[32,2,512]{2,1,0:T(2,128)S(1)} %fusion.5, f32[32,2,512]{2,1,0:T(2,128)S(1)} %get-tuple-element.36, f32[32,512,512,2]{2,1,3,0:T(8,128)} %get-tuple-element.37, pred[512,512]{0,1:T(8,128)(4,1)S(1)} %iota_compare_fusion), kind=kOutput, calls=%fused_computation.69 | convolution fusion | flops 4380950528 | bytes 80216064 | tf_op jit(solution)/shard_map/bgrqk,bqgrd->bkgd/dot_general | solution.py:66
  597.4 17.8 %convert_bitcast_fusion.1 = bf16[32,512,2,128]{1,3,2,0:T(8,128)(2,1)} fusion(bf16[32,512,128,1]{2,1,3,0:T(8,128)(2,1)} %bitcast.219, bf16[32,2,512,512]{2,3,1,0:T(8,128)(2,1)} %fusion.7), kind=kOutput, calls=%fused_computation.59 | convolution fusion | flops 4299161600 | bytes 46137344 | tf_op jit(solution)/shard_map/bgrqk,bkgd->bqgrd/dot_general | solution.py:70
  615.2 21.2 %copy.75 = bf16[32,512,2,128]{3,2,0,1:T(2,128)(2,1)} copy(bf16[32,512,2,128]{1,3,2,0:T(8,128)(2,1)} %convert_bitcast_fusion.1) | data formatting | bytes 16777216 | tf_op jit(solution)/shard_map/reshape | solution.py:120
  650.1 29.6 %convert_bitcast_fusion.3 = bf16[32,512,2,128]{1,3,2,0:T(8,128)(2,1)} fusion(bf16[32,512,128,1]{2,1,3,0:T(8,128)(2,1)} %bitcast.237, f32[32,2,512]{2,1,0:T(2,128)S(1)} %fusion.5, f32[32,2,512]{2,1,0:T(2,128)S(1)} %get-tuple-element.36, f32[32,512,512,2]{2,1,3,0:T(8,128)} %get-tuple-element.37, pred[512,512]{0,1:T(8,128)(4,1)S(1)} %iota_compare_fusion), kind=kOutput, calls=%fused_computation.61 | convolution fusion | flops 4383047680 | bytes 80216064 | tf_op jit(solution)/shard_map/bgrqk,bkgd->bqgrd/dot_general | solution.py:61
  679.6 21.1 %copy.68 = bf16[32,512,2,128]{3,2,0,1:T(2,128)(2,1)} copy(bf16[32,512,2,128]{1,3,2,0:T(8,128)(2,1)} %convert_bitcast_fusion.3) | data formatting | bytes 16777216 | tf_op jit(solution)/shard_map/reshape | solution.py:109
  773.5 16.5 %copy.76 = bf16[32,512,2,128]{3,1,2,0:T(8,128)(2,1)} copy(bf16[32,512,2,128]{3,2,0,1:T(2,128)(2,1)} %all-to-all-done.5) | data formatting | bytes 16777216 | tf_op jit(solution)/shard_map/all_to_all | solution.py:120
  813.8 25.5 %multiply_add_fusion.1 = (f32[32,64,16,64]{3,1,2,0:T(8,128)}, f32[32,64,16,64]{3,1,2,0:T(8,128)}) fusion(f32[32,64,16,128]{3,1,2,0:T(8,128)} %bitcast.213, f32[32,64,64]{2,1,0:T(8,128)S(1)} %copy-done.9, f32[32,64,64]{2,1,0:T(8,128)S(1)} %copy-done.6), kind=kLoop, calls=%fused_computation.24 | loop fusion | flops 14680064 | bytes 34603008 | tf_op jit(solution)/shard_map/transpose(jvp())/add_any | solution.py:25
  839.3 17.9 %multiply_reduce_fusion = (f32[128]{0:T(128)S(1)}, f32[32,64,16]{1,2,0:T(8,128)S(1)}) fusion(f32[32,64,16,128]{3,1,2,0:T(8,128)S(1)} %bitcast.212, f32[32,64,16]{1,2,0:T(8,128)} %copy-done.10, f32[32,64,16,64]{3,1,2,0:T(8,128)} %get-tuple-element.23, f32[32,64,16,64]{3,1,2,0:T(8,128)} %get-tuple-element.22, f32[128]{0:T(128)S(1)} %copy-done.37), kind=kLoop, calls=%fused_computation.20 | loop fusion | flops 29327232 | bytes 33817600 | tf_op jit(solution)/shard_map/transpose(jvp())/reduce_sum | solution.py:37
  857.3 19.9 %fusion.13 = bf16[32,64,16,128]{3,1,2,0:T(8,128)(2,1)} fusion(f32[32,64,16,128]{3,1,2,0:T(8,128)} %get-tuple-element.35, f32[32,64,16]{1,2,0:T(8,128)S(1)} %multiply_multiply_fusion.2, f32[128]{0:T(128)S(1)} %copy-done.37, f32[32,64,16]{1,2,0:T(8,128)S(1)} %copy-done.11, f32[32,64,16,64]{3,1,2,0:T(8,128)} %get-tuple-element.23, ...), kind=kLoop, calls=%fused_computation.18 | loop fusion | flops 29360128 | bytes 42205696 | tf_op jit(solution)/shard_map/convert_element_type | solution.py:125
  877.2 23.5 %copy.78 = bf16[32,64,16,128]{3,2,1,0:T(8,128)(2,1)} copy(bf16[32,64,16,128]{3,1,2,0:T(8,128)(2,1)} %fusion.13) | data formatting | bytes 16777216 | tf_op jit(solution)/shard_map/convert_element_type | solution.py:125
  914.6 16.5 %copy.69 = bf16[32,512,2,128]{3,1,2,0:T(8,128)(2,1)} copy(bf16[32,512,2,128]{3,2,0,1:T(2,128)(2,1)} %all-to-all-done.3) | data formatting | bytes 16777216 | tf_op jit(solution)/shard_map/all_to_all | solution.py:109
  931.1 16.2 %copy.70 = bf16[32,64,8,2,128]{4,3,2,1,0:T(2,128)(2,1)} copy(bf16[32,64,8,2,128]{4,1,2,3,0:T(8,128)(2,1)} %bitcast.222) | data formatting | bytes 16777216 | tf_op jit(solution)/shard_map/all_to_all | solution.py:109
  961.7 14.8 %fusion.63 = f32[2048,1024]{1,0:T(8,128)} fusion(bf16[2048,2048]{1,0:T(8,128)(2,1)} %reshape.228, bf16[2048,1024]{1,0:T(8,128)(2,1)} %bitcast.244), kind=kOutput, calls=%fused_computation.103 | convolution fusion | flops 8589934592 | bytes 20971520 | tf_op jit(solution)/shard_map/dot_general | solution.py:115
  1000.0 14.8 %fusion.26 = f32[2048,1024]{1,0:T(8,128)} fusion(bf16[1024,2048]{1,0:T(8,128)(2,1)} %param.13, bf16[256,8,16,128]{3,2,1,0:T(8,128)(2,1)} %bitcast.228), kind=kOutput, calls=%fused_computation.48 | convolution fusion | flops 8589934592 | bytes 20971520 | tf_op jit(solution)/shard_map/dot_general | solution.py:131
  1031.3 24.2 %all-reduce.4 = (f32[1024]{0:T(1024)}, f32[128]{0:T(128)}, f32[128]{0:T(128)}) all-reduce(f32[1024]{0:T(1024)S(1)} %get-tuple-element.13, f32[128]{0:T(128)S(1)} %get-tuple-element.9, f32[128]{0:T(128)S(1)} %copy-done.38), channel_id=1, replica_groups=mesh['sp'=8] {'sp'}, use_global_device_ids=true, to_apply=%region_14.15 | all-reduce | flops 1280 | bytes 10240 | tf_op jit(solution)/shard_map/psum | solution.py:136
  1078.0 196.7 %all-reduce.8.cloned.1.call-done = (f32[1024,2048]{1,0:T(8,128)}, f32[1024,1024]{1,0:T(8,128)}, f32[1024,1024]{1,0:T(8,128)}, f32[2048,1024]{1,0:T(8,128)}) async-done(((f32[1024,2048]{1,0:T(8,128)}, f32[1024,1024]{1,0:T(8,128)}, f32[1024,1024]{1,0:T(8,128)}, f32[2048,1024]{1,0:T(8,128)}), (f32[1024,2048]{1,0:T(8,128)}, f32[1024,1024]{1,0:T(8,128)}, f32[1024,1024]{1,0:T(8,128)}, ...) | async-done | bytes 25165840 | tf_op jit(solution)/shard_map/psum | solution.py:136
  (175 shorter events, 456.8 us)
Async XLA Ops:
  7.2 43.6 %copy-start = (bf16[1024,1024]{1,0:T(8,128)(2,1)S(1)}, bf16[1024,1024]{1,0:T(8,128)(2,1)}, u32[]{:S(2)}) copy-start(bf16[1024,1024]{1,0:T(8,128)(2,1)} %param.15) | copy-start | bytes 6291460
  28.5 86.4 %copy-start.5 = (f32[32,64,64]{2,1,0:T(8,128)}, f32[32,64,64]{2,1,0:T(8,128)S(1)}, u32[]{:S(2)}) copy-start(f32[32,64,64]{2,1,0:T(8,128)S(1)} %get-tuple-element.30) | copy-start | bytes 1572868
  40.1 53.5 %all-to-all-start.1 = ((bf16[32,64,8,128]{3,1,0,2:T(8,128)(2,1)}), bf16[32,64,8,128]{3,1,0,2:T(8,128)(2,1)}, u32[]{:S(2)}, u32[]{:S(2)}) async-start(bf16[32,64,8,128]{3,1,0,2:T(8,128)(2,1)} %copy.61), calls=%async_computation.1 | async-start | bytes 8388608 | tf_op jit(solution)/shard_map/all_to_all | solution.py:105
  50.8 56.3 %copy-start.36 = (f32[128]{0:T(128)}, f32[128]{0:T(128)S(1)}, u32[]{:S(2)}) copy-start(f32[128]{0:T(128)S(1)} %convert_element_type.130) | copy-start | bytes 1540
  77.3 37.6 %copy-start.10 = (f32[32,64,16]{1,2,0:T(8,128)}, f32[32,64,16]{1,2,0:T(8,128)S(1)}, u32[]{:S(2)}) copy-start(f32[32,64,16]{1,2,0:T(8,128)S(1)} %fusion.58) | copy-start | bytes 393220
  93.6 62.3 %all-to-all-start = ((bf16[32,64,8,128]{3,1,0,2:T(8,128)(2,1)}), bf16[32,64,8,128]{3,1,0,2:T(8,128)(2,1)}, u32[]{:S(2)}, u32[]{:S(2)}) async-start(bf16[32,64,8,128]{3,1,0,2:T(8,128)(2,1)} %copy.58), calls=%async_computation | async-start | bytes 8388608 | tf_op jit(solution)/shard_map/all_to_all | solution.py:106
  155.9 97.7 %all-to-all-start.2 = ((bf16[32,64,16,128]{3,1,0,2:T(8,128)(2,1)}), bf16[32,64,16,128]{3,1,0,2:T(8,128)(2,1)}, u32[]{:S(2)}, u32[]{:S(2)}) async-start(bf16[32,64,16,128]{3,1,0,2:T(8,128)(2,1)} %copy.64), calls=%async_computation.2 | async-start | bytes 16777216 | tf_op jit(solution)/shard_map/all_to_all | solution.py:104
  253.6 98.1 %all-to-all-start.4 = ((bf16[32,64,16,128]{3,1,0,2:T(8,128)(2,1)}), bf16[32,64,16,128]{3,1,0,2:T(8,128)(2,1)}, u32[]{:S(2)}, u32[]{:S(2)}) async-start(bf16[32,64,16,128]{3,1,0,2:T(8,128)(2,1)} %copy.71), calls=%async_computation.4 | async-start | bytes 16777216 | tf_op jit(solution)/shard_map/all_to_all | solution.py:117
  541.3 52.3 %all-to-all-start.6 = ((bf16[32,512,1,128]{3,0,2,1:T(8,128)(2,1)}), bf16[32,512,1,128]{3,0,2,1:T(8,128)(2,1)}, u32[]{:S(2)}, u32[]{:S(2)}) async-start(bf16[32,512,1,128]{3,0,2,1:T(8,128)(2,1)} %copy.81), calls=%async_computation.6 | async-start | bytes 8388608 | tf_op jit(solution)/shard_map/all_to_all | solution.py:121
  593.6 52.7 %all-to-all-start.7 = ((bf16[32,512,1,128]{3,0,2,1:T(8,128)(2,1)}), bf16[32,512,1,128]{3,0,2,1:T(8,128)(2,1)}, u32[]{:S(2)}, u32[]{:S(2)}) async-start(bf16[32,512,1,128]{3,0,2,1:T(8,128)(2,1)} %copy.86), calls=%async_computation.7 | async-start | bytes 8388608 | tf_op jit(solution)/shard_map/all_to_all | solution.py:122
  646.4 122.9 %all-to-all-start.5 = ((bf16[32,512,2,128]{3,2,0,1:T(2,128)(2,1)}), bf16[32,512,2,128]{3,2,0,1:T(2,128)(2,1)}, u32[]{:S(2)}, u32[]{:S(2)}) async-start(bf16[32,512,2,128]{3,2,0,1:T(2,128)(2,1)} %copy.75), calls=%async_computation.5 | async-start | bytes 16777216 | tf_op jit(solution)/shard_map/all_to_all | solution.py:120
  743.0 13.8 %copy-start.12 = (bf16[32,64,8,128]{3,2,1,0:T(8,128)(2,1)}, bf16[32,64,8,128]{3,2,1,0:T(8,128)(2,1)S(1)}, u32[]{:S(2)}) copy-start(bf16[32,64,8,128]{3,2,1,0:T(8,128)(2,1)S(1)} %copy.83) | copy-start | bytes 12582916
  743.0 13.8 %copy-start.19 = (bf16[32,64,1024]{2,1,0:T(8,128)(2,1)S(1)}, bf16[32,64,1024]{2,1,0:T(8,128)(2,1)}, u32[]{:S(2)}) copy-start(bf16[32,64,1024]{2,1,0:T(8,128)(2,1)} %copy-done.17) | copy-start | bytes 12582916
  769.3 145.3 %all-to-all-start.3 = ((bf16[32,512,2,128]{3,2,0,1:T(2,128)(2,1)}), bf16[32,512,2,128]{3,2,0,1:T(2,128)(2,1)}, u32[]{:S(2)}, u32[]{:S(2)}) async-start(bf16[32,512,2,128]{3,2,0,1:T(2,128)(2,1)} %copy.68), calls=%async_computation.3 | async-start | bytes 16777216 | tf_op jit(solution)/shard_map/all_to_all | solution.py:109
  773.0 501.7 %all-reduce.8.cloned.1.call-start = ((), (), s32[]{:S(2)}) async-start(), calls=%async_computation.8 | async-start | bytes 50331648 | tf_op jit(solution)/shard_map/psum | solution.py:136
  813.7 25.5 %slice-start = ((s8[16777216]{0:T(1024)(128)(4,1)}), s8[4194304]{0:T(1024)(128)(4,1)S(1)}, s32[]{:S(2)}) async-start(s8[16777216]{0:T(1024)(128)(4,1)} %bitcast.211), calls=%async_computation.9 | async-start | bytes 8388608
  813.7 25.5 %slice-start.1 = ((s8[16777216]{0:T(1024)(128)(4,1)}), s8[4194304]{0:T(1024)(128)(4,1)S(1)}, s32[]{:S(2)}) async-start(s8[16777216]{0:T(1024)(128)(4,1)} %bitcast.211), calls=%async_computation.10 | async-start | bytes 8388608
  813.7 25.5 %slice-start.2 = ((s8[16777216]{0:T(1024)(128)(4,1)}), s8[4194304]{0:T(1024)(128)(4,1)S(1)}, s32[]{:S(2)}) async-start(s8[16777216]{0:T(1024)(128)(4,1)} %bitcast.211), calls=%async_computation.11 | async-start | bytes 8388608
  813.7 25.5 %slice-start.3 = ((s8[16777216]{0:T(1024)(128)(4,1)}), s8[4194304]{0:T(1024)(128)(4,1)S(1)}, s32[]{:S(2)}) async-start(s8[16777216]{0:T(1024)(128)(4,1)} %bitcast.211), calls=%async_computation.12 | async-start | bytes 8388608
  813.7 25.5 %copy-start.37 = (f32[128]{0:T(128)S(1)}, f32[128]{0:T(128)}, u32[]{:S(2)}) copy-start(f32[128]{0:T(128)} %copy-done.36) | copy-start | bytes 1540
  839.3 17.9 %copy-start.25 = (f32[32,64,16]{1,2,0:T(8,128)S(1)}, f32[32,64,16]{1,2,0:T(8,128)}, u32[]{:S(2)}) copy-start(f32[32,64,16]{1,2,0:T(8,128)} %copy-done.24) | copy-start | bytes 393220
  839.3 18.0 %copy-start.11 = (f32[32,64,16]{1,2,0:T(8,128)S(1)}, f32[32,64,16]{1,2,0:T(8,128)}, u32[]{:S(2)}) copy-start(f32[32,64,16]{1,2,0:T(8,128)} %copy-done.10) | copy-start | bytes 393220
  877.2 23.5 %copy-start.20 = (bf16[32,64,1024]{2,1,0:T(8,128)(2,1)S(1)}, bf16[32,64,1024]{2,1,0:T(8,128)(2,1)}, u32[]{:S(2)}) copy-start(bf16[32,64,1024]{2,1,0:T(8,128)(2,1)} %copy-done.17) | copy-start | bytes 12582916
  1027.9 27.6 %copy-start.31 = (f32[32,64]{1,0:T(8,128)S(1)}, f32[32,64]{1,0:T(8,128)}, u32[]{:S(2)}) copy-start(f32[32,64]{1,0:T(8,128)} %copy-done.30) | copy-start | bytes 24580
  (33 other events, 238.3 us)
Sparse Core Ops, SparseCore 0:
  976.7 297.9 all-reduce.7
where the time goes:
time: 1310 us; the launch traced here: 1300 us
  waiting for transfers between devices  379 us (29%)
  matrix products  306 us (23%)
  local copies, waits for them, and re-layouts  299 us (23%)
  other arithmetic  237 us (18%)
  starting transfers between devices  40.5 us (3%)
  blocking collectives  24.2 us (2%)
  between operations  15.3 us (1%)
    psum x1, waiting for transfers between devices, shard_body(): lax.psum((grad_wq, grad_wk, grad_wv, grad_wo, grad_gin, grad_qn, grad_kn)...  197 us
    all_to_all x1, waiting for transfers between devices, shard_body(): lax.all_to_all(d_attn.reshape(batch, seq_dev, heads, head_dim), 'sp', 2,...  72.9 us
    another operation x3, other arithmetic  66.1 us
    all_to_all x1, waiting for transfers between devices, shard_body(): q_att = lax.all_to_all(q_rot.astype(jnp.bfloat16), 'sp', 2, 1, tiled=True)  61.1 us
    dot_general x1, matrix products, attend_back(): jnp.einsum('bqgrd,bkgd->bgrqk', d_grp, v_att, preferred_element_type=jnp....  49.3 us
    add_any x2, other arithmetic, rotate_half(): second * rope_sin  34.2 us
    unnamed x102, local copies, waits for them, and re-layouts  32.9 us
    all_to_all x2, local copies, waits for them, and re-layouts, shard_body(): lax.all_to_all(attended.reshape(batch, seq_len, heads_dev, head_dim), 'sp...  32.7 us
  transfers between devices with their start and end apart: 9, of which 7 were waited for; matrix products, arithmetic and copies ran while one was open for 41% of the time, Pallas kernels for 0%

commit v1 on v0

v1 whole, which is shorter than its diff:
```python
import functools
import jax
import jax.numpy as jnp
from jax import lax
from jax.experimental import pallas as pl
from jax.experimental.pallas import tpu as pltpu
from jax.sharding import PartitionSpec as P

EPSILON = 1e-6
ROPE_THETA = 1000000.0
NEG_LARGE = -1e30
NT = (((1,), (1,)), ((), ()))
TN = (((0,), (0,)), ((), ()))
ROW_BLOCK = 256


def dot(a, b, dims=(((1,), (0,)), ((), ()))):
    return lax.dot_general(a, b, dims, preferred_element_type=jnp.float32)


def rope_tables(positions, head_dim):
    exponents = jnp.arange(0, head_dim, 2).astype(jnp.float32) / head_dim
    inv_freq = jnp.power(ROPE_THETA, -exponents)
    angles = positions.astype(jnp.float32)[:, :, None] * inv_freq
    cos, sin = jnp.cos(angles), jnp.sin(angles)
    return jnp.concatenate([cos, cos], axis=-1), jnp.concatenate([-sin, sin], axis=-1)


def block_kernel(x_ref, dy_ref, cos_ref, sin_ref, gin_ref, qn_ref, kn_ref, wq_ref, wk_ref, wv_ref, wo_ref,
                 out_ref, gi_ref, h_ref, o_ref, dq_ref, dk_ref, dv_ref, dgin_ref, dqn_ref, dkn_ref,
                 out_acc, dh_acc):
    seq, group = pl.program_id(0), pl.program_id(1)
    groups = pl.num_programs(1)
    head_dim = qn_ref.shape[1]
    per_kv = wq_ref.shape[1] // head_dim
    seq_len = x_ref.shape[1]
    scale = head_dim ** -0.5
    half = head_dim // 2

    @pl.when((seq == 0) & (group == 0))
    def _():
        dgin_ref[...] = jnp.zeros_like(dgin_ref)
        dqn_ref[...] = jnp.zeros_like(dqn_ref)
        dkn_ref[...] = jnp.zeros_like(dkn_ref)

    @pl.when(group == 0)
    def _():
        x = x_ref[0].astype(jnp.float32)
        inv = lax.rsqrt(jnp.mean(x * x, axis=-1, keepdims=True) + EPSILON)
        h_ref[0] = (x * inv * gin_ref[...]).astype(jnp.bfloat16)
        out_acc[...] = jnp.zeros_like(out_acc)
        dh_acc[...] = jnp.zeros_like(dh_acc)

    cos, sin = cos_ref[0], sin_ref[0]

    def norm_rotate(t, gain):
        inv = lax.rsqrt(jnp.mean(t * t, axis=-1, keepdims=True) + EPSILON)
        unit = t * inv
        scaled = unit * gain
        return (scaled * cos + pltpu.roll(scaled, half, 1) * sin).astype(jnp.bfloat16), unit, inv

    def norm_rotate_back(grad, unit, inv, gain):
        d_scaled = grad * cos - pltpu.roll(grad, half, 1) * sin
        d_gain = jnp.sum(d_scaled * unit, axis=0, keepdims=True)
        d_unit = d_scaled * gain
        return inv * (d_unit - unit * jnp.mean(d_unit * unit, axis=-1, keepdims=True)), d_gain

    h = h_ref[0]
    dy = dy_ref[0]
    q_proj = dot(h, wq_ref[...])
    k_proj = dot(h, wk_ref[...])
    v = dot(h, wv_ref[...]).astype(jnp.bfloat16)
    d_o = dot(dy, wo_ref[...], NT).astype(jnp.bfloat16)
    k_rot, k_unit, k_inv = norm_rotate(k_proj, kn_ref[...])

    blocks = seq_len // ROW_BLOCK
    dk_parts = [None] * blocks
    dv_parts = [None] * blocks
    rows_id = lax.broadcasted_iota(jnp.int32, (ROW_BLOCK, ROW_BLOCK), 0)
    cols_id = lax.broadcasted_iota(jnp.int32, (ROW_BLOCK, ROW_BLOCK), 1)
    causal = rows_id >= cols_id
    dqn_sum = None
    for head in range(per_kv):
        lanes = slice(head * head_dim, (head + 1) * head_dim)
        q_rot, q_unit, q_inv = norm_rotate(q_proj[:, lanes], qn_ref[...])
        do_head = d_o[:, lanes]
        dq_rows = []
        o_rows = []
        for i in range(blocks):
            rows = slice(i * ROW_BLOCK, (i + 1) * ROW_BLOCK)
            q_i, do_i = q_rot[rows], do_head[rows]
            s_parts = []
            for j in range(i + 1):
                s = dot(q_i, k_rot[j * ROW_BLOCK:(j + 1) * ROW_BLOCK], NT)
                if j == i:
                    s = jnp.where(causal, s, NEG_LARGE)
                s_parts.append(s)
            top = functools.reduce(jnp.maximum, [jnp.max(s, axis=-1, keepdims=True) for s in s_parts])
            e_parts = [jnp.exp((s - top) * scale) for s in s_parts]
            total = functools.reduce(jnp.add, [jnp.sum(e, axis=-1, keepdims=True) for e in e_parts])
            recip = 1.0 / total
            p_parts = [e * recip for e in e_parts]
            pb_parts = [p.astype(jnp.bfloat16) for p in p_parts]
            o_i = None
            for j in range(i + 1):
                part = dot(pb_parts[j], v[j * ROW_BLOCK:(j + 1) * ROW_BLOCK])
                o_i = part if o_i is None else o_i + part
            o_rows.append(o_i.astype(jnp.bfloat16))
            dp_parts = [dot(do_i, v[j * ROW_BLOCK:(j + 1) * ROW_BLOCK], NT) for j in range(i + 1)]
            delta = functools.reduce(jnp.add, [jnp.sum(p * dp, axis=-1, keepdims=True) for p, dp in zip(p_parts, dp_parts)])
            ds_parts = [(p * (dp - delta)).astype(jnp.bfloat16) for p, dp in zip(p_parts, dp_parts)]
            dq_i = None
            for j in range(i + 1):
                cols = slice(j * ROW_BLOCK, (j + 1) * ROW_BLOCK)
                part = dot(ds_parts[j], k_rot[cols])
                dq_i = part if dq_i is None else dq_i + part
                dk_j = dot(ds_parts[j], q_i, TN)
                dv_j = dot(pb_parts[j], do_i, TN)
                dk_parts[j] = dk_j if dk_parts[j] is None else dk_parts[j] + dk_j
                dv_parts[j] = dv_j if dv_parts[j] is None else dv_parts[j] + dv_j
            dq_rows.append(dq_i)
        o_ref[0, :, lanes] = jnp.concatenate(o_rows, axis=0)
        dq_head, d_gain = norm_rotate_back(jnp.concatenate(dq_rows, axis=0) * scale, q_unit, q_inv, qn_ref[...])
        dqn_sum = d_gain if dqn_sum is None else dqn_sum + d_gain
        dq_ref[0, :, lanes] = dq_head.astype(jnp.bfloat16)
    dqn_ref[...] += dqn_sum
    dk_head, d_gain = norm_rotate_back(jnp.concatenate(dk_parts, axis=0) * scale, k_unit, k_inv, kn_ref[...])
    dkn_ref[...] += d_gain
    dk_ref[0] = dk_head.astype(jnp.bfloat16)
    dv_ref[0] = jnp.concatenate(dv_parts, axis=0).astype(jnp.bfloat16)
    out_acc[...] += dot(o_ref[0], wo_ref[...])
    dh_acc[...] += dot(dq_ref[0], wq_ref[...], NT) + dot(dk_ref[0], wk_ref[...], NT) + dot(dv_ref[0], wv_ref[...], NT)

    @pl.when(group == groups - 1)
    def _():
        x = x_ref[0].astype(jnp.float32)
        out_ref[0] = (x + out_acc[...]).astype(jnp.bfloat16)
        inv = lax.rsqrt(jnp.mean(x * x, axis=-1, keepdims=True) + EPSILON)
        unit = x * inv
        d_norm = dh_acc[...]
        dgin_ref[...] += jnp.sum(d_norm * unit, axis=0, keepdims=True)
        d_unit = d_norm * gin_ref[...]
        grad = inv * (d_unit - unit * jnp.mean(d_unit * unit, axis=-1, keepdims=True))
        gi_ref[0] = (dy_ref[0].astype(jnp.float32) + grad).astype(jnp.bfloat16)


def block_call(x, dy, cos, sin, g_in, q_norm, k_norm, w_q, w_k, w_v, w_o):
    seqs, seq_len, model = x.shape
    head_dim = q_norm.shape[1]
    q_width, kv_width = w_q.shape[1], w_k.shape[1]
    groups = kv_width // head_dim
    q_cols = q_width // groups
    tokens = seqs * seq_len
    row = lambda s, g: (s, 0, 0)
    col = lambda s, g: (s, 0, g)
    fixed = lambda s, g: (0, 0)
    wcol = lambda s, g: (0, g)
    bf = lambda *shape: jax.ShapeDtypeStruct(shape, jnp.bfloat16)
    f32 = lambda *shape: jax.ShapeDtypeStruct(shape, jnp.float32)
    flops = 4 * tokens * model * (q_width * 2 + kv_width * 2) + 12 * tokens * seq_len * q_width
    return pl.pallas_call(
        block_kernel,
        grid=(seqs, groups),
        in_specs=[
            pl.BlockSpec((1, seq_len, model), row),
            pl.BlockSpec((1, seq_len, model), row),
            pl.BlockSpec((1, seq_len, head_dim), row),
            pl.BlockSpec((1, seq_len, head_dim), row),
            pl.BlockSpec((1, model), fixed),
            pl.BlockSpec((1, head_dim), fixed),
            pl.BlockSpec((1, head_dim), fixed),
            pl.BlockSpec((model, q_cols), wcol),
            pl.BlockSpec((model, head_dim), wcol),
            pl.BlockSpec((model, head_dim), wcol),
            pl.BlockSpec((q_cols, model), lambda s, g: (g, 0)),
        ],
        out_specs=[
            pl.BlockSpec((1, seq_len, model), row),
            pl.BlockSpec((1, seq_len, model), row),
            pl.BlockSpec((1, seq_len, model), row),
            pl.BlockSpec((1, seq_len, q_cols), col),
            pl.BlockSpec((1, seq_len, q_cols), col),
            pl.BlockSpec((1, seq_len, head_dim), col),
            pl.BlockSpec((1, seq_len, head_dim), col),
            pl.BlockSpec((1, model), fixed),
            pl.BlockSpec((1, head_dim), fixed),
            pl.BlockSpec((1, head_dim), fixed),
        ],
        out_shape=[
            bf(seqs, seq_len, model), bf(seqs, seq_len, model), bf(seqs, seq_len, model),
            bf(seqs, seq_len, q_width), bf(seqs, seq_len, q_width),
            bf(seqs, seq_len, kv_width), bf(seqs, seq_len, kv_width),
            f32(1, model), f32(1, head_dim), f32(1, head_dim),
        ],
        scratch_shapes=[pltpu.VMEM((seq_len, model), jnp.float32), pltpu.VMEM((seq_len, model), jnp.float32)],
        compiler_params=pltpu.CompilerParams(
            dimension_semantics=("arbitrary", "arbitrary"), vmem_limit_bytes=60 * 1024 * 1024),
        cost_estimate=pl.CostEstimate(flops=flops, bytes_accessed=50_000_000, transcendentals=tokens * seq_len * 8),
        name="block",
    )(x, dy, cos, sin, g_in, q_norm, k_norm, w_q, w_k, w_v, w_o)


def reduce_grad(part, c, x, y):
    bit = {1: c, 2: x, 4: y}

    def swap(values, axis_bit):
        return lax.ppermute(values, 'sp', [(d, d ^ axis_bit) for d in range(8)])

    def split(values, axis_bit):
        n = values.shape[0] // 2
        b = bit[axis_bit]
        mine = lax.dynamic_slice_in_dim(values, b * n, n, 0)
        other = lax.dynamic_slice_in_dim(values, (1 - b) * n, n, 0)
        got = swap(other.astype(jnp.bfloat16), axis_bit)
        return mine + got.astype(jnp.float32)

    def join(values, axis_bit):
        got = swap(values, axis_bit)
        b = bit[axis_bit]
        return jnp.where(b == 0, jnp.concatenate([values, got], 0), jnp.concatenate([got, values], 0))

    half = split(part, 1)
    n = half.shape[0] // 2
    xy = split(split(half[:n], 2), 4).astype(jnp.bfloat16)
    yx = split(split(half[n:], 4), 2).astype(jnp.bfloat16)
    full = jnp.concatenate([join(join(xy, 4), 2), join(join(yx, 2), 4)], 0)
    return join(full, 1).astype(jnp.float32)


def solution(mesh):
    group_size = mesh.shape['sp']
    seq_spec = P(None, 'sp', None)
    replicated = P()

    def shard_body(hidden_in, grad_out, positions, w_q, w_k, w_v, w_o, g_in, q_norm, k_norm):
        batch, seq_dev, model_dim = hidden_in.shape
        head_dim = q_norm.shape[0]
        per_dev = batch // group_size
        seq_len = seq_dev * group_size
        me = lax.axis_index('sp')
        c, xi, yi = me % 2, (me // 2) % 2, me // 4

        pos = lax.all_to_all(positions.reshape(per_dev, group_size, seq_dev), 'sp', 1, 1, tiled=True).reshape(per_dev, seq_len)
        cos, sin = rope_tables(pos, head_dim)
        gains = (g_in.astype(jnp.float32)[None], q_norm.astype(jnp.float32)[None], k_norm.astype(jnp.float32)[None])

        def to_batch(values, j):
            piece = values[j * group_size:(j + 1) * group_size]
            return lax.all_to_all(piece, 'sp', 0, 0, tiled=True).reshape(1, seq_len, model_dim)

        def to_seq(values):
            return lax.all_to_all(values.reshape(group_size, seq_dev, model_dim), 'sp', 0, 0, tiled=True)

        outs = []
        for j in range(per_dev):
            xj, dyj = to_batch(hidden_in, j), to_batch(grad_out, j)
            res = block_call(xj, dyj, cos[j:j + 1], sin[j:j + 1], *gains, w_q, w_k, w_v, w_o)
            outs.append((to_seq(res[0]), to_seq(res[1]), dyj) + tuple(res[2:]))
        hidden_out, grad_in = (jnp.concatenate([o[i] for o in outs], axis=0) for i in range(2))
        dy, h, o, dq, dk, dv = (jnp.concatenate([t[i] for t in outs], axis=0).reshape(per_dev * seq_len, -1) for i in range(2, 8))
        small = [sum(t[i] for t in outs)[0] for i in range(8, 11)]
        grad_wo, grad_wq, grad_wk, grad_wv = (reduce_grad(dot(a, b, TN), c, xi, yi) for a, b in ((o, dy), (h, dq), (h, dk), (h, dv)))
        small = lax.psum(tuple(small), 'sp')
        return (hidden_out, grad_in, grad_wq, grad_wk, grad_wv, grad_wo) + tuple(small)

    return jax.shard_map(shard_body, mesh=mesh,
                         in_specs=(seq_spec, seq_spec, P(None, 'sp'), replicated, replicated, replicated, replicated, replicated, replicated, replicated),
                         out_specs=(seq_spec, seq_spec, replicated, replicated, replicated, replicated, replicated, replicated, replicated),
                         check_vma=False)
```

time: 1310 us -> 684 us (0.52)
  waiting for transfers between devices: 379 us -> 106 us
  matrix products: 306 us -> 35.2 us
  other arithmetic: 237 us -> 81 us
  local copies, waits for them, and re-layouts: 299 us -> 206 us
  blocking collectives: 24.2 us -> 101 us
  Pallas kernels: 0 us -> 54.8 us
  starting transfers between devices: 40.5 us -> 90.8 us
    dot_general x18 -> x4, matrix products: 306 us -> 35.2 us  [dot(): return lax.dot_general(a, b, dims, preferred_element_type=jnp.float32)]
    psum x1 -> x0, waiting for transfers between devices: 197 us -> none  [shard_body(): lax.psum((grad_wq, grad_wk, grad_wv, grad_wo, grad_gin, grad_qn, grad_kn)...]
    pallas_call x0 -> x3, local copies, waits for them, and re-layouts: none -> 164 us  [block_call(): pl.pallas_call(block_kernel, grid=(seqs, groups), in_specs=[pl.BlockSpec(...]
    all_to_all x8 -> x13, waiting for transfers between devices: 182 us -> 82 us  [the longest x8 47.9 us: to_seq(): lax.all_to_all(values.reshape(group_size, seq_dev, model_dim), 'sp', 0, 0...]
    all_to_all x9 -> x1, local copies, waits for them, and re-layouts: 93.7 us -> 0.51 us  [shard_body(): lax.all_to_all(positions.reshape(per_dev, group_size, seq_dev), 'sp', 1,...]
    all_to_all x0 -> x4, blocking collectives: none -> 69 us  [to_batch(): lax.all_to_all(piece, 'sp', 0, 0, tiled=True).reshape(1, seq_len, model_dim)]
    reshape x5 -> x1, local copies, waits for them, and re-layouts: 68.9 us -> 0.72 us  [shard_body(): positions.reshape(per_dev, group_size, seq_dev)]
    another operation x3 -> x0, other arithmetic: 66.1 us -> none
  transfers between devices with their start and end apart: 9 -> 53, of which waited for: 7 -> 24; matrix products, arithmetic and copies ran while one was open for 41% -> 34% of each run, Pallas kernels for 0% -> 8%
where the time goes in v1:
time: 684 us; the launch traced here: 677 us
  local copies, waits for them, and re-layouts  206 us (30%)
  waiting for transfers between devices  106 us (15%)
  blocking collectives  101 us (15%)
  starting transfers between devices  90.8 us (13%)
  other arithmetic  81 us (12%)
  Pallas kernels  54.8 us (8%)
  matrix products  35.2 us (5%)
    pallas_call x3, local copies, waits for them, and re-layouts, block_call(): pl.pallas_call(block_kernel, grid=(seqs, groups), in_specs=[pl.BlockSpec(...  164 us
    all_to_all x4, blocking collectives, to_batch(): lax.all_to_all(piece, 'sp', 0, 0, tiled=True).reshape(1, seq_len, model_dim)  69 us
    pallas_call x1, Pallas kernels, block_call(): pl.pallas_call(block_kernel, grid=(seqs, groups), in_specs=[pl.BlockSpec(...  54.8 us
    ppermute x40, starting transfers between devices, swap(): return lax.ppermute(values, 'sp', [(d, d ^ axis_bit) for d in range(8)])  54.5 us
    all_to_all x8, waiting for transfers between devices, to_seq(): lax.all_to_all(values.reshape(group_size, seq_dev, model_dim), 'sp', 0, 0...  47.9 us
    dot_general x4, matrix products, dot(): return lax.dot_general(a, b, dims, preferred_element_type=jnp.float32)  35.2 us
    all_to_all x4, waiting for transfers between devices, to_batch(): lax.all_to_all(piece, 'sp', 0, 0, tiled=True).reshape(1, seq_len, model_dim)  33.7 us
    psum x1, blocking collectives, shard_body(): small = lax.psum(tuple(small), 'sp')  31.9 us
  transfers between devices with their start and end apart: 53, of which 24 were waited for; matrix products, arithmetic and copies ran while one was open for 34% of the time, Pallas kernels for 8%

profile of v1, /device:TPU:0, one launch (start us, length us, event | category | flops | bytes accessed | tf_op | source)
XLA Modules:
  0.0 677.3 jit_solution(501721956235013942)
XLA Ops:
  17.9 11.2 %all-to-all-done.1 = bf16[8,64,1024]{2,1,0:T(8,128)(2,1)} async-done(((bf16[8,64,1024]{2,1,0:T(8,128)(2,1)}), bf16[8,64,1024]{2,1,0:T(8,128)(2,1)}, u32[]{:S(2)}, u32[]{:S(2)}) %all-to-all-start.1) | async-done | bytes 1048608 | tf_op jit(solution)/shard_map/all_to_all | solution.py:249
  29.1 18.0 %all_to_all.85 = bf16[8,64,1024]{2,1,0:T(8,128)(2,1)} all-to-all(bf16[8,64,1024]{2,1,0:T(8,128)(2,1)} %get-tuple-element.162), channel_id=1, replica_groups=mesh['sp'=8] {'sp'}, dimensions={0} | all-to-all | bytes 2097152 | tf_op jit(solution)/shard_map/all_to_all | solution.py:249
  47.1 17.2 %all_to_all.86 = bf16[8,64,1024]{2,1,0:T(8,128)(2,1)} all-to-all(bf16[8,64,1024]{2,1,0:T(8,128)(2,1)S(1)} %get-tuple-element.157), channel_id=1, replica_groups=mesh['sp'=8] {'sp'}, dimensions={0} | all-to-all | bytes 2097152 | tf_op jit(solution)/shard_map/all_to_all | solution.py:249
  64.3 17.2 %all_to_all.87 = bf16[8,64,1024]{2,1,0:T(8,128)(2,1)} all-to-all(bf16[8,64,1024]{2,1,0:T(8,128)(2,1)S(1)} %get-tuple-element.161), channel_id=1, replica_groups=mesh['sp'=8] {'sp'}, dimensions={0} | all-to-all | bytes 2097152 | tf_op jit(solution)/shard_map/all_to_all | solution.py:249
  81.6 16.5 %all_to_all.88 = bf16[8,64,1024]{2,1,0:T(8,128)(2,1)S(1)} all-to-all(bf16[8,64,1024]{2,1,0:T(8,128)(2,1)S(1)} %get-tuple-element.159), channel_id=1, replica_groups=mesh['sp'=8] {'sp'}, dimensions={0} | all-to-all | bytes 2097152 | tf_op jit(solution)/shard_map/all_to_all | solution.py:249
  101.1 14.6 %all-to-all-done.7 = bf16[8,64,1024]{2,1,0:T(8,128)(2,1)S(1)} async-done(((bf16[8,64,1024]{2,1,0:T(8,128)(2,1)}), bf16[8,64,1024]{2,1,0:T(8,128)(2,1)S(1)}, u32[]{:S(2)}, u32[]{:S(2)}) %all-to-all-start.7) | async-done | bytes 1048608 | tf_op jit(solution)/shard_map/all_to_all | solution.py:249
  125.4 7.9 %all-to-all-done.11 = bf16[8,64,1024]{2,1,0:T(8,128)(2,1)S(1)} async-done(((bf16[8,64,1024]{2,1,0:T(8,128)(2,1)}), bf16[8,64,1024]{2,1,0:T(8,128)(2,1)S(1)}, u32[]{:S(2)}, u32[]{:S(2)}) %all-to-all-start.11) | async-done | bytes 1048608 | tf_op jit(solution)/shard_map/all_to_all | solution.py:249
  136.8 54.8 %block.4 = (bf16[1,512,1024]{2,1,0:T(8,128)(2,1)}, bf16[1,512,1024]{2,1,0:T(8,128)(2,1)}, bf16[1,512,1024]{2,1,0:T(8,128)(2,1)}, bf16[1,512,2048]{2,1,0:T(8,128)...) custom-call(bf16[1,512,1024]{2,1,0:T(8,128)(2,1)} %bitcast.61, ...), custom_call_target="tpu_custom_call" | custom-call | flops 19327352832 | bytes 50000000 | tf_op jit(solution)/shard_map/block/pallas_call | solution.py:161
  193.9 54.6 %block.7 = (bf16[4,512,1024]{2,1,0:T(8,128)(2,1)}, bf16[1,512,1024]{2,1,0:T(8,128)(2,1)}, bf16[1,512,1024]{2,1,0:T(8,128)(2,1)}, bf16[1,512,2048]{2,1,0:T(8,128)...) fusion(bf16[4,512,1024]{2,1,0:T(8,128)(2,1)} %constant_dynamic-, ...), kind=kCustom, calls=%fused_computation.139 | custom fusion | bytes 24651776 | tf_op jit(solution)/shard_map/block/pallas_call | solution.py:161
  248.5 53.7 %block.6 = (bf16[4,512,1024]{2,1,0:T(8,128)(2,1)}, bf16[1,512,1024]{2,1,0:T(8,128)(2,1)}, bf16[1,512,1024]{2,1,0:T(8,128)(2,1)}, bf16[1,512,2048]{2,1,0:T(8,128)...) fusion(bf16[4,512,1024]{2,1,0:T(8,128)(2,1)} %get-tuple-element, ...), kind=kCustom, calls=%fused_computation.138 | custom fusion | bytes 24651776 | tf_op jit(solution)/shard_map/block/pallas_call | solution.py:161
  302.3 55.2 %block.5 = (bf16[4,512,1024]{2,1,0:T(8,128)(2,1)}, bf16[1,512,1024]{2,1,0:T(8,128)(2,1)}, bf16[1,512,1024]{2,1,0:T(8,128)(2,1)}, bf16[1,512,2048]{2,1,0:T(8,128)...) fusion(bf16[4,512,1024]{2,1,0:T(8,128)(2,1)} %get-tuple-element, ...), kind=kCustom, calls=%fused_computation.137 | custom fusion | bytes 24651776 | tf_op jit(solution)/shard_map/block/pallas_call | solution.py:161
  357.5 13.0 %fusion.16 = f32[2048,1024]{1,0:T(8,128)S(1)} fusion(bf16[1,512,2048]{2,1,0:T(8,128)(2,1)} %get-tuple-element.142, bf16[1,512,2048]{2,1,0:T(8,128)(2,1)} %get-tuple-element.102, bf16[1,512,2048]{2,1,0:T(8,128)(2,1)} %get-tuple-element.122, bf16[1,512,2048]{2,1,0:T(8,128)(2,1)} %get-tuple-element.73, bf16[1,512,1024]{2,1,0:T(8,128)(2,1)S(1)} %bitcast.63, ...), kind=kOutput, calls=%fused_computation.16 | convolution fusion | flops 8608808960 | bytes 20971520 | tf_op jit(solution)/shard_map/dot_general | solution.py:18
  375.8 6.3 fusion.47
  391.5 11.2 %fusion.19 = f32[1024,2048]{1,0:T(8,128)S(1)} fusion(bf16[4,512,1024]{2,1,0:T(8,128)(2,1)S(1)} %copy-done.37, bf16[1,512,2048]{2,1,0:T(8,128)(2,1)} %get-tuple-element.136, bf16[1,512,2048]{2,1,0:T(8,128)(2,1)S(1)} %copy-done.56, bf16[1,512,2048]{2,1,0:T(8,128)(2,1)S(1)} %copy-done.55, bf16[1,512,2048]{2,1,0:T(8,128)(2,1)S(1)} %copy-done.54), kind=kOutput, calls=%fused_computation.17 | convolution fusion | flops 8602517504 | bytes 20971520 | tf_op jit(solution)/shard_map/dot_general | solution.py:18
  410.8 31.9 %all-reduce = (f32[1024]{0:T(1024)}, f32[128]{0:T(128)}, f32[128]{0:T(128)}) all-reduce(f32[1024]{0:T(1024)S(1)} %bitcast.66, f32[128]{0:T(128)S(1)} %add_bitcast_fusion.1, f32[128]{0:T(128)S(1)} %add_bitcast_fusion), channel_id=1, replica_groups=mesh['sp'=8] {'sp'}, use_global_device_ids=true, to_apply=%region_0.1 | all-reduce | flops 1280 | bytes 10240 | tf_op jit(solution)/shard_map/psum | solution.py:263
  533.2 9.5 %all-to-all-done.14 = bf16[8,64,1024]{2,1,0:T(8,128)(2,1)} async-done(((bf16[8,64,1024]{2,1,0:T(8,128)(2,1)}), bf16[8,64,1024]{2,1,0:T(8,128)(2,1)}, u32[]{:S(2)}, u32[]{:S(2)}) %all-to-all-start.14) | async-done | bytes 1048608 | tf_op jit(solution)/shard_map/all_to_all | solution.py:252
  552.4 8.2 %all-to-all-done.13 = bf16[8,64,1024]{2,1,0:T(8,128)(2,1)S(1)} async-done(((bf16[8,64,1024]{2,1,0:T(8,128)(2,1)}), bf16[8,64,1024]{2,1,0:T(8,128)(2,1)S(1)}, u32[]{:S(2)}, u32[]{:S(2)}) %all-to-all-start.13) | async-done | bytes 1048608 | tf_op jit(solution)/shard_map/all_to_all | solution.py:252
  571.7 6.9 %all-to-all-done.12 = bf16[8,64,1024]{2,1,0:T(8,128)(2,1)S(1)} async-done(((bf16[8,64,1024]{2,1,0:T(8,128)(2,1)}), bf16[8,64,1024]{2,1,0:T(8,128)(2,1)S(1)}, u32[]{:S(2)}, u32[]{:S(2)}) %all-to-all-start.12) | async-done | bytes 1048608 | tf_op jit(solution)/shard_map/all_to_all | solution.py:252
  607.5 4.9 collective-permute-done.34
  617.6 6.1 collective-permute-done.4
  625.7 9.8 %all-to-all-done.6 = bf16[8,64,1024]{2,1,0:T(8,128)(2,1)} async-done(((bf16[8,64,1024]{2,1,0:T(8,128)(2,1)}), bf16[8,64,1024]{2,1,0:T(8,128)(2,1)}, u32[]{:S(2)}, u32[]{:S(2)}) %all-to-all-start.6) | async-done | bytes 1048608 | tf_op jit(solution)/shard_map/all_to_all | solution.py:252
  648.0 5.7 all-to-all-done.3
  665.0 5.8 fusion.46
  670.8 6.0 fusion.22
  (307 shorter events, 228.7 us)
Async XLA Ops:
  133.2 169.0 %all-to-all-start.10 = ((bf16[8,64,1024]{2,1,0:T(8,128)(2,1)}), bf16[8,64,1024]{2,1,0:T(8,128)(2,1)}, u32[]{:S(2)}, u32[]{:S(2)}) async-start(bf16[8,64,1024]{2,1,0:T(8,128)(2,1)} %get-tuple-element.160), calls=%async_computation.10 | async-start | bytes 2097152 | tf_op jit(solution)/shard_map/all_to_all | solution.py:249
  370.9 118.3 %collective-permute-start.30 = (bf16[1024,1024]{1,0:T(8,128)(2,1)S(1)}, bf16[1024,1024]{1,0:T(8,128)(2,1)}, u32[]{:S(2)}, u32[]{:S(2)}) collective-permute-start(bf16[1024,1024]{1,0:T(8,128)(2,1)S(1)} %dynamic-slice_convert_fusion), channel_id=1, source_target_pairs={{0,1},{1,0},{2,3},{3,2},{4,5},{5,4},{6,7},{7,6}} | collective-permute-start | bytes 6291464 | tf_op jit(solution)/shard_map/ppermute | solution.py:207
  383.4 59.3 %collective-permute-start.20 = (bf16[512,1024]{1,0:T(8,128)(2,1)}, bf16[512,1024]{1,0:T(8,128)(2,1)}, u32[]{:S(2)}, u32[]{:S(2)}) collective-permute-start(bf16[512,1024]{1,0:T(8,128)(2,1)} %dynamic-slice_convert_fusion.2), channel_id=1, source_target_pairs={{0,1},{1,0},{2,3},{3,2},{4,5},{5,4},{6,7},{7,6}} | collective-permute-start | bytes 3145736 | tf_op jit(solution)/shard_map/ppermute | solution.py:207
  390.5 58.0 %collective-permute-start.10 = (bf16[512,1024]{1,0:T(8,128)(2,1)}, bf16[512,1024]{1,0:T(8,128)(2,1)}, u32[]{:S(2)}, u32[]{:S(2)}) collective-permute-start(bf16[512,1024]{1,0:T(8,128)(2,1)} %dynamic-slice_convert_fusion.3), channel_id=1, source_target_pairs={{0,1},{1,0},{2,3},{3,2},{4,5},{5,4},{6,7},{7,6}} | collective-permute-start | bytes 3145736 | tf_op jit(solution)/shard_map/ppermute | solution.py:207
  407.7 89.3 %collective-permute-start = (bf16[512,2048]{1,0:T(8,128)(2,1)}, bf16[512,2048]{1,0:T(8,128)(2,1)}, u32[]{:S(2)}, u32[]{:S(2)}) collective-permute-start(bf16[512,2048]{1,0:T(8,128)(2,1)} %dynamic-slice_convert_fusion.1), channel_id=1, source_target_pairs={{0,1},{1,0},{2,3},{3,2},{4,5},{5,4},{6,7},{7,6}} | collective-permute-start | bytes 6291464 | tf_op jit(solution)/shard_map/ppermute | solution.py:207
  408.2 93.2 %all-to-all-start.16 = ((bf16[8,64,1024]{2,1,0:T(8,128)(2,1)}), bf16[8,64,1024]{2,1,0:T(8,128)(2,1)S(1)}, u32[]{:S(2)}, u32[]{:S(2)}) async-start(bf16[8,64,1024]{2,1,0:T(8,128)(2,1)} %bitcast.59), calls=%async_computation.16 | async-start | bytes 2097152 | tf_op jit(solution)/shard_map/all_to_all | solution.py:252
  485.0 172.6 %collective-permute-start.29 = (bf16[512,1024]{1,0:T(8,128)(2,1)}, bf16[512,1024]{1,0:T(8,128)(2,1)}, u32[]{:S(2)}, u32[]{:S(2)}) collective-permute-start(bf16[512,1024]{1,0:T(8,128)(2,1)} %pad_maximum_fusion.5), channel_id=1, source_target_pairs={{0,1},{1,0},{2,3},{3,2},{4,5},{5,4},{6,7},{7,6}} | collective-permute-start | bytes 3145736 | tf_op jit(solution)/shard_map/ppermute | solution.py:207
  495.7 30.7 %collective-permute-start.35 = (bf16[256,1024]{1,0:T(8,128)(2,1)}, bf16[256,1024]{1,0:T(8,128)(2,1)}, u32[]{:S(2)}, u32[]{:S(2)}) collective-permute-start(bf16[256,1024]{1,0:T(8,128)(2,1)} %dynamic-slice_convert_fusion.4), channel_id=1, source_target_pairs={{0,4},{1,5},{2,6},{3,7},{4,0},{5,1},{6,2},{7,3}} | collective-permute-start | bytes 1572872 | tf_op jit(solution)/shard_map/ppermute | solution.py:207
  509.5 21.6 %collective-permute-start.1 = (bf16[128,2048]{1,0:T(8,128)(2,1)}, bf16[128,2048]{1,0:T(8,128)(2,1)}, u32[]{:S(2)}, u32[]{:S(2)}) collective-permute-start(bf16[128,2048]{1,0:T(8,128)(2,1)} %dynamic-slice_convert_fusion.7), channel_id=1, source_target_pairs={{0,2},{1,3},{2,0},{3,1},{4,6},{5,7},{6,4},{7,5}} | collective-permute-start | bytes 1572872 | tf_op jit(solution)/shard_map/ppermute | solution.py:207
  512.3 36.5 %collective-permute-start.5 = (bf16[128,2048]{1,0:T(8,128)(2,1)}, bf16[128,2048]{1,0:T(8,128)(2,1)}, u32[]{:S(2)}, u32[]{:S(2)}) collective-permute-start(bf16[128,2048]{1,0:T(8,128)(2,1)} %dynamic-slice_convert_fusion.6), channel_id=1, source_target_pairs={{0,4},{1,5},{2,6},{3,7},{4,0},{5,1},{6,2},{7,3}} | collective-permute-start | bytes 1572872 | tf_op jit(solution)/shard_map/ppermute | solution.py:207
  520.2 22.5 %all-to-all-start.14 = ((bf16[8,64,1024]{2,1,0:T(8,128)(2,1)}), bf16[8,64,1024]{2,1,0:T(8,128)(2,1)}, u32[]{:S(2)}, u32[]{:S(2)}) async-start(bf16[8,64,1024]{2,1,0:T(8,128)(2,1)} %bitcast.53), calls=%async_computation.14 | async-start | bytes 2097152 | tf_op jit(solution)/shard_map/all_to_all | solution.py:252
  524.5 38.5 %collective-permute-start.32 = (bf16[128,1024]{1,0:T(8,128)(2,1)S(1)}, bf16[128,1024]{1,0:T(8,128)(2,1)}, u32[]{:S(2)}, u32[]{:S(2)}) collective-permute-start(bf16[128,1024]{1,0:T(8,128)(2,1)S(1)} %dynamic-slice_convert_fusion.9), channel_id=1, source_target_pairs={{0,4},{1,5},{2,6},{3,7},{4,0},{5,1},{6,2},{7,3}} | collective-permute-start | bytes 786440 | tf_op jit(solution)/shard_map/ppermute | solution.py:207
  529.6 36.5 %collective-permute-start.36 = (bf16[128,1024]{1,0:T(8,128)(2,1)}, bf16[128,1024]{1,0:T(8,128)(2,1)}, u32[]{:S(2)}, u32[]{:S(2)}) collective-permute-start(bf16[128,1024]{1,0:T(8,128)(2,1)} %dynamic-slice_convert_fusion.8), channel_id=1, source_target_pairs={{0,2},{1,3},{2,0},{3,1},{4,6},{5,7},{6,4},{7,5}} | collective-permute-start | bytes 786440 | tf_op jit(solution)/shard_map/ppermute | solution.py:207
  546.8 22.7 %collective-permute-start.2 = (bf16[64,2048]{1,0:T(8,128)(2,1)}, bf16[64,2048]{1,0:T(8,128)(2,1)}, u32[]{:S(2)}, u32[]{:S(2)}) collective-permute-start(bf16[64,2048]{1,0:T(8,128)(2,1)} %dynamic-slice_convert_fusion.15), channel_id=1, source_target_pairs={{0,4},{1,5},{2,6},{3,7},{4,0},{5,1},{6,2},{7,3}} | collective-permute-start | bytes 786440 | tf_op jit(solution)/shard_map/ppermute | solution.py:207
  550.9 30.0 %collective-permute-start.6 = (bf16[64,2048]{1,0:T(8,128)(2,1)}, bf16[64,2048]{1,0:T(8,128)(2,1)}, u32[]{:S(2)}, u32[]{:S(2)}) collective-permute-start(bf16[64,2048]{1,0:T(8,128)(2,1)} %dynamic-slice_convert_fusion.14), channel_id=1, source_target_pairs={{0,2},{1,3},{2,0},{3,1},{4,6},{5,7},{6,4},{7,5}} | collective-permute-start | bytes 786440 | tf_op jit(solution)/shard_map/ppermute | solution.py:207
  578.6 21.5 %all-to-all-start.9 = ((bf16[8,64,1024]{2,1,0:T(8,128)(2,1)}), bf16[8,64,1024]{2,1,0:T(8,128)(2,1)S(1)}, u32[]{:S(2)}, u32[]{:S(2)}) async-start(bf16[8,64,1024]{2,1,0:T(8,128)(2,1)} %bitcast.50), calls=%async_computation.9 | async-start | bytes 2097152 | tf_op jit(solution)/shard_map/all_to_all | solution.py:252
  582.8 20.6 %collective-permute-start.7 = (bf16[64,2048]{1,0:T(8,128)(2,1)}, bf16[64,2048]{1,0:T(8,128)(2,1)}, u32[]{:S(2)}, u32[]{:S(2)}) collective-permute-start(bf16[64,2048]{1,0:T(8,128)(2,1)} %add_convert_fusion.2), channel_id=1, source_target_pairs={{0,2},{1,3},{2,0},{3,1},{4,6},{5,7},{6,4},{7,5}} | collective-permute-start | bytes 786440 | tf_op jit(solution)/shard_map/ppermute | solution.py:207
  585.9 26.5 %collective-permute-start.34 = (bf16[256,1024]{1,0:T(8,128)(2,1)S(1)}, bf16[256,1024]{1,0:T(8,128)(2,1)}, u32[]{:S(2)}, u32[]{:S(2)}) collective-permute-start(bf16[256,1024]{1,0:T(8,128)(2,1)S(1)} %maximum_select_fusion.14), channel_id=1, source_target_pairs={{0,2},{1,3},{2,0},{3,1},{4,6},{5,7},{6,4},{7,5}} | collective-permute-start | bytes 1572872 | tf_op jit(solution)/shard_map/ppermute | solution.py:207
  588.2 25.9 %collective-permute-start.38 = (bf16[256,1024]{1,0:T(8,128)(2,1)}, bf16[256,1024]{1,0:T(8,128)(2,1)}, u32[]{:S(2)}, u32[]{:S(2)}) collective-permute-start(bf16[256,1024]{1,0:T(8,128)(2,1)} %maximum_select_fusion.15), channel_id=1, source_target_pairs={{0,4},{1,5},{2,6},{3,7},{4,0},{5,1},{6,2},{7,3}} | collective-permute-start | bytes 1572872 | tf_op jit(solution)/shard_map/ppermute | solution.py:207
  593.1 30.6 %collective-permute-start.4 = (bf16[128,2048]{1,0:T(8,128)(2,1)S(1)}, bf16[128,2048]{1,0:T(8,128)(2,1)}, u32[]{:S(2)}, u32[]{:S(2)}) collective-permute-start(bf16[128,2048]{1,0:T(8,128)(2,1)S(1)} %maximum_select_fusion.8), channel_id=1, source_target_pairs={{0,2},{1,3},{2,0},{3,1},{4,6},{5,7},{6,4},{7,5}} | collective-permute-start | bytes 1572872 | tf_op jit(solution)/shard_map/ppermute | solution.py:207
  600.1 35.4 %all-to-all-start.6 = ((bf16[8,64,1024]{2,1,0:T(8,128)(2,1)}), bf16[8,64,1024]{2,1,0:T(8,128)(2,1)}, u32[]{:S(2)}, u32[]{:S(2)}) async-start(bf16[8,64,1024]{2,1,0:T(8,128)(2,1)} %bitcast.49), calls=%async_computation.6 | async-start | bytes 2097152 | tf_op jit(solution)/shard_map/all_to_all | solution.py:252
  605.5 33.0 %collective-permute-start.8 = (bf16[128,2048]{1,0:T(8,128)(2,1)}, bf16[128,2048]{1,0:T(8,128)(2,1)}, u32[]{:S(2)}, u32[]{:S(2)}) collective-permute-start(bf16[128,2048]{1,0:T(8,128)(2,1)} %maximum_select_fusion.9), channel_id=1, source_target_pairs={{0,4},{1,5},{2,6},{3,7},{4,0},{5,1},{6,2},{7,3}} | collective-permute-start | bytes 1572872 | tf_op jit(solution)/shard_map/ppermute | solution.py:207
  617.6 47.4 %collective-permute-start.39 = (bf16[1024,1024]{1,0:T(8,128)(2,1)}, bf16[1024,1024]{1,0:T(8,128)(2,1)}, u32[]{:S(2)}, u32[]{:S(2)}) collective-permute-start(bf16[1024,1024]{1,0:T(8,128)(2,1)} %pad_maximum_fusion.3), channel_id=1, source_target_pairs={{0,1},{1,0},{2,3},{3,2},{4,5},{5,4},{6,7},{7,6}} | collective-permute-start | bytes 6291464 | tf_op jit(solution)/shard_map/ppermute | solution.py:207
  643.1 27.7 %collective-permute-start.9 = (bf16[512,2048]{1,0:T(8,128)(2,1)}, bf16[512,2048]{1,0:T(8,128)(2,1)}, u32[]{:S(2)}, u32[]{:S(2)}) collective-permute-start(bf16[512,2048]{1,0:T(8,128)(2,1)} %pad_maximum_fusion.2), channel_id=1, source_target_pairs={{0,1},{1,0},{2,3},{3,2},{4,5},{5,4},{6,7},{7,6}} | collective-permute-start | bytes 6291464 | tf_op jit(solution)/shard_map/ppermute | solution.py:207
  (90 other events, 1307.2 us)

commit v2 on v1

v2 whole, which is shorter than its diff:
```python
import functools
import jax
import jax.numpy as jnp
from jax import lax
from jax.experimental import pallas as pl
from jax.experimental.pallas import tpu as pltpu
from jax.sharding import PartitionSpec as P

EPSILON = 1e-6
ROPE_THETA = 1000000.0
NEG_LARGE = -1e30
NT = (((1,), (1,)), ((), ()))
TN = (((0,), (0,)), ((), ()))
ROW_BLOCK = 256
DEVICES = 8
BF16 = jnp.bfloat16
F32 = jnp.float32


def dot(a, b, dims=(((1,), (0,)), ((), ()))):
    return lax.dot_general(a, b, dims, preferred_element_type=F32)


def peer_of(me, step):
    core, x, y = me % 2, (me // 2) % 2, me // 4
    return ((y + step // 4) % 2) * 4 + ((x + (step // 2) % 2) % 2) * 2 + (core + step % 2) % 2


def entry_barrier(me):
    barrier = pltpu.get_barrier_semaphore()
    for step in range(1, DEVICES):
        pl.semaphore_signal(barrier, inc=1, device_id=(peer_of(me, step),), device_id_type=pl.DeviceIdType.MESH)
    pl.semaphore_wait(barrier, DEVICES - 1)


def remote(src, dst, send, recv, device):
    return pltpu.make_async_remote_copy(src_ref=src, dst_ref=dst, send_sem=send, recv_sem=recv,
                                        device_id=(device,), device_id_type=pl.DeviceIdType.MESH)


def block_kernel(x_hbm, dy_hbm, pos_hbm, freq_ref, gin_ref, qn_ref, kn_ref, wq_ref, wk_ref, wv_ref, wo_ref,
                 out_hbm, gi_hbm, ht_ref, dyo_ref, o_ref, dq_ref, dk_ref, dv_ref, dgin_ref, dqn_ref, dkn_ref,
                 xb, dyb, gib, posb, h_ref, cos_ref, sin_ref, out_acc, dh_acc, in_send, in_recv, out_send, out_recv):
    seq, group = pl.program_id(0), pl.program_id(1)
    seqs, groups = pl.num_programs(0), pl.num_programs(1)
    me = lax.axis_index('sp')
    head_dim = qn_ref.shape[1]
    per_kv = wq_ref.shape[1] // head_dim
    seq_len = xb.shape[1]
    piece = seq_len // DEVICES
    scale = head_dim ** -0.5
    half = head_dim // 2

    def rows_of(device):
        return pl.ds(pl.multiple_of(device * piece, piece), piece)

    def incoming(kind, s, step, arrival=False):
        peer = peer_of(me, step)
        src = (x_hbm, dy_hbm, pos_hbm)[kind].at[DEVICES * s + peer]

        def landing(device):
            return posb.at[s, device] if kind == 2 else (xb, dyb)[kind].at[s, rows_of(device)]

        if step == 0:
            return pltpu.make_async_copy(src, landing(me), in_recv.at[kind, s, 0])
        return remote(src, landing(peer if arrival else me), in_send.at[kind, s, step], in_recv.at[kind, s, step], peer)

    def outgoing(kind, s, step, arrival=False):
        peer = peer_of(me, step)
        src = (xb, gib)[kind].at[s, rows_of(peer)]
        dst = (out_hbm, gi_hbm)[kind]
        if step == 0:
            return pltpu.make_async_copy(src, dst.at[DEVICES * s + me], out_recv.at[kind, s, 0])
        return remote(src, dst.at[DEVICES * s + (peer if arrival else me)],
                      out_send.at[kind, s, step], out_recv.at[kind, s, step], peer)

    @pl.when((seq == 0) & (group == 0))
    def _():
        entry_barrier(me)

        def send_all(s, carry):
            for kind in (2, 0, 1):
                for step in (2, 4, 6, 3, 5, 7, 1, 0):
                    incoming(kind, s, step).start()
            return carry

        lax.fori_loop(0, seqs, send_all, 0)
        dgin_ref[...] = jnp.zeros_like(dgin_ref)
        dqn_ref[...] = jnp.zeros_like(dqn_ref)
        dkn_ref[...] = jnp.zeros_like(dkn_ref)

    @pl.when(group == 0)
    def _():
        for kind in (2, 0, 1):
            for step in range(DEVICES):
                arrived = incoming(kind, seq, step, arrival=True)
                if step == 0:
                    arrived.wait()
                else:
                    arrived.wait_recv()
        x = xb[seq].astype(F32)
        inv = lax.rsqrt(jnp.mean(x * x, axis=-1, keepdims=True) + EPSILON)
        h = (x * inv * gin_ref[...]).astype(BF16)
        h_ref[...] = h
        ht_ref[...] = h.T
        dyo_ref[0] = dyb[seq]
        out_acc[...] = jnp.zeros_like(out_acc)
        dh_acc[...] = jnp.zeros_like(dh_acc)
        on_diag = lax.broadcasted_iota(jnp.int32, (piece, head_dim), 0) == lax.broadcasted_iota(jnp.int32, (piece, head_dim), 1)
        low = lax.broadcasted_iota(jnp.int32, (piece, head_dim), 1) < half
        for device in range(DEVICES):
            row = jnp.broadcast_to(posb[seq, device, 0:1, :], (piece, head_dim))
            column = jnp.sum(jnp.where(on_diag, row, 0.0), axis=-1, keepdims=True)
            angles = column * freq_ref[...]
            sin = jnp.sin(angles)
            cos_ref[device * piece:(device + 1) * piece, :] = jnp.cos(angles)
            sin_ref[device * piece:(device + 1) * piece, :] = jnp.where(low, -sin, sin)

    cos, sin = cos_ref[...], sin_ref[...]

    def norm_rotate(t, gain):
        inv = lax.rsqrt(jnp.mean(t * t, axis=-1, keepdims=True) + EPSILON)
        unit = t * inv
        scaled = unit * gain
        return (scaled * cos + pltpu.roll(scaled, half, 1) * sin).astype(BF16), unit, inv

    def norm_rotate_back(grad, unit, inv, gain):
        d_scaled = grad * cos - pltpu.roll(grad, half, 1) * sin
        d_gain = jnp.sum(d_scaled * unit, axis=0, keepdims=True)
        d_unit = d_scaled * gain
        return inv * (d_unit - unit * jnp.mean(d_unit * unit, axis=-1, keepdims=True)), d_gain

    h = h_ref[...]
    q_proj = dot(h, wq_ref[...])
    k_proj = dot(h, wk_ref[...])
    v = dot(h, wv_ref[...]).astype(BF16)
    d_o = dot(dyb[seq], wo_ref[...], NT).astype(BF16)
    k_rot, k_unit, k_inv = norm_rotate(k_proj, kn_ref[...])

    blocks = seq_len // ROW_BLOCK
    dk_parts = [None] * blocks
    dv_parts = [None] * blocks
    rows_id = lax.broadcasted_iota(jnp.int32, (ROW_BLOCK, ROW_BLOCK), 0)
    cols_id = lax.broadcasted_iota(jnp.int32, (ROW_BLOCK, ROW_BLOCK), 1)
    causal = rows_id >= cols_id
    dqn_sum = None
    for head in range(per_kv):
        lanes = slice(head * head_dim, (head + 1) * head_dim)
        q_rot, q_unit, q_inv = norm_rotate(q_proj[:, lanes], qn_ref[...])
        do_head = d_o[:, lanes]
        dq_rows = []
        o_rows = []
        for i in range(blocks):
            rows = slice(i * ROW_BLOCK, (i + 1) * ROW_BLOCK)
            q_i, do_i = q_rot[rows], do_head[rows]
            s_parts = []
            for j in range(i + 1):
                s = dot(q_i, k_rot[j * ROW_BLOCK:(j + 1) * ROW_BLOCK], NT)
                if j == i:
                    s = jnp.where(causal, s, NEG_LARGE)
                s_parts.append(s)
            top = functools.reduce(jnp.maximum, [jnp.max(s, axis=-1, keepdims=True) for s in s_parts])
            e_parts = [jnp.exp((s - top) * scale) for s in s_parts]
            total = functools.reduce(jnp.add, [jnp.sum(e, axis=-1, keepdims=True) for e in e_parts])
            recip = 1.0 / total
            p_parts = [e * recip for e in e_parts]
            pb_parts = [p.astype(BF16) for p in p_parts]
            o_i = None
            for j in range(i + 1):
                part = dot(pb_parts[j], v[j * ROW_BLOCK:(j + 1) * ROW_BLOCK])
                o_i = part if o_i is None else o_i + part
            o_rows.append(o_i.astype(BF16))
            dp_parts = [dot(do_i, v[j * ROW_BLOCK:(j + 1) * ROW_BLOCK], NT) for j in range(i + 1)]
            delta = functools.reduce(jnp.add, [jnp.sum(p * dp, axis=-1, keepdims=True) for p, dp in zip(p_parts, dp_parts)])
            ds_parts = [(p * (dp - delta)).astype(BF16) for p, dp in zip(p_parts, dp_parts)]
            dq_i = None
            for j in range(i + 1):
                cols = slice(j * ROW_BLOCK, (j + 1) * ROW_BLOCK)
                part = dot(ds_parts[j], k_rot[cols])
                dq_i = part if dq_i is None else dq_i + part
                dk_j = dot(ds_parts[j], q_i, TN)
                dv_j = dot(pb_parts[j], do_i, TN)
                dk_parts[j] = dk_j if dk_parts[j] is None else dk_parts[j] + dk_j
                dv_parts[j] = dv_j if dv_parts[j] is None else dv_parts[j] + dv_j
            dq_rows.append(dq_i)
        o_ref[0, :, lanes] = jnp.concatenate(o_rows, axis=0)
        dq_head, d_gain = norm_rotate_back(jnp.concatenate(dq_rows, axis=0) * scale, q_unit, q_inv, qn_ref[...])
        dqn_sum = d_gain if dqn_sum is None else dqn_sum + d_gain
        dq_ref[0, :, lanes] = dq_head.astype(BF16)
    dqn_ref[...] += dqn_sum
    dk_head, d_gain = norm_rotate_back(jnp.concatenate(dk_parts, axis=0) * scale, k_unit, k_inv, kn_ref[...])
    dkn_ref[...] += d_gain
    dk_ref[0] = dk_head.astype(BF16)
    dv_ref[0] = jnp.concatenate(dv_parts, axis=0).astype(BF16)
    out_acc[...] += dot(o_ref[0], wo_ref[...])
    dh_acc[...] += dot(dq_ref[0], wq_ref[...], NT) + dot(dk_ref[0], wk_ref[...], NT) + dot(dv_ref[0], wv_ref[...], NT)

    @pl.when(group == groups - 1)
    def _():
        x = xb[seq].astype(F32)
        inv = lax.rsqrt(jnp.mean(x * x, axis=-1, keepdims=True) + EPSILON)
        unit = x * inv
        xb[seq] = (x + out_acc[...]).astype(BF16)
        d_norm = dh_acc[...]
        dgin_ref[...] += jnp.sum(d_norm * unit, axis=0, keepdims=True)
        d_unit = d_norm * gin_ref[...]
        grad = inv * (d_unit - unit * jnp.mean(d_unit * unit, axis=-1, keepdims=True))
        gib[seq] = (dyb[seq].astype(F32) + grad).astype(BF16)
        for kind in range(2):
            for step in (2, 4, 6, 3, 5, 7, 1, 0):
                outgoing(kind, seq, step).start()

    @pl.when((seq == seqs - 1) & (group == groups - 1))
    def _():
        def drain(s, carry):
            for step in range(1, DEVICES):
                for kind in range(3):
                    incoming(kind, s, step).wait_send()
            for step in range(DEVICES):
                for kind in range(2):
                    if step == 0:
                        outgoing(kind, s, 0).wait()
                    else:
                        outgoing(kind, s, step).wait_send()
                        outgoing(kind, s, step, arrival=True).wait_recv()
            return carry

        lax.fori_loop(0, seqs, drain, 0)


def block_call(x, dy, pos, freq, g_in, q_norm, k_norm, w_q, w_k, w_v, w_o):
    batch, piece, model = x.shape
    seqs, seq_len = batch // DEVICES, piece * DEVICES
    head_dim = q_norm.shape[1]
    q_width, kv_width = w_q.shape[1], w_k.shape[1]
    groups = kv_width // head_dim
    q_cols = q_width // groups
    tokens = seqs * seq_len
    row = lambda s, g: (s, 0, 0)
    col = lambda s, g: (s, 0, g)
    fixed = lambda s, g: (0, 0)
    wcol = lambda s, g: (0, g)
    bf = lambda *shape: jax.ShapeDtypeStruct(shape, BF16)
    f32 = lambda *shape: jax.ShapeDtypeStruct(shape, F32)
    anywhere = pl.BlockSpec(memory_space=pl.ANY)
    flops = 4 * tokens * model * (q_width * 2 + kv_width * 2) + 12 * tokens * seq_len * q_width
    return pl.pallas_call(
        block_kernel,
        grid=(seqs, groups),
        in_specs=[
            anywhere, anywhere, anywhere,
            pl.BlockSpec((1, head_dim), fixed),
            pl.BlockSpec((1, model), fixed),
            pl.BlockSpec((1, head_dim), fixed),
            pl.BlockSpec((1, head_dim), fixed),
            pl.BlockSpec((model, q_cols), wcol),
            pl.BlockSpec((model, head_dim), wcol),
            pl.BlockSpec((model, head_dim), wcol),
            pl.BlockSpec((q_cols, model), lambda s, g: (g, 0)),
        ],
        out_specs=[
            anywhere, anywhere,
            pl.BlockSpec((model, seq_len), lambda s, g: (0, s)),
            pl.BlockSpec((1, seq_len, model), row),
            pl.BlockSpec((1, seq_len, q_cols), col),
            pl.BlockSpec((1, seq_len, q_cols), col),
            pl.BlockSpec((1, seq_len, head_dim), col),
            pl.BlockSpec((1, seq_len, head_dim), col),
            pl.BlockSpec((1, model), fixed),
            pl.BlockSpec((1, head_dim), fixed),
            pl.BlockSpec((1, head_dim), fixed),
        ],
        out_shape=[
            bf(batch, piece, model), bf(batch, piece, model),
            bf(model, tokens), bf(seqs, seq_len, model),
            bf(seqs, seq_len, q_width), bf(seqs, seq_len, q_width),
            bf(seqs, seq_len, kv_width), bf(seqs, seq_len, kv_width),
            f32(1, model), f32(1, head_dim), f32(1, head_dim),
        ],
        scratch_shapes=[
            pltpu.VMEM((seqs, seq_len, model), BF16),
            pltpu.VMEM((seqs, seq_len, model), BF16),
            pltpu.VMEM((seqs, seq_len, model), BF16),
            pltpu.VMEM((seqs, DEVICES, 8, head_dim), F32),
            pltpu.VMEM((seq_len, model), BF16),
            pltpu.VMEM((seq_len, head_dim), F32),
            pltpu.VMEM((seq_len, head_dim), F32),
            pltpu.VMEM((seq_len, model), F32),
            pltpu.VMEM((seq_len, model), F32),
            pltpu.SemaphoreType.DMA((3, seqs, DEVICES)),
            pltpu.SemaphoreType.DMA((3, seqs, DEVICES)),
            pltpu.SemaphoreType.DMA((2, seqs, DEVICES)),
            pltpu.SemaphoreType.DMA((2, seqs, DEVICES)),
        ],
        compiler_params=pltpu.CompilerParams(
            dimension_semantics=("arbitrary", "arbitrary"), vmem_limit_bytes=62 * 1024 * 1024,
            collective_id=0, has_side_effects=True),
        cost_estimate=pl.CostEstimate(flops=flops, bytes_accessed=50_000_000, transcendentals=tokens * seq_len * 8),
        name="block",
    )(x, dy, pos, freq, g_in, q_norm, k_norm, w_q, w_k, w_v, w_o)


def grads_kernel(ht_ref, dy_ref, small_ref, o_hbm, dq_hbm, dk_hbm, dv_hbm,
                 ga_hbm, gb_hbm, small_out,
                 ob, qkvb, s1a, s1b, l1a, l1b, s2a, s2b, l2a, l2b, acc_a, acc_b, ra, rb, smallb,
                 load_sem, pair_send, pair_recv, chip_send, chip_recv, all_send, all_recv, fwd_send, fwd_recv,
                 small_send, small_recv):
    me = lax.axis_index('sp')
    partner = peer_of(me, 1)
    q_cols, head_dim = ob.shape[2], (qkvb.shape[2] - ob.shape[2]) // 2
    chips = l1a.shape[0]

    def peer_group(order):
        return peer_of(me, (1 - order // 2) * 2 + (((order + 1) // 2) % 2) * 4)

    def loads(group, slot):
        wide = pl.ds(pl.multiple_of(group * q_cols, q_cols), q_cols)
        narrow = pl.ds(pl.multiple_of(group * head_dim, head_dim), head_dim)
        return [
            pltpu.make_async_copy(o_hbm.at[:, wide], ob.at[slot], load_sem.at[slot, 0]),
            pltpu.make_async_copy(dq_hbm.at[:, wide], qkvb.at[slot, :, pl.ds(0, q_cols)], load_sem.at[slot, 1]),
            pltpu.make_async_copy(dk_hbm.at[:, narrow], qkvb.at[slot, :, pl.ds(q_cols, head_dim)], load_sem.at[slot, 2]),
            pltpu.make_async_copy(dv_hbm.at[:, narrow], qkvb.at[slot, :, pl.ds(q_cols + head_dim, head_dim)], load_sem.at[slot, 3]),
        ]

    def start(copies):
        for copy in copies:
            copy.start()

    def pair(order):
        return [remote(s1a.at[order], l1a.at[order], pair_send.at[0, order], pair_recv.at[0, order], partner),
                remote(s1b.at[order], l1b.at[order], pair_send.at[1, order], pair_recv.at[1, order], partner)]

    def chip(order, device):
        return [remote(s2a.at[order], l2a.at[order], chip_send.at[0, order], chip_recv.at[0, order], device),
                remote(s2b.at[order], l2b.at[order], chip_send.at[1, order], chip_recv.at[1, order], device)]

    start(loads(peer_of(peer_group(0), 1), 0))
    entry_barrier(me)
    for step in range(1, DEVICES):
        remote(small_ref, smallb.at[me], small_send.at[step], small_recv.at[step], peer_of(me, step)).start()

    def products(slot):
        return dot(ob[slot], dy_ref[...], TN), dot(ht_ref[...], qkvb[slot])

    def body(order, carry):
        mine = peer_group(order)
        other = peer_of(mine, 1)
        start(loads(mine, 1))
        for copy in loads(other, 0):
            copy.wait()
        prod_a, prod_b = products(0)
        s1a[order] = prod_a.astype(BF16)
        s1b[order] = prod_b.astype(BF16)
        start(pair(order))

        @pl.when(order < chips - 1)
        def _():
            start(loads(peer_of(peer_group(order + 1), 1), 0))

        for copy in loads(mine, 1):
            copy.wait()
        prod_a, prod_b = products(1)
        acc_a[...] = prod_a
        acc_b[...] = prod_b
        for copy in pair(order):
            copy.wait_recv()
        sum_a = acc_a[...] + l1a[order].astype(F32)
        sum_b = acc_b[...] + l1b[order].astype(F32)

        @pl.when(order < chips - 1)
        def _():
            s2a[order] = sum_a.astype(BF16)
            s2b[order] = sum_b.astype(BF16)
            start(chip(order, mine))

        @pl.when(order == chips - 1)
        def _():
            acc_a[...] = sum_a
            acc_b[...] = sum_b
        return carry

    lax.fori_loop(0, chips, body, 0)

    for order in range(chips - 1):
        for copy in chip(order, me):
            copy.wait_recv()
    ra[...] = (acc_a[...] + l2a[0].astype(F32) + l2a[1].astype(F32) + l2a[2].astype(F32)).astype(BF16)
    rb[...] = (acc_b[...] + l2b[0].astype(F32) + l2b[1].astype(F32) + l2b[2].astype(F32)).astype(BF16)

    pairs = ((ra, ga_hbm), (rb, gb_hbm))

    def spread(step, arrival=False):
        peer = peer_of(me, step)
        return [remote(src, dst.at[peer if arrival else me], all_send.at[i, step], all_recv.at[i, step], peer)
                for i, (src, dst) in enumerate(pairs)]

    def forward(step, arrival=False):
        owner, theirs = peer_of(me, step), peer_of(partner, step)
        return [remote(dst.at[owner], dst.at[theirs if arrival else owner], fwd_send.at[i, step], fwd_recv.at[i, step], partner)
                for i, (_, dst) in enumerate(pairs)]

    def wait_send(copies):
        for copy in copies:
            copy.wait_send()

    def wait_recv(copies):
        for copy in copies:
            copy.wait_recv()

    local = [pltpu.make_async_copy(src, dst.at[me], all_recv.at[i, 0]) for i, (src, dst) in enumerate(pairs)]
    for step in (2, 4, 6, 1):
        start(spread(step))
    start(local)

    for step in range(1, DEVICES):
        remote(small_ref, smallb.at[peer_of(me, step)], small_send.at[step], small_recv.at[step], me).wait_recv()
    smallb[me] = small_ref[...]
    total = smallb[0]
    for device in range(1, DEVICES):
        total = total + smallb[device]
    small_out[...] = total

    for step in (2, 4, 6):
        for arrived, onward in zip(spread(step, arrival=True), forward(step)):
            arrived.wait_recv()
            onward.start()
    wait_recv(spread(1, arrival=True))
    for copy in local:
        copy.wait()
    for step in (1, 2, 4, 6):
        wait_send(spread(step))
    for step in (2, 4, 6):
        wait_send(forward(step))
        wait_recv(forward(step, arrival=True))
    for order in range(chips):
        wait_send(pair(order))
    for order in range(chips - 1):
        wait_send(chip(order, me))
    for step in range(1, DEVICES):
        remote(small_ref, smallb.at[me], small_send.at[step], small_recv.at[step], me).wait_send()


def grads_call(ht, dy, small, o, dq, dk, dv):
    model, tokens = ht.shape
    groups, chips = DEVICES, DEVICES // 2
    q_cols, head_dim = o.shape[1] // groups, dk.shape[1] // groups
    width = q_cols + 2 * head_dim
    vmem = pl.BlockSpec(memory_space=pltpu.VMEM)
    anywhere = pl.BlockSpec(memory_space=pl.ANY)
    a, b = (q_cols, model), (model, width)
    dma = lambda *shape: pltpu.SemaphoreType.DMA(shape)
    return pl.pallas_call(
        grads_kernel,
        in_specs=[vmem, vmem, vmem, anywhere, anywhere, anywhere, anywhere],
        out_specs=[anywhere, anywhere, vmem],
        out_shape=[jax.ShapeDtypeStruct((groups,) + a, BF16), jax.ShapeDtypeStruct((groups,) + b, BF16),
                   jax.ShapeDtypeStruct(small.shape, F32)],
        scratch_shapes=[
            pltpu.VMEM((2, tokens, q_cols), BF16), pltpu.VMEM((2, tokens, width), BF16),
            pltpu.VMEM((chips,) + a, BF16), pltpu.VMEM((chips,) + b, BF16),
            pltpu.VMEM((chips,) + a, BF16), pltpu.VMEM((chips,) + b, BF16),
            pltpu.VMEM((chips - 1,) + a, BF16), pltpu.VMEM((chips - 1,) + b, BF16),
            pltpu.VMEM((chips - 1,) + a, BF16), pltpu.VMEM((chips - 1,) + b, BF16),
            pltpu.VMEM(a, F32), pltpu.VMEM(b, F32), pltpu.VMEM(a, BF16), pltpu.VMEM(b, BF16),
            pltpu.VMEM((DEVICES,) + small.shape, F32),
            dma(2, 4), dma(2, chips), dma(2, chips), dma(2, chips), dma(2, chips),
            dma(2, DEVICES), dma(2, DEVICES), dma(2, DEVICES), dma(2, DEVICES), dma(DEVICES), dma(DEVICES),
        ],
        compiler_params=pltpu.CompilerParams(vmem_limit_bytes=62 * 1024 * 1024, collective_id=1, has_side_effects=True),
        cost_estimate=pl.CostEstimate(flops=2 * tokens * model * 6144, bytes_accessed=60_000_000, transcendentals=0),
        name="grads",
    )(ht, dy, small, o, dq, dk, dv)


def widen_kernel(ga_ref, gb_ref, wq_ref, wk_ref, wv_ref, wo_ref):
    q_cols, head_dim = wq_ref.shape[1], wk_ref.shape[1]
    wo_ref[...] = ga_ref[0].astype(F32)
    wq_ref[...] = gb_ref[0, :, :q_cols].astype(F32)
    wk_ref[...] = gb_ref[0, :, q_cols:q_cols + head_dim].astype(F32)
    wv_ref[...] = gb_ref[0, :, q_cols + head_dim:].astype(F32)


def widen_call(ga, gb):
    groups, q_cols, model = ga.shape
    head_dim = (gb.shape[2] - q_cols) // 2
    f32 = lambda *shape: jax.ShapeDtypeStruct(shape, F32)
    across = lambda g: (0, g)
    return pl.pallas_call(
        widen_kernel,
        grid=(groups,),
        in_specs=[pl.BlockSpec((1, q_cols, model), lambda g: (g, 0, 0)),
                  pl.BlockSpec((1, model, gb.shape[2]), lambda g: (g, 0, 0))],
        out_specs=[pl.BlockSpec((model, q_cols), across), pl.BlockSpec((model, head_dim), across),
                   pl.BlockSpec((model, head_dim), across), pl.BlockSpec((q_cols, model), lambda g: (g, 0))],
        out_shape=[f32(model, groups * q_cols), f32(model, groups * head_dim), f32(model, groups * head_dim),
                   f32(groups * q_cols, model)],
        compiler_params=pltpu.CompilerParams(dimension_semantics=("arbitrary",)),
        name="widen",
    )(ga, gb)


def solution(mesh):
    seq_spec = P(None, 'sp', None)
    replicated = P()

    def shard_body(hidden_in, grad_out, positions, w_q, w_k, w_v, w_o, g_in, q_norm, k_norm):
        batch, seq_dev, model_dim = hidden_in.shape
        head_dim = q_norm.shape[0]
        exponents = jnp.arange(0, head_dim, 2).astype(F32) / head_dim
        inv_freq = jnp.power(ROPE_THETA, -exponents)
        freq = jnp.concatenate([inv_freq, inv_freq])[None]
        pos = jnp.broadcast_to(jnp.pad(positions.astype(F32), ((0, 0), (0, head_dim - seq_dev)))[:, None, :], (batch, 8, head_dim))
        gains = (g_in.astype(F32)[None], q_norm.astype(F32)[None], k_norm.astype(F32)[None])
        hidden_out, grad_in, ht, dy, o, dq, dk, dv, dgin, dqn, dkn = block_call(
            hidden_in, grad_out, pos, freq, *gains, w_q, w_k, w_v, w_o)
        small = jnp.concatenate([dgin.reshape(-1, head_dim), dqn, dkn, jnp.zeros((6, head_dim), F32)], axis=0)
        flat = lambda t: t.reshape(-1, t.shape[-1])
        ga, gb, small = grads_call(ht, flat(dy), small, flat(o), flat(dq), flat(dk), flat(dv))
        grad_wq, grad_wk, grad_wv, grad_wo = widen_call(ga, gb)
        rows = model_dim // head_dim
        return (hidden_out, grad_in, grad_wq, grad_wk, grad_wv, grad_wo,
                small[:rows].reshape(-1), small[rows], small[rows + 1])

    return jax.shard_map(shard_body, mesh=mesh,
                         in_specs=(seq_spec, seq_spec, P(None, 'sp'), replicated, replicated, replicated, replicated, replicated, replicated, replicated),
                         out_specs=(seq_spec, seq_spec, replicated, replicated, replicated, replicated, replicated, replicated, replicated),
                         check_vma=False)
```

time: 684 us -> 475 us (0.69)
  Pallas kernels: 54.8 us -> 458 us
  local copies, waits for them, and re-layouts: 206 us -> 10.4 us
  waiting for transfers between devices: 106 us -> 0 us
  blocking collectives: 101 us -> 0 us
  starting transfers between devices: 90.8 us -> 0 us
  other arithmetic: 81 us -> 5.17 us
  matrix products: 35.2 us -> 0 us
    pallas_call x1 -> x3, Pallas kernels: 54.8 us -> 458 us  [the longest x1 273 us: block_call(): pl.pallas_call(block_kernel, grid=(seqs, groups), in_specs=[anywhere, any...]
    pallas_call x3 -> x0, local copies, waits for them, and re-layouts: 164 us -> none  [block_call(): pl.pallas_call(block_kernel, grid=(seqs, groups), in_specs=[pl.BlockSpec(...]
    all_to_all x13 -> x0, waiting for transfers between devices: 82 us -> none  [the longest x8 47.9 us: to_seq(): lax.all_to_all(values.reshape(group_size, seq_dev, model_dim), 'sp', 0, 0...]
    all_to_all x4 -> x0, blocking collectives: 69 us -> none  [to_batch(): lax.all_to_all(piece, 'sp', 0, 0, tiled=True).reshape(1, seq_len, model_dim)]
    ppermute x40 -> x0, starting transfers between devices: 54.5 us -> none  [swap(): return lax.ppermute(values, 'sp', [(d, d ^ axis_bit) for d in range(8)])]
    all_to_all x13 -> x0, starting transfers between devices: 36.3 us -> none  [the longest x8 20.9 us: to_seq(): lax.all_to_all(values.reshape(group_size, seq_dev, model_dim), 'sp', 0, 0...]
    dot_general x4 -> x0, matrix products: 35.2 us -> none  [dot(): return lax.dot_general(a, b, dims, preferred_element_type=jnp.float32)]
    psum x1 -> x0, blocking collectives: 31.9 us -> none  [shard_body(): small = lax.psum(tuple(small), 'sp')]
  transfers between devices with their start and end apart: 53 -> 0, of which waited for: 24 -> 0; matrix products, arithmetic and copies ran while one was open for 34% -> 0% of each run, Pallas kernels for 8% -> 0%
where the time goes in v2:
time: 475 us; the launch traced here: 474 us
  Pallas kernels  458 us (96%)
  local copies, waits for them, and re-layouts  10.4 us (2%)
  other arithmetic  5.17 us (1%)
    pallas_call x1, Pallas kernels, block_call(): pl.pallas_call(block_kernel, grid=(seqs, groups), in_specs=[anywhere, any...  273 us
    pallas_call x1, Pallas kernels, grads_call(): pl.pallas_call(grads_kernel, in_specs=[vmem, vmem, vmem, anywhere, anywhe...  171 us
    pallas_call x1, Pallas kernels, widen_call(): pl.pallas_call(widen_kernel, grid=(groups,), in_specs=[pl.BlockSpec((1, q...  14.1 us

profile of v2, /device:TPU:0, one launch (start us, length us, event | category | flops | bytes accessed | tf_op | source)
XLA Modules:
  0.0 474.1 jit_solution(2787956731945817696)
XLA Ops:
  0.7 0.1 pad.8.clone
  0.7 0.6 maximum_bitcast_fusion.freq_ref
  1.3 1.2 bitcast_convert_fusion
  2.5 1.3 broadcast_in_dim.36
  3.8 0.7 convert_element_type.13
  4.5 0.7 broadcast_in_dim.27.pos_hbm
  5.2 272.9 %block.1 = (bf16[32,64,1024]{2,1,0:T(8,128)(2,1)}, bf16[32,64,1024]{2,1,0:T(8,128)(2,1)}, bf16[1024,2048]{1,0:T(8,128)(2,1)}, bf16[4,512,1024]{2,1,0:T(8,128)(2,...) custom-call(bf16[32,64,1024]{2,1,0:T(8,128)(2,1)} %x_hbm.1, ...), custom_call_target="tpu_custom_call" | custom-call | flops 77309411328 | bytes 50000000 | tf_op jit(solution)/shard_map/block/pallas_call | solution.py:247
  278.1 1.4 maximum_maximum_fusion.small_ref
  279.5 170.8 %grads.1 = (bf16[8,256,1024]{2,1,0:T(8,128)(2,1)}, bf16[8,1024,512]{2,1,0:T(8,128)(2,1)}, f32[16,128]{1,0:T(8,128)}) custom-call(bf16[1024,2048]{1,0:T(8,128)(2,1)} %get-tuple-element.29.ht_ref, bf16[2048,1024]{1,0:T(8,128)(2,1)} %bitcast.25, f32[16,128]{1,0:T(8,128)} %maximum_maximum_fusion.small_ref, bf16[2048,2048]{1,0:T(8,128)(2,1)} %bitcast.23, ...), custom_call_target="tpu_custom_call" | custom-call | flops 25769803776 | bytes 60000000 | tf_op jit(solution)/shard_map/grads/pallas_call | solution.py:453
  450.4 1.3 slice_bitcast_fusion.1
  451.6 1.3 slice_bitcast_fusion
  452.9 14.1 %widen.1 = (f32[1024,2048]{1,0:T(8,128)}, f32[1024,1024]{1,0:T(8,128)}, f32[1024,1024]{1,0:T(8,128)}, f32[2048,1024]{1,0:T(8,128)}) custom-call(bf16[8,256,1024]{2,1,0:T(8,128)(2,1)} %get-tuple-element.38.ga_ref, bf16[8,1024,512]{2,1,0:T(8,128)(2,1)} %get-tuple-element.39.gb_ref), custom_call_target="tpu_custom_call" | custom-call | tf_op jit(solution)/shard_map/widen/pallas_call | solution.py:489
  467.0 0.0 copy-start
  467.0 5.1 %copy.21 = bf16[32,64,1024]{2,1,0:T(8,128)(2,1)} copy(bf16[32,64,1024]{2,1,0:T(8,128)(2,1)} %get-tuple-element.58) | data formatting | bytes 8388608
  472.1 0.0 copy-done
  472.1 2.0 copy.22
  (3 shorter events, 0.0 us)
Async XLA Ops:
  467.0 5.1 %copy-start = (bf16[32,64,1024]{2,1,0:T(8,128)(2,1)S(1)}, bf16[32,64,1024]{2,1,0:T(8,128)(2,1)}, u32[]{:S(2)}) copy-start(bf16[32,64,1024]{2,1,0:T(8,128)(2,1)} %get-tuple-element.59) | copy-start | bytes 12582916

commit v3 on v2

--- a/solution.py
+++ b/solution.py
@@ -9,6 +9,7 @@
 EPSILON = 1e-6
 ROPE_THETA = 1000000.0
 NEG_LARGE = -1e30
+LOG2_E = 1.4426950408889634
 NT = (((1,), (1,)), ((), ()))
 TN = (((0,), (0,)), ((), ()))
 ROW_BLOCK = 256
@@ -38,18 +39,22 @@
                                         device_id=(device,), device_id_type=pl.DeviceIdType.MESH)
 
 
-def block_kernel(x_hbm, dy_hbm, pos_hbm, freq_ref, gin_ref, qn_ref, kn_ref, wq_ref, wk_ref, wv_ref, wo_ref,
+def block_kernel(x_hbm, dy_hbm, pos_hbm, wq_hbm, wk_hbm, wv_hbm, wo_hbm, freq_ref, gin_ref, qn_ref, kn_ref,
                  out_hbm, gi_hbm, ht_ref, dyo_ref, o_ref, dq_ref, dk_ref, dv_ref, dgin_ref, dqn_ref, dkn_ref,
-                 xb, dyb, gib, posb, h_ref, cos_ref, sin_ref, out_acc, dh_acc, in_send, in_recv, out_send, out_recv):
+                 xb, dyb, gib, posb, wqkv, wo, h_ref, rope_cos, rope_sin, next_cos, next_sin, out_acc, dh_acc,
+                 q_next, k_next, v_next, do_next, v_now, do_now, o_now, dqkv_now, o_last, dqkv_last,
+                 weight_sem, in_send, in_recv, out_send, out_recv):
     seq, group = pl.program_id(0), pl.program_id(1)
     seqs, groups = pl.num_programs(0), pl.num_programs(1)
     me = lax.axis_index('sp')
     head_dim = qn_ref.shape[1]
-    per_kv = wq_ref.shape[1] // head_dim
+    q_cols = o_now.shape[1]
+    per_kv = q_cols // head_dim
     seq_len = xb.shape[1]
     piece = seq_len // DEVICES
     scale = head_dim ** -0.5
     half = head_dim // 2
+    tiles = [slice(i, i + ROW_BLOCK) for i in range(0, seq_len, ROW_BLOCK)]
 
     def rows_of(device):
         return pl.ds(pl.multiple_of(device * piece, piece), piece)
@@ -74,6 +79,80 @@
         return remote(src, dst.at[DEVICES * s + (peer if arrival else me)],
                       out_send.at[kind, s, step], out_recv.at[kind, s, step], peer)
 
+    def weight_loads():
+        copies = [pltpu.make_async_copy(wo_hbm.at[g * q_cols:(g + 1) * q_cols], wo.at[g], weight_sem.at[3, g]) for g in range(wo.shape[0])]
+        for i, src in enumerate((wq_hbm, wk_hbm, wv_hbm)):
+            start, size = (0, q_cols, q_cols + head_dim)[i], q_cols if i == 0 else head_dim
+            copies += [pltpu.make_async_copy(src.at[:, g * size:(g + 1) * size], wqkv.at[g, :, start:start + size], weight_sem.at[i, g])
+                       for g in range(wo.shape[0])]
+        return copies
+
+    def arrive(kind, s):
+        for step in range(DEVICES):
+            if step == 0:
+                incoming(kind, s, 0).wait()
+            else:
+                incoming(kind, s, step, arrival=True).wait_recv()
+
+    def prepare(s):
+        arrive(2, s)
+        on_diag = lax.broadcasted_iota(jnp.int32, (piece, head_dim), 0) == lax.broadcasted_iota(jnp.int32, (piece, head_dim), 1)
+        low = lax.broadcasted_iota(jnp.int32, (piece, head_dim), 1) < half
+        for device in range(DEVICES):
+            row = jnp.broadcast_to(posb[s, device, 0:1, :], (piece, head_dim))
+            column = jnp.sum(jnp.where(on_diag, row, 0.0), axis=-1, keepdims=True)
+            angles = column * freq_ref[...]
+            sin = jnp.sin(angles)
+            next_cos[device * piece:(device + 1) * piece, :] = jnp.cos(angles)
+            next_sin[device * piece:(device + 1) * piece, :] = jnp.where(low, -sin, sin)
+        arrive(0, s)
+        x = xb[s].astype(F32)
+        inv = lax.rsqrt(jnp.mean(x * x, axis=-1, keepdims=True) + EPSILON)
+        h_ref[...] = (x * inv * gin_ref[...]).astype(BF16)
+        arrive(1, s)
+
+    def project(s, g):
+        def q_rows(rows):
+            q_next[rows] = dot(h_ref[rows], wqkv[g, :, :q_cols])
+
+        def kv_rows(rows):
+            kv = dot(h_ref[rows], wqkv[g, :, q_cols:])
+            k_next[rows] = kv[:, :head_dim]
+            v_next[rows] = kv[:, head_dim:].astype(BF16)
+
+        def do_rows(rows):
+            do_next[rows] = dot(dyb[s, rows], wo[g], NT).astype(BF16)
+
+        return [functools.partial(f, rows) for f in (q_rows, kv_rows, do_rows) for rows in tiles]
+
+    def accumulate(g):
+        def out_cols(cols):
+            out_acc[:, cols] += dot(o_last[...], wo[g, :, cols])
+
+        def dh_cols(cols):
+            dh_acc[:, cols] += dot(dqkv_last[...], wqkv[g, cols, :], NT)
+
+        columns = [slice(c, c + 256) for c in range(0, out_acc.shape[1], 256)]
+        return [functools.partial(f, cols) for f in (out_cols, dh_cols) for cols in columns]
+
+    def run(products):
+        for product in products:
+            product()
+
+    def finish(s):
+        x = xb[s].astype(F32)
+        inv = lax.rsqrt(jnp.mean(x * x, axis=-1, keepdims=True) + EPSILON)
+        unit = x * inv
+        xb[s] = (x + out_acc[...]).astype(BF16)
+        d_norm = dh_acc[...]
+        dgin_ref[...] += jnp.sum(d_norm * unit, axis=0, keepdims=True)
+        d_unit = d_norm * gin_ref[...]
+        grad = inv * (d_unit - unit * jnp.mean(d_unit * unit, axis=-1, keepdims=True))
+        gib[s] = (dyb[s].astype(F32) + grad).astype(BF16)
+        for kind in range(2):
+            for step in (2, 4, 6, 3, 5, 7, 1, 0):
+                outgoing(kind, s, step).start()
+
     @pl.when((seq == 0) & (group == 0))
     def _():
         entry_barrier(me)
@@ -85,38 +164,34 @@
             return carry
 
         lax.fori_loop(0, seqs, send_all, 0)
+        for copy in weight_loads():
+            copy.start()
         dgin_ref[...] = jnp.zeros_like(dgin_ref)
         dqn_ref[...] = jnp.zeros_like(dqn_ref)
         dkn_ref[...] = jnp.zeros_like(dkn_ref)
+        o_now[...] = jnp.zeros_like(o_now)
+        dqkv_now[...] = jnp.zeros_like(dqkv_now)
+        out_acc[...] = jnp.zeros_like(out_acc)
+        dh_acc[...] = jnp.zeros_like(dh_acc)
+        for copy in weight_loads():
+            copy.wait()
+        prepare(0)
+        run(project(0, 0))
 
     @pl.when(group == 0)
     def _():
-        for kind in (2, 0, 1):
-            for step in range(DEVICES):
-                arrived = incoming(kind, seq, step, arrival=True)
-                if step == 0:
-                    arrived.wait()
-                else:
-                    arrived.wait_recv()
-        x = xb[seq].astype(F32)
-        inv = lax.rsqrt(jnp.mean(x * x, axis=-1, keepdims=True) + EPSILON)
-        h = (x * inv * gin_ref[...]).astype(BF16)
-        h_ref[...] = h
-        ht_ref[...] = h.T
+        rope_cos[...] = next_cos[...]
+        rope_sin[...] = next_sin[...]
+        ht_ref[...] = h_ref[...].T
         dyo_ref[0] = dyb[seq]
-        out_acc[...] = jnp.zeros_like(out_acc)
-        dh_acc[...] = jnp.zeros_like(dh_acc)
-        on_diag = lax.broadcasted_iota(jnp.int32, (piece, head_dim), 0) == lax.broadcasted_iota(jnp.int32, (piece, head_dim), 1)
-        low = lax.broadcasted_iota(jnp.int32, (piece, head_dim), 1) < half
-        for device in range(DEVICES):
-            row = jnp.broadcast_to(posb[seq, device, 0:1, :], (piece, head_dim))
-            column = jnp.sum(jnp.where(on_diag, row, 0.0), axis=-1, keepdims=True)
-            angles = column * freq_ref[...]
-            sin = jnp.sin(angles)
-            cos_ref[device * piece:(device + 1) * piece, :] = jnp.cos(angles)
-            sin_ref[device * piece:(device + 1) * piece, :] = jnp.where(low, -sin, sin)
-
-    cos, sin = cos_ref[...], sin_ref[...]
+
+    last_group = group == groups - 1
+
+    @pl.when(last_group & (seq < seqs - 1))
+    def _():
+        prepare(seq + 1)
+
+    cos, sin = rope_cos[...], rope_sin[...]
 
     def norm_rotate(t, gain):
         inv = lax.rsqrt(jnp.mean(t * t, axis=-1, keepdims=True) + EPSILON)
@@ -130,88 +205,97 @@
         d_unit = d_scaled * gain
         return inv * (d_unit - unit * jnp.mean(d_unit * unit, axis=-1, keepdims=True)), d_gain
 
-    h = h_ref[...]
-    q_proj = dot(h, wq_ref[...])
-    k_proj = dot(h, wk_ref[...])
-    v = dot(h, wv_ref[...]).astype(BF16)
-    d_o = dot(dyb[seq], wo_ref[...], NT).astype(BF16)
-    k_rot, k_unit, k_inv = norm_rotate(k_proj, kn_ref[...])
-
-    blocks = seq_len // ROW_BLOCK
-    dk_parts = [None] * blocks
-    dv_parts = [None] * blocks
-    rows_id = lax.broadcasted_iota(jnp.int32, (ROW_BLOCK, ROW_BLOCK), 0)
-    cols_id = lax.broadcasted_iota(jnp.int32, (ROW_BLOCK, ROW_BLOCK), 1)
-    causal = rows_id >= cols_id
-    dqn_sum = None
-    for head in range(per_kv):
-        lanes = slice(head * head_dim, (head + 1) * head_dim)
-        q_rot, q_unit, q_inv = norm_rotate(q_proj[:, lanes], qn_ref[...])
-        do_head = d_o[:, lanes]
-        dq_rows = []
-        o_rows = []
-        for i in range(blocks):
-            rows = slice(i * ROW_BLOCK, (i + 1) * ROW_BLOCK)
-            q_i, do_i = q_rot[rows], do_head[rows]
-            s_parts = []
-            for j in range(i + 1):
-                s = dot(q_i, k_rot[j * ROW_BLOCK:(j + 1) * ROW_BLOCK], NT)
-                if j == i:
-                    s = jnp.where(causal, s, NEG_LARGE)
-                s_parts.append(s)
-            top = functools.reduce(jnp.maximum, [jnp.max(s, axis=-1, keepdims=True) for s in s_parts])
-            e_parts = [jnp.exp((s - top) * scale) for s in s_parts]
-            total = functools.reduce(jnp.add, [jnp.sum(e, axis=-1, keepdims=True) for e in e_parts])
-            recip = 1.0 / total
-            p_parts = [e * recip for e in e_parts]
-            pb_parts = [p.astype(BF16) for p in p_parts]
-            o_i = None
-            for j in range(i + 1):
-                part = dot(pb_parts[j], v[j * ROW_BLOCK:(j + 1) * ROW_BLOCK])
-                o_i = part if o_i is None else o_i + part
-            o_rows.append(o_i.astype(BF16))
-            dp_parts = [dot(do_i, v[j * ROW_BLOCK:(j + 1) * ROW_BLOCK], NT) for j in range(i + 1)]
-            delta = functools.reduce(jnp.add, [jnp.sum(p * dp, axis=-1, keepdims=True) for p, dp in zip(p_parts, dp_parts)])
-            ds_parts = [(p * (dp - delta)).astype(BF16) for p, dp in zip(p_parts, dp_parts)]
-            dq_i = None
-            for j in range(i + 1):
-                cols = slice(j * ROW_BLOCK, (j + 1) * ROW_BLOCK)
-                part = dot(ds_parts[j], k_rot[cols])
-                dq_i = part if dq_i is None else dq_i + part
-                dk_j = dot(ds_parts[j], q_i, TN)
-                dv_j = dot(pb_parts[j], do_i, TN)
-                dk_parts[j] = dk_j if dk_parts[j] is None else dk_parts[j] + dk_j
-                dv_parts[j] = dv_j if dv_parts[j] is None else dv_parts[j] + dv_j
-            dq_rows.append(dq_i)
-        o_ref[0, :, lanes] = jnp.concatenate(o_rows, axis=0)
-        dq_head, d_gain = norm_rotate_back(jnp.concatenate(dq_rows, axis=0) * scale, q_unit, q_inv, qn_ref[...])
-        dqn_sum = d_gain if dqn_sum is None else dqn_sum + d_gain
-        dq_ref[0, :, lanes] = dq_head.astype(BF16)
-    dqn_ref[...] += dqn_sum
+    v_now[...] = v_next[...]
+    do_now[...] = do_next[...]
+    o_last[...] = o_now[...]
+    dqkv_last[...] = dqkv_now[...]
+
+    ahead = project(jnp.minimum(seq + last_group.astype(jnp.int32), seqs - 1), (group + 1) % groups)
+    behind = accumulate((group + groups - 1) % groups)
+    lanes = [slice(head * head_dim, (head + 1) * head_dim) for head in range(per_kv)]
+    stacked = per_kv * ROW_BLOCK
+    rows_id = lax.broadcasted_iota(jnp.int32, (stacked, ROW_BLOCK), 0) % ROW_BLOCK
+    causal = rows_id >= lax.broadcasted_iota(jnp.int32, (stacked, ROW_BLOCK), 1)
+    blocks = len(tiles)
+
+    run(behind[:6])
+    k_rot, k_unit, k_inv = norm_rotate(k_next[...], kn_ref[...])
+    q_parts = [norm_rotate(q_next[:, lane], qn_ref[...]) for lane in lanes]
+    q_tile = [jnp.concatenate([part[0][tile] for part in q_parts], axis=0) for tile in tiles]
+    do_tile = [jnp.concatenate([do_now[tile, lane] for lane in lanes], axis=0) for tile in tiles]
+
+    def scores(i):
+        s_parts = [dot(q_tile[i], k_rot[tiles[j]], NT) for j in range(i + 1)]
+        s_parts[i] = jnp.where(causal, s_parts[i], NEG_LARGE)
+        return s_parts
+
+    def softmax(s_parts):
+        top = functools.reduce(jnp.maximum, [jnp.max(s, axis=-1, keepdims=True) for s in s_parts])
+        e_parts = [jnp.exp2((s - top) * (scale * LOG2_E)) for s in s_parts]
+        recip = 1.0 / functools.reduce(jnp.add, [jnp.sum(e, axis=-1, keepdims=True) for e in e_parts])
+        p_parts = [e * recip for e in e_parts]
+        return p_parts, [p.astype(BF16) for p in p_parts]
+
+    def softmax_back(p_parts, dp_parts):
+        delta = functools.reduce(jnp.add, [jnp.sum(p * dp, axis=-1, keepdims=True) for p, dp in zip(p_parts, dp_parts)])
+        return [(p * (dp - delta)).astype(BF16) for p, dp in zip(p_parts, dp_parts)]
+
+    def rows_sum(parts, values):
+        return functools.reduce(jnp.add, [dot(part, values[tiles[j]]) for j, part in enumerate(parts)])
+
+    def store_output(i, o_i):
+        for head, lane in enumerate(lanes):
+            o_head = o_i[head * ROW_BLOCK:(head + 1) * ROW_BLOCK].astype(BF16)
+            o_ref[0, tiles[i], lane] = o_head
+            o_now[tiles[i], lane] = o_head
+
+    fill = [ahead[0:2], behind[6:7], behind[7:8] + ahead[2:3], ahead[3:4]]
+    s_all = [scores(i) for i in range(blocks)]
+    dp_all = [[dot(do_tile[i], v_now[tiles[j]], NT) for j in range(i + 1)] for i in range(blocks)]
+    dk_parts, dv_parts, dq_tile = [None] * blocks, [None] * blocks, []
+    for i in range(blocks):
+        p_parts, pb_parts = softmax(s_all[i])
+        run(fill[2 * i])
+        store_output(i, rows_sum(pb_parts, v_now))
+        for j in range(i + 1):
+            dv_j = dot(pb_parts[j], do_tile[i], TN)
+            dv_parts[j] = dv_j if dv_parts[j] is None else dv_parts[j] + dv_j
+        ds_parts = softmax_back(p_parts, dp_all[i])
+        run(fill[2 * i + 1])
+        dq_tile.append(rows_sum(ds_parts, k_rot))
+        for j in range(i + 1):
+            dk_j = dot(ds_parts[j], q_tile[i], TN)
+            dk_parts[j] = dk_j if dk_parts[j] is None else dk_parts[j] + dk_j
+    run(ahead[4:])
+    for head, lane in enumerate(lanes):
+        dq_head = jnp.concatenate([dq[head * ROW_BLOCK:(head + 1) * ROW_BLOCK] for dq in dq_tile], axis=0)
+        dq_head, d_gain = norm_rotate_back(dq_head * scale, q_parts[head][1], q_parts[head][2], qn_ref[...])
+        dqn_ref[...] += d_gain
+        dq_head = dq_head.astype(BF16)
+        dq_ref[0, :, lane] = dq_head
+        dqkv_now[:, lane] = dq_head
     dk_head, d_gain = norm_rotate_back(jnp.concatenate(dk_parts, axis=0) * scale, k_unit, k_inv, kn_ref[...])
     dkn_ref[...] += d_gain
-    dk_ref[0] = dk_head.astype(BF16)
-    dv_ref[0] = jnp.concatenate(dv_parts, axis=0).astype(BF16)
-    out_acc[...] += dot(o_ref[0], wo_ref[...])
-    dh_acc[...] += dot(dq_ref[0], wq_ref[...], NT) + dot(dk_ref[0], wk_ref[...], NT) + dot(dv_ref[0], wv_ref[...], NT)
-
-    @pl.when(group == groups - 1)
+    dk_head = dk_head.astype(BF16)
+    dk_ref[0] = dk_head
+    dqkv_now[:, q_cols:q_cols + head_dim] = dk_head
+    dv_head = jnp.concatenate(dv_parts, axis=0).astype(BF16)
+    dv_ref[0] = dv_head
+    dqkv_now[:, q_cols + head_dim:] = dv_head
+
+    @pl.when((group == 0) & (seq > 0))
     def _():
-        x = xb[seq].astype(F32)
-        inv = lax.rsqrt(jnp.mean(x * x, axis=-1, keepdims=True) + EPSILON)
-        unit = x * inv
-        xb[seq] = (x + out_acc[...]).astype(BF16)
-        d_norm = dh_acc[...]
-        dgin_ref[...] += jnp.sum(d_norm * unit, axis=0, keepdims=True)
-        d_unit = d_norm * gin_ref[...]
-        grad = inv * (d_unit - unit * jnp.mean(d_unit * unit, axis=-1, keepdims=True))
-        gib[seq] = (dyb[seq].astype(F32) + grad).astype(BF16)
-        for kind in range(2):
-            for step in (2, 4, 6, 3, 5, 7, 1, 0):
-                outgoing(kind, seq, step).start()
-
-    @pl.when((seq == seqs - 1) & (group == groups - 1))
+        finish(seq - 1)
+        out_acc[...] = jnp.zeros_like(out_acc)
+        dh_acc[...] = jnp.zeros_like(dh_acc)
+
+    @pl.when((seq == seqs - 1) & last_group)
     def _():
+        o_last[...] = o_now[...]
+        dqkv_last[...] = dqkv_now[...]
+        run(accumulate(groups - 1))
+        finish(seqs - 1)
+
         def drain(s, carry):
             for step in range(1, DEVICES):
                 for kind in range(3):
@@ -236,27 +320,25 @@
     groups = kv_width // head_dim
     q_cols = q_width // groups
     tokens = seqs * seq_len
+    width = q_cols + 2 * head_dim
     row = lambda s, g: (s, 0, 0)
     col = lambda s, g: (s, 0, g)
     fixed = lambda s, g: (0, 0)
-    wcol = lambda s, g: (0, g)
     bf = lambda *shape: jax.ShapeDtypeStruct(shape, BF16)
     f32 = lambda *shape: jax.ShapeDtypeStruct(shape, F32)
     anywhere = pl.BlockSpec(memory_space=pl.ANY)
     flops = 4 * tokens * model * (q_width * 2 + kv_width * 2) + 12 * tokens * seq_len * q_width
+    vb = lambda *shape: pltpu.VMEM(shape, BF16)
+    vf = lambda *shape: pltpu.VMEM(shape, F32)
     return pl.pallas_call(
         block_kernel,
         grid=(seqs, groups),
         in_specs=[
-            anywhere, anywhere, anywhere,
+            anywhere, anywhere, anywhere, anywhere, anywhere, anywhere, anywhere,
             pl.BlockSpec((1, head_dim), fixed),
             pl.BlockSpec((1, model), fixed),
             pl.BlockSpec((1, head_dim), fixed),
             pl.BlockSpec((1, head_dim), fixed),
-            pl.BlockSpec((model, q_cols), wcol),
-            pl.BlockSpec((model, head_dim), wcol),
-            pl.BlockSpec((model, head_dim), wcol),
-            pl.BlockSpec((q_cols, model), lambda s, g: (g, 0)),
         ],
         out_specs=[
             anywhere, anywhere,
@@ -278,15 +360,16 @@
             f32(1, model), f32(1, head_dim), f32(1, head_dim),
         ],
         scratch_shapes=[
-            pltpu.VMEM((seqs, seq_len, model), BF16),
-            pltpu.VMEM((seqs, seq_len, model), BF16),
-            pltpu.VMEM((seqs, seq_len, model), BF16),
-            pltpu.VMEM((seqs, DEVICES, 8, head_dim), F32),
-            pltpu.VMEM((seq_len, model), BF16),
-            pltpu.VMEM((seq_len, head_dim), F32),
-            pltpu.VMEM((seq_len, head_dim), F32),
-            pltpu.VMEM((seq_len, model), F32),
-            pltpu.VMEM((seq_len, model), F32),
+            vb(seqs, seq_len, model), vb(seqs, seq_len, model), vb(seqs, seq_len, model),
+            vf(seqs, DEVICES, 8, head_dim),
+            vb(groups, model, width), vb(groups, q_cols, model),
+            vb(seq_len, model),
+            vf(seq_len, head_dim), vf(seq_len, head_dim), vf(seq_len, head_dim), vf(seq_len, head_dim),
+            vf(seq_len, model), vf(seq_len, model),
+            vf(seq_len, q_cols), vf(seq_len, head_dim), vb(seq_len, head_dim), vb(seq_len, q_cols),
+            vb(seq_len, head_dim), vb(seq_len, q_cols),
+            vb(seq_len, q_cols), vb(seq_len, width), vb(seq_len, q_cols), vb(seq_len, width),
+            pltpu.SemaphoreType.DMA((4, groups)),
             pltpu.SemaphoreType.DMA((3, seqs, DEVICES)),
             pltpu.SemaphoreType.DMA((3, seqs, DEVICES)),
             pltpu.SemaphoreType.DMA((2, seqs, DEVICES)),
@@ -297,7 +380,7 @@
             collective_id=0, has_side_effects=True),
         cost_estimate=pl.CostEstimate(flops=flops, bytes_accessed=50_000_000, transcendentals=tokens * seq_len * 8),
         name="block",
-    )(x, dy, pos, freq, g_in, q_norm, k_norm, w_q, w_k, w_v, w_o)
+    )(x, dy, pos, w_q, w_k, w_v, w_o, freq, g_in, q_norm, k_norm)
 
 
 def grads_kernel(ht_ref, dy_ref, small_ref, o_hbm, dq_hbm, dk_hbm, dv_hbm,

time: 475 us -> 418 us (0.88)
  Pallas kernels: 458 us -> 401 us
    pallas_call x1, Pallas kernels: 273 us -> 216 us  [block_call(): pl.pallas_call(block_kernel, grid=(seqs, groups), in_specs=[anywhere, any...]
where the time goes in v3:
time: 418 us; the launch traced here: 417 us
  Pallas kernels  401 us (96%)
  local copies, waits for them, and re-layouts  10.4 us (2%)
  other arithmetic  5.17 us (1%)
    pallas_call x1, Pallas kernels, block_call(): pl.pallas_call(block_kernel, grid=(seqs, groups), in_specs=[anywhere, any...  216 us
    pallas_call x1, Pallas kernels, grads_call(): pl.pallas_call(grads_kernel, in_specs=[vmem, vmem, vmem, anywhere, anywhe...  171 us
    pallas_call x1, Pallas kernels, widen_call(): pl.pallas_call(widen_kernel, grid=(groups,), in_specs=[pl.BlockSpec((1, q...  14.1 us

profile of v3, /device:TPU:0, one launch (start us, length us, event | category | flops | bytes accessed | tf_op | source)
XLA Modules:
  0.0 417.1 jit_solution(6302437837341419584)
XLA Ops:
  0.7 0.1 pad.8.clone
  0.7 0.6 maximum_bitcast_fusion.freq_ref
  1.3 1.2 bitcast_convert_fusion
  2.5 1.3 broadcast_in_dim.36
  3.8 0.7 convert_element_type.13
  4.5 0.7 broadcast_in_dim.27.pos_hbm
  5.2 215.9 %block.1 = (bf16[32,64,1024]{2,1,0:T(8,128)(2,1)}, bf16[32,64,1024]{2,1,0:T(8,128)(2,1)}, bf16[1024,2048]{1,0:T(8,128)(2,1)}, bf16[4,512,1024]{2,1,0:T(8,128)(2,...) custom-call(bf16[32,64,1024]{2,1,0:T(8,128)(2,1)} %x_hbm.1, ...), custom_call_target="tpu_custom_call" | custom-call | flops 77309411328 | bytes 50000000 | tf_op jit(solution)/shard_map/block/pallas_call | solution.py:333
  221.1 1.4 maximum_maximum_fusion.small_ref
  222.5 170.8 %grads.1 = (bf16[8,256,1024]{2,1,0:T(8,128)(2,1)}, bf16[8,1024,512]{2,1,0:T(8,128)(2,1)}, f32[16,128]{1,0:T(8,128)}) custom-call(bf16[1024,2048]{1,0:T(8,128)(2,1)} %get-tuple-element.29.ht_ref, bf16[2048,1024]{1,0:T(8,128)(2,1)} %bitcast.25, f32[16,128]{1,0:T(8,128)} %maximum_maximum_fusion.small_ref, bf16[2048,2048]{1,0:T(8,128)(2,1)} %bitcast.23, ...), custom_call_target="tpu_custom_call" | custom-call | flops 25769803776 | bytes 60000000 | tf_op jit(solution)/shard_map/grads/pallas_call | solution.py:536
  393.3 1.3 slice_bitcast_fusion.1
  394.6 1.3 slice_bitcast_fusion
  395.9 14.1 %widen.1 = (f32[1024,2048]{1,0:T(8,128)}, f32[1024,1024]{1,0:T(8,128)}, f32[1024,1024]{1,0:T(8,128)}, f32[2048,1024]{1,0:T(8,128)}) custom-call(bf16[8,256,1024]{2,1,0:T(8,128)(2,1)} %get-tuple-element.38.ga_ref, bf16[8,1024,512]{2,1,0:T(8,128)(2,1)} %get-tuple-element.39.gb_ref), custom_call_target="tpu_custom_call" | custom-call | tf_op jit(solution)/shard_map/widen/pallas_call | solution.py:572
  410.0 0.0 copy-start
  410.0 5.1 %copy.21 = bf16[32,64,1024]{2,1,0:T(8,128)(2,1)} copy(bf16[32,64,1024]{2,1,0:T(8,128)(2,1)} %get-tuple-element.58) | data formatting | bytes 8388608
  415.0 0.0 copy-done
  415.0 2.0 copy.22
  (3 shorter events, 0.0 us)
Async XLA Ops:
  410.0 5.1 %copy-start = (bf16[32,64,1024]{2,1,0:T(8,128)(2,1)S(1)}, bf16[32,64,1024]{2,1,0:T(8,128)(2,1)}, u32[]{:S(2)}) copy-start(bf16[32,64,1024]{2,1,0:T(8,128)(2,1)} %get-tuple-element.59) | copy-start | bytes 12582916

commit v4 on v3

v4 whole, which is shorter than its diff:
```python
import functools
import jax
import jax.numpy as jnp
from jax import lax
from jax.experimental import pallas as pl
from jax.experimental.pallas import tpu as pltpu
from jax.sharding import PartitionSpec as P

EPSILON = 1e-6
ROPE_THETA = 1000000.0
NEG_LARGE = -1e30
LOG2_E = 1.4426950408889634
NT = (((1,), (1,)), ((), ()))
TN = (((0,), (0,)), ((), ()))
ROW_BLOCK = 256
DEVICES = 8
BF16 = jnp.bfloat16
F32 = jnp.float32


def dot(a, b, dims=(((1,), (0,)), ((), ()))):
    return lax.dot_general(a, b, dims, preferred_element_type=F32)


def peer_of(me, step):
    core, x, y = me % 2, (me // 2) % 2, me // 4
    return ((y + step // 4) % 2) * 4 + ((x + (step // 2) % 2) % 2) * 2 + (core + step % 2) % 2


def entry_barrier(me):
    barrier = pltpu.get_barrier_semaphore()
    for step in range(1, DEVICES):
        pl.semaphore_signal(barrier, inc=1, device_id=(peer_of(me, step),), device_id_type=pl.DeviceIdType.MESH)
    pl.semaphore_wait(barrier, DEVICES - 1)


def remote(src, dst, send, recv, device):
    return pltpu.make_async_remote_copy(src_ref=src, dst_ref=dst, send_sem=send, recv_sem=recv,
                                        device_id=(device,), device_id_type=pl.DeviceIdType.MESH)


def block_kernel(x_hbm, dy_hbm, pos_hbm, wq_hbm, wk_hbm, wv_hbm, wo_hbm, gains_ref,
                 out_hbm, gi_hbm, ga_hbm, gb_hbm, o_hbm, dqkv_hbm, small_out,
                 xb, dyb, gib, posb, wqkv, wo, h_ref, ht_ref, rope_cos, rope_sin, next_cos, next_sin, out_acc, dh_acc,
                 q_next, k_next, v_next, do_next, v_now, do_now, o_now, dqkv_now, o_last, dqkv_last, o_stage, dqkv_stage,
                 dgin_ref, dqn_ref, dkn_ref, small, smallb, ob, qkvb, l1a, l1b, t_a, t_b, l2a, l2b,
                 weight_sem, in_send, in_recv, out_send, out_recv, store_sem, load_sem, pair_send, pair_recv,
                 turn_send, turn_recv, chip_send, chip_recv, all_send, all_recv, small_send, small_recv):
    seq, group = pl.program_id(0), pl.program_id(1)
    seqs, groups = pl.num_programs(0), pl.num_programs(1)
    me = lax.axis_index('sp')
    head_dim, model = dqn_ref.shape[1], dgin_ref.shape[1]
    gin_ref = gains_ref.at[:, pl.ds(0, model)]
    qn_ref, kn_ref, freq_ref = (gains_ref.at[:, pl.ds(model + i * head_dim, head_dim)] for i in range(3))
    q_cols = o_now.shape[1]
    per_kv = q_cols // head_dim
    seq_len = xb.shape[1]
    piece = seq_len // DEVICES
    scale = head_dim ** -0.5
    half = head_dim // 2
    tiles = [slice(i, i + ROW_BLOCK) for i in range(0, seq_len, ROW_BLOCK)]

    def rows_of(device):
        return pl.ds(pl.multiple_of(device * piece, piece), piece)

    def incoming(kind, s, step, arrival=False):
        peer = peer_of(me, step)
        src = (x_hbm, dy_hbm, pos_hbm)[kind].at[DEVICES * s + peer]

        def landing(device):
            return posb.at[s, device] if kind == 2 else (xb, dyb)[kind].at[s, rows_of(device)]

        if step == 0:
            return pltpu.make_async_copy(src, landing(me), in_recv.at[kind, s, 0])
        return remote(src, landing(peer if arrival else me), in_send.at[kind, s, step], in_recv.at[kind, s, step], peer)

    def outgoing(kind, s, step, arrival=False):
        peer = peer_of(me, step)
        src = xb.at[s, rows_of(peer)] if kind == 0 else gib.at[s % 2, rows_of(peer)]
        dst = (out_hbm, gi_hbm)[kind]
        if step == 0:
            return pltpu.make_async_copy(src, dst.at[DEVICES * s + me], out_recv.at[kind, s, 0])
        return remote(src, dst.at[DEVICES * s + (peer if arrival else me)],
                      out_send.at[kind, s, step], out_recv.at[kind, s, step], peer)

    def sent(kind, s):
        outgoing(kind, s, 0).wait()
        for step in range(1, DEVICES):
            outgoing(kind, s, step).wait_send()

    def weight_loads():
        copies = [pltpu.make_async_copy(wo_hbm.at[g * q_cols:(g + 1) * q_cols], wo.at[g], weight_sem.at[3, g]) for g in range(wo.shape[0])]
        for i, src in enumerate((wq_hbm, wk_hbm, wv_hbm)):
            start, size = (0, q_cols, q_cols + head_dim)[i], q_cols if i == 0 else head_dim
            copies += [pltpu.make_async_copy(src.at[:, g * size:(g + 1) * size], wqkv.at[g, :, start:start + size], weight_sem.at[i, g])
                       for g in range(wo.shape[0])]
        return copies

    def arrive(kind, s):
        for step in range(DEVICES):
            if step == 0:
                incoming(kind, s, 0).wait()
            else:
                incoming(kind, s, step, arrival=True).wait_recv()

    def prepare(s):
        arrive(2, s)
        on_diag = lax.broadcasted_iota(jnp.int32, (piece, head_dim), 0) == lax.broadcasted_iota(jnp.int32, (piece, head_dim), 1)
        low = lax.broadcasted_iota(jnp.int32, (piece, head_dim), 1) < half
        half_count = DEVICES // 2

        def column(device):
            row = jnp.broadcast_to(posb[s, device, 0:1, :], (piece, head_dim))
            return jnp.sum(jnp.where(on_diag, row, 0.0), axis=-1, keepdims=True)

        for device in range(half_count):
            angles = jnp.where(low, column(device), column(device + half_count)) * freq_ref[...]
            cos, sin = jnp.cos(angles), jnp.sin(angles)
            cos_turned, sin_turned = pltpu.roll(cos, half, 1), pltpu.roll(sin, half, 1)
            first = slice(device * piece, (device + 1) * piece)
            second = slice((device + half_count) * piece, (device + half_count + 1) * piece)
            next_cos[first, :] = jnp.where(low, cos, cos_turned)
            next_sin[first, :] = jnp.where(low, -sin, sin_turned)
            next_cos[second, :] = jnp.where(low, cos_turned, cos)
            next_sin[second, :] = jnp.where(low, -sin_turned, sin)
        arrive(0, s)
        x = xb[s].astype(F32)
        inv = lax.rsqrt(jnp.mean(x * x, axis=-1, keepdims=True) + EPSILON)
        h_ref[...] = (x * inv * gin_ref[...]).astype(BF16)
        arrive(1, s)

    def project(s, g):
        def q_rows(rows):
            q_next[rows] = dot(h_ref[rows], wqkv[g, :, :q_cols])

        def kv_rows(rows):
            kv = dot(h_ref[rows], wqkv[g, :, q_cols:])
            k_next[rows] = kv[:, :head_dim]
            v_next[rows] = kv[:, head_dim:].astype(BF16)

        def do_rows(rows):
            do_next[rows] = dot(dyb[s, rows], wo[g], NT).astype(BF16)

        return [functools.partial(f, rows) for f in (q_rows, kv_rows, do_rows) for rows in tiles]

    def accumulate(g):
        def out_cols(cols):
            out_acc[:, cols] += dot(o_last[...], wo[g, :, cols])

        def dh_cols(cols):
            dh_acc[:, cols] += dot(dqkv_last[...], wqkv[g, cols, :], NT)

        columns = [slice(c, c + 256) for c in range(0, out_acc.shape[1], 256)]
        return [functools.partial(f, cols) for f in (out_cols, dh_cols) for cols in columns]

    def run(products):
        for product in products:
            product()

    def finish(s):
        x = xb[s].astype(F32)
        inv = lax.rsqrt(jnp.mean(x * x, axis=-1, keepdims=True) + EPSILON)
        unit = x * inv
        xb[s] = (x + out_acc[...]).astype(BF16)
        d_norm = dh_acc[...]
        dgin_ref[...] += jnp.sum(d_norm * unit, axis=0, keepdims=True)
        d_unit = d_norm * gin_ref[...]
        grad = inv * (d_unit - unit * jnp.mean(d_unit * unit, axis=-1, keepdims=True))

        @pl.when(s >= 2)
        def _():
            sent(1, s - 2)

        gib[s % 2] = (dyb[s].astype(F32) + grad).astype(BF16)
        for kind in range(2):
            for step in (2, 4, 6, 3, 5, 7, 1, 0):
                outgoing(kind, s, step).start()

    @pl.when((seq == 0) & (group == 0))
    def _():
        entry_barrier(me)

        def send_all(s, carry):
            for kind in (2, 0, 1):
                for step in (2, 4, 6, 3, 5, 7, 1, 0):
                    incoming(kind, s, step).start()
            return carry

        lax.fori_loop(0, seqs, send_all, 0)
        for copy in weight_loads():
            copy.start()
        dgin_ref[...] = jnp.zeros_like(dgin_ref)
        dqn_ref[...] = jnp.zeros_like(dqn_ref)
        dkn_ref[...] = jnp.zeros_like(dkn_ref)
        o_now[...] = jnp.zeros_like(o_now)
        dqkv_now[...] = jnp.zeros_like(dqkv_now)
        out_acc[...] = jnp.zeros_like(out_acc)
        dh_acc[...] = jnp.zeros_like(dh_acc)
        for copy in weight_loads():
            copy.wait()
        prepare(0)
        run(project(0, 0))

    @pl.when(group == 0)
    def _():
        rope_cos[...] = next_cos[...]
        rope_sin[...] = next_sin[...]
        ht_ref[:, pl.ds(pl.multiple_of(seq * seq_len, seq_len), seq_len)] = h_ref[...].T

    last_group = group == groups - 1

    @pl.when(last_group & (seq < seqs - 1))
    def _():
        prepare(seq + 1)

    cos, sin = rope_cos[...], rope_sin[...]

    def norm_rotate(t, gain):
        inv = lax.rsqrt(jnp.mean(t * t, axis=-1, keepdims=True) + EPSILON)
        unit = t * inv
        scaled = unit * gain
        return (scaled * cos + pltpu.roll(scaled, half, 1) * sin).astype(BF16), unit, inv

    def norm_rotate_back(grad, unit, inv, gain):
        d_scaled = grad * cos - pltpu.roll(grad, half, 1) * sin
        d_gain = jnp.sum(d_scaled * unit, axis=0, keepdims=True)
        d_unit = d_scaled * gain
        return inv * (d_unit - unit * jnp.mean(d_unit * unit, axis=-1, keepdims=True)), d_gain

    step_id = seq * groups + group
    slot = step_id % 2

    def stores(step):
        g, rows = step % groups, pl.ds(pl.multiple_of((step // groups) * seq_len, seq_len), seq_len)
        return [pltpu.make_async_copy(o_stage.at[step % 2], o_hbm.at[g, rows], store_sem.at[0, step % 2]),
                pltpu.make_async_copy(dqkv_stage.at[step % 2], dqkv_hbm.at[g, rows], store_sem.at[1, step % 2])]

    @pl.when(step_id >= 2)
    def _():
        for copy in stores(step_id - 2):
            copy.wait()

    @pl.when(step_id >= 1)
    def _():
        for copy in stores(step_id - 1):
            copy.start()

    v_now[...] = v_next[...]
    do_now[...] = do_next[...]
    o_last[...] = o_now[...]
    dqkv_last[...] = dqkv_now[...]

    ahead = project(jnp.minimum(seq + last_group.astype(jnp.int32), seqs - 1), (group + 1) % groups)
    behind = accumulate((group + groups - 1) % groups)
    lanes = [slice(head * head_dim, (head + 1) * head_dim) for head in range(per_kv)]
    stacked = per_kv * ROW_BLOCK
    rows_id = lax.broadcasted_iota(jnp.int32, (stacked, ROW_BLOCK), 0) % ROW_BLOCK
    causal = rows_id >= lax.broadcasted_iota(jnp.int32, (stacked, ROW_BLOCK), 1)
    blocks = len(tiles)

    run(behind[:6])
    k_rot, k_unit, k_inv = norm_rotate(k_next[...], kn_ref[...])
    q_parts = [norm_rotate(q_next[:, lane], qn_ref[...]) for lane in lanes]
    q_tile = [jnp.concatenate([part[0][tile] for part in q_parts], axis=0) for tile in tiles]
    do_tile = [jnp.concatenate([do_now[tile, lane] for lane in lanes], axis=0) for tile in tiles]

    def scores(i):
        s_parts = [dot(q_tile[i], k_rot[tiles[j]], NT) for j in range(i + 1)]
        s_parts[i] = jnp.where(causal, s_parts[i], NEG_LARGE)
        return s_parts

    def softmax(s_parts):
        top = functools.reduce(jnp.maximum, [jnp.max(s, axis=-1, keepdims=True) for s in s_parts])
        e_parts = [jnp.exp2((s - top) * (scale * LOG2_E)) for s in s_parts]
        recip = 1.0 / functools.reduce(jnp.add, [jnp.sum(e, axis=-1, keepdims=True) for e in e_parts])
        p_parts = [e * recip for e in e_parts]
        return p_parts, [p.astype(BF16) for p in p_parts]

    def softmax_back(p_parts, dp_parts):
        delta = functools.reduce(jnp.add, [jnp.sum(p * dp, axis=-1, keepdims=True) for p, dp in zip(p_parts, dp_parts)])
        return [(p * (dp - delta)).astype(BF16) for p, dp in zip(p_parts, dp_parts)]

    def rows_sum(parts, values):
        return functools.reduce(jnp.add, [dot(part, values[tiles[j]]) for j, part in enumerate(parts)])

    def store_output(i, o_i):
        for head, lane in enumerate(lanes):
            o_head = o_i[head * ROW_BLOCK:(head + 1) * ROW_BLOCK].astype(BF16)
            o_stage[slot, tiles[i], lane] = o_head
            o_now[tiles[i], lane] = o_head

    fill = [ahead[0:2], behind[6:7], behind[7:8] + ahead[2:3], ahead[3:4]]
    s_all = [scores(i) for i in range(blocks)]
    dp_all = [[dot(do_tile[i], v_now[tiles[j]], NT) for j in range(i + 1)] for i in range(blocks)]
    dk_parts, dv_parts, dq_tile = [None] * blocks, [None] * blocks, []
    for i in range(blocks):
        p_parts, pb_parts = softmax(s_all[i])
        run(fill[2 * i])
        store_output(i, rows_sum(pb_parts, v_now))
        for j in range(i + 1):
            dv_j = dot(pb_parts[j], do_tile[i], TN)
            dv_parts[j] = dv_j if dv_parts[j] is None else dv_parts[j] + dv_j
        ds_parts = softmax_back(p_parts, dp_all[i])
        run(fill[2 * i + 1])
        dq_tile.append(rows_sum(ds_parts, k_rot))
        for j in range(i + 1):
            dk_j = dot(ds_parts[j], q_tile[i], TN)
            dk_parts[j] = dk_j if dk_parts[j] is None else dk_parts[j] + dk_j
    run(ahead[4:])
    for head, lane in enumerate(lanes):
        dq_head = jnp.concatenate([dq[head * ROW_BLOCK:(head + 1) * ROW_BLOCK] for dq in dq_tile], axis=0)
        dq_head, d_gain = norm_rotate_back(dq_head * scale, q_parts[head][1], q_parts[head][2], qn_ref[...])
        dqn_ref[...] += d_gain
        dq_head = dq_head.astype(BF16)
        dqkv_stage[slot, :, lane] = dq_head
        dqkv_now[:, lane] = dq_head
    dk_head, d_gain = norm_rotate_back(jnp.concatenate(dk_parts, axis=0) * scale, k_unit, k_inv, kn_ref[...])
    dkn_ref[...] += d_gain
    dk_head = dk_head.astype(BF16)
    dqkv_stage[slot, :, q_cols:q_cols + head_dim] = dk_head
    dqkv_now[:, q_cols:q_cols + head_dim] = dk_head
    dv_head = jnp.concatenate(dv_parts, axis=0).astype(BF16)
    dqkv_stage[slot, :, q_cols + head_dim:] = dv_head
    dqkv_now[:, q_cols + head_dim:] = dv_head

    @pl.when((group == 0) & (seq > 0))
    def _():
        finish(seq - 1)
        out_acc[...] = jnp.zeros_like(out_acc)
        dh_acc[...] = jnp.zeros_like(dh_acc)

    @pl.when((seq == seqs - 1) & last_group)
    def _():
        o_last[...] = o_now[...]
        dqkv_last[...] = dqkv_now[...]
        run(accumulate(groups - 1))
        finish(seqs - 1)
        for copy in stores(step_id - 1):
            copy.wait()
        for copy in stores(step_id):
            copy.start()
        for copy in stores(step_id):
            copy.wait()
        reduce_gradients(me, (ga_hbm, gb_hbm), o_hbm, dqkv_hbm, small_out, dyb, ht_ref, wo, wqkv,
                         dgin_ref, dqn_ref, dkn_ref, small, smallb, ob, qkvb, (l1a, l1b), (t_a, t_b), (l2a, l2b), (out_acc, dh_acc),
                         load_sem, pair_send, pair_recv, turn_send, turn_recv, chip_send, chip_recv,
                         all_send, all_recv, small_send, small_recv)

        def drain(s, carry):
            for step in range(1, DEVICES):
                for kind in range(3):
                    incoming(kind, s, step).wait_send()
                for kind in range(2):
                    outgoing(kind, s, step, arrival=True).wait_recv()
            sent(0, s)
            return carry

        lax.fori_loop(0, seqs, drain, 0)
        for s in range(2):
            sent(1, seqs - 2 + s)


def start(copies):
    for copy in copies:
        copy.start()


def wait_send(copies):
    for copy in copies:
        copy.wait_send()


def wait_recv(copies):
    for copy in copies:
        copy.wait_recv()


X, Y, DIAG, PARTNER = 2, 4, 6, 1


def reduce_gradients(me, gathered, o_hbm, dqkv_hbm, small_out, dyb, ht_ref, wo, wqkv,
                     dgin_ref, dqn_ref, dkn_ref, small, smallb, ob, qkvb, pair_in, turn_in, chip_in, acc,
                     load_sem, pair_send, pair_recv, turn_send, turn_recv, chip_send, chip_recv,
                     all_send, all_recv, small_send, small_recv):
    partner = peer_of(me, PARTNER)
    chips = 4
    stage = (wo, wqkv)
    sizes = [ref.shape[1] // 2 for ref in stage]
    result = 2 * chips - 1

    def half_of(i, half):
        return pl.ds(half * sizes[i], sizes[i])

    def own(i, half):
        cols = stage[i].shape[2]
        return acc[i].at[pl.ds(half * sizes[i], sizes[i])] if i == 0 else acc[i].at[:, pl.ds(half * cols, cols)]

    small[...] = jnp.zeros_like(small)
    lanes = dqn_ref.shape[1]
    rows = dgin_ref.shape[1] // lanes
    for row in range(rows):
        small[row:row + 1] = dgin_ref[:, row * lanes:(row + 1) * lanes]
    small[rows:rows + 1] = dqn_ref[...]
    small[rows + 1:rows + 2] = dkn_ref[...]

    def small_copy(step, arrival=False):
        peer = peer_of(me, step)
        return remote(small, smallb.at[peer if arrival else me], small_send.at[step], small_recv.at[step], peer)

    def peer_group(order):
        return peer_of(me, (1 - order // 2) * X + ((order + 1) % 2) * Y)

    def loads(group, slot):
        return [pltpu.make_async_copy(o_hbm.at[group], ob.at[slot], load_sem.at[0, slot]),
                pltpu.make_async_copy(dqkv_hbm.at[group], qkvb.at[slot], load_sem.at[1, slot])]

    def wait(copies):
        for copy in copies:
            copy.wait()

    def pair(order):
        return [remote(stage[i].at[order], pair_in[i].at[order % 2], pair_send.at[i, order], pair_recv.at[i, order], partner) for i in range(2)]

    def turn(half):
        return [remote(stage[i].at[chips, half_of(i, half)], turn_in[i].at[half], turn_send.at[i, half], turn_recv.at[i, half],
                       peer_of(me, (X, Y)[half])) for i in range(2)]

    def chip(axis, half):
        return [remote(stage[i].at[chips + 1 + axis, half_of(i, half)], chip_in[i].at[axis, half_of(i, half)],
                       chip_send.at[i, axis, half], chip_recv.at[i, axis, half], peer_of(me, (X, Y)[axis])) for i in range(2)]

    def join_turn(axis, half):
        wait_recv(turn(half))
        for i in range(2):
            part = stage[i][chips + 1 + axis, half * sizes[i]:(half + 1) * sizes[i]].astype(F32)
            stage[i][chips + 1 + axis, half * sizes[i]:(half + 1) * sizes[i]] = (part + turn_in[i][half].astype(F32)).astype(BF16)
        start(chip(axis, half))

    start(loads(peer_of(peer_group(0), PARTNER), 0))
    for step in range(1, DEVICES):
        small_copy(step).start()

    def products(slot):
        tokens = dyb.shape[0] * dyb.shape[1]
        return dot(ob[slot], dyb[...].reshape(tokens, dyb.shape[2]), TN), dot(ht_ref[...], qkvb[slot])

    def body(order, carry):
        mine = peer_group(order)
        other = peer_of(mine, PARTNER)
        start(loads(mine, 1))
        wait(loads(other, 0))
        for i, product in enumerate(products(0)):
            stage[i][order] = product.astype(BF16)
        start(pair(order))

        @pl.when(order < chips - 1)
        def _():
            start(loads(peer_of(peer_group(order + 1), PARTNER), 0))

        wait(loads(mine, 1))
        for i, product in enumerate(products(1)):
            for half in range(2):
                own(i, half)[...] = product[half * sizes[i]:(half + 1) * sizes[i]]
        wait_recv(pair(order))

        @pl.when(order < chips - 1)
        def _():
            for i in range(2):
                for half in range(2):
                    part = slice(half * sizes[i], (half + 1) * sizes[i])
                    stage[i][chips + order, part] = (own(i, half)[...] + pair_in[i][order % 2, part].astype(F32)).astype(BF16)

        @pl.when(order == 0)
        def _():
            start(turn(0))
            start(turn(1))

        @pl.when(order == 1)
        def _():
            start(chip(0, 0))

        @pl.when(order == 2)
        def _():
            start(chip(1, 1))
            join_turn(0, 1)
            join_turn(1, 0)
        return carry

    lax.fori_loop(0, chips, body, 0)

    def spread(half, slot, arrival=False):
        x, y, diag = (peer_of(me, step) for step in (X, Y, DIAG))
        target = (x, y, (y, x)[half], partner, partner, partner, partner)[slot]
        owner = (me, me, (x, y)[half], me, x, y, diag)[slot]
        sender = (x, y, diag, partner, peer_of(partner, X), peer_of(partner, Y), peer_of(partner, DIAG))[slot]
        copies = []
        for i in range(2):
            part = half_of(i, half)
            src = stage[i].at[result, part] if slot in (0, 1, 3) else gathered[i].at[owner, part]
            copies.append(remote(src, gathered[i].at[sender if arrival else owner, part],
                                 all_send.at[i, half, slot], all_recv.at[i, half, slot], target))
        return copies

    for half in range(2):
        for axis in range(2):
            wait_recv(chip(axis, half))
        for i in range(2):
            part = slice(half * sizes[i], (half + 1) * sizes[i])
            total = own(i, half)[...] + pair_in[i][(chips - 1) % 2, part].astype(F32) + chip_in[i][0, part].astype(F32) + chip_in[i][1, part].astype(F32)
            stage[i][result, part] = total.astype(BF16)
        for slot in ((0, 1, 3), (1, 0, 3))[half]:
            start(spread(half, slot))
    local = [pltpu.make_async_copy(stage[i].at[result], gathered[i].at[me], load_sem.at[i, 0]) for i in range(2)]
    start(local)

    for step in range(1, DEVICES):
        small_copy(step, arrival=True).wait_recv()
    smallb[me] = small[...]
    sums = smallb[0]
    for device in range(1, DEVICES):
        sums = sums + smallb[device]
    small_out[...] = sums

    for half, slot, onward in ((0, 0, (2, 4)), (1, 1, (2, 5)), (1, 0, (4,)), (0, 1, (5,)), (0, 2, (6,)), (1, 2, (6,))):
        wait_recv(spread(half, slot, arrival=True))
        for forward in onward:
            start(spread(half, forward))
    wait(local)
    for half in range(2):
        for slot in (3, 4, 5, 6):
            wait_recv(spread(half, slot, arrival=True))
        for slot in range(7):
            wait_send(spread(half, slot))
        wait_send(turn(half))
        for axis in range(2):
            wait_send(chip(axis, half))
    for order in range(chips):
        wait_send(pair(order))
    for step in range(1, DEVICES):
        small_copy(step).wait_send()


def block_call(x, dy, pos, gains, w_q, w_k, w_v, w_o, head_dim):
    batch, piece, model = x.shape
    seqs, seq_len = batch // DEVICES, piece * DEVICES
    q_width, kv_width = w_q.shape[1], w_k.shape[1]
    groups = kv_width // head_dim
    q_cols = q_width // groups
    tokens = seqs * seq_len
    width = q_cols + 2 * head_dim
    fixed = lambda s, g: (0, 0)
    bf = lambda *shape: jax.ShapeDtypeStruct(shape, BF16)
    f32 = lambda *shape: jax.ShapeDtypeStruct(shape, F32)
    anywhere = pl.BlockSpec(memory_space=pl.ANY)
    flops = 4 * tokens * model * (q_width * 2 + kv_width * 2) + 12 * tokens * seq_len * q_width
    vb = lambda *shape: pltpu.VMEM(shape, BF16)
    vf = lambda *shape: pltpu.VMEM(shape, F32)
    dma = lambda *shape: pltpu.SemaphoreType.DMA(shape)
    return pl.pallas_call(
        block_kernel,
        grid=(seqs, groups),
        in_specs=[
            anywhere, anywhere, anywhere, anywhere, anywhere, anywhere, anywhere,
            pl.BlockSpec(gains.shape, fixed),
        ],
        out_specs=[anywhere] * 6 + [pl.BlockSpec((16, head_dim), fixed)],
        out_shape=[
            bf(batch, piece, model), bf(batch, piece, model),
            bf(groups, q_cols, model), bf(groups, model, width),
            bf(groups, tokens, q_cols), bf(groups, tokens, width),
            f32(16, head_dim),
        ],
        scratch_shapes=[
            vb(seqs, seq_len, model), vb(seqs, seq_len, model), vb(2, seq_len, model),
            vf(seqs, DEVICES, 8, head_dim),
            vb(groups, model, width), vb(groups, q_cols, model),
            vb(seq_len, model), vb(model, tokens),
            vf(seq_len, head_dim), vf(seq_len, head_dim), vf(seq_len, head_dim), vf(seq_len, head_dim),
            vf(seq_len, model), vf(seq_len, model),
            vf(seq_len, q_cols), vf(seq_len, head_dim), vb(seq_len, head_dim), vb(seq_len, q_cols),
            vb(seq_len, head_dim), vb(seq_len, q_cols),
            vb(seq_len, q_cols), vb(seq_len, width), vb(seq_len, q_cols), vb(seq_len, width),
            vb(2, seq_len, q_cols), vb(2, seq_len, width),
            vf(1, model), vf(1, head_dim), vf(1, head_dim), vf(16, head_dim), vf(DEVICES, 16, head_dim),
            vb(2, tokens, q_cols), vb(2, tokens, width),
            vb(2, q_cols, model), vb(2, model, width),
            vb(2, q_cols // 2, model), vb(2, model // 2, width),
            vb(2, q_cols, model), vb(2, model, width),
            pltpu.SemaphoreType.DMA((4, groups)),
            pltpu.SemaphoreType.DMA((3, seqs, DEVICES)),
            pltpu.SemaphoreType.DMA((3, seqs, DEVICES)),
            pltpu.SemaphoreType.DMA((2, seqs, DEVICES)),
            pltpu.SemaphoreType.DMA((2, seqs, DEVICES)),
            dma(2, 2), dma(2, 2), dma(2, 4), dma(2, 4), dma(2, 2), dma(2, 2), dma(2, 2, 2), dma(2, 2, 2),
            dma(2, 2, 7), dma(2, 2, 7), dma(DEVICES), dma(DEVICES),
        ],
        compiler_params=pltpu.CompilerParams(
            dimension_semantics=("arbitrary", "arbitrary"), vmem_limit_bytes=67_000_000,
            collective_id=0, has_side_effects=True),
        cost_estimate=pl.CostEstimate(flops=flops, bytes_accessed=50_000_000, transcendentals=tokens * seq_len * 8),
        name="block",
    )(x, dy, pos, w_q, w_k, w_v, w_o, gains)


def widen_kernel(ga_ref, gb_ref, small_ref, wq_ref, wk_ref, wv_ref, wo_ref, dgin_ref, dqn_ref, dkn_ref):
    @pl.when(pl.program_id(0) == 0)
    def _():
        lanes = small_ref.shape[1]
        rows = dgin_ref.shape[1] // lanes
        for row in range(rows):
            dgin_ref[:, row * lanes:(row + 1) * lanes] = small_ref[row:row + 1]
        dqn_ref[...] = small_ref[rows:rows + 1]
        dkn_ref[...] = small_ref[rows + 1:rows + 2]

    q_cols, head_dim = wq_ref.shape[1], wk_ref.shape[1]
    wo_ref[...] = ga_ref[0].astype(F32)
    wq_ref[...] = gb_ref[0, :, :q_cols].astype(F32)
    wk_ref[...] = gb_ref[0, :, q_cols:q_cols + head_dim].astype(F32)
    wv_ref[...] = gb_ref[0, :, q_cols + head_dim:].astype(F32)


def widen_call(ga, gb, small):
    groups, q_cols, model = ga.shape
    head_dim = (gb.shape[2] - q_cols) // 2
    f32 = lambda *shape: jax.ShapeDtypeStruct(shape, F32)
    across = lambda g: (0, g)
    return pl.pallas_call(
        widen_kernel,
        grid=(groups,),
        in_specs=[pl.BlockSpec((1, q_cols, model), lambda g: (g, 0, 0)),
                  pl.BlockSpec((1, model, gb.shape[2]), lambda g: (g, 0, 0)),
                  pl.BlockSpec(small.shape, lambda g: (0, 0))],
        out_specs=[pl.BlockSpec((model, q_cols), across), pl.BlockSpec((model, head_dim), across),
                   pl.BlockSpec((model, head_dim), across), pl.BlockSpec((q_cols, model), lambda g: (g, 0))]
        + [pl.BlockSpec((1, n), lambda g: (0, 0)) for n in (model, head_dim, head_dim)],
        out_shape=[f32(model, groups * q_cols), f32(model, groups * head_dim), f32(model, groups * head_dim),
                   f32(groups * q_cols, model), f32(1, model), f32(1, head_dim), f32(1, head_dim)],
        compiler_params=pltpu.CompilerParams(dimension_semantics=("arbitrary",)),
        name="widen",
    )(ga, gb, small)


def solution(mesh):
    seq_spec = P(None, 'sp', None)
    replicated = P()

    def shard_body(hidden_in, grad_out, positions, w_q, w_k, w_v, w_o, g_in, q_norm, k_norm):
        batch, seq_dev, model_dim = hidden_in.shape
        head_dim = q_norm.shape[0]
        exponents = jnp.arange(0, head_dim, 2).astype(F32) / head_dim
        inv_freq = jnp.power(ROPE_THETA, -exponents)
        gains = jnp.concatenate([g_in.astype(F32), q_norm.astype(F32), k_norm.astype(F32), inv_freq, inv_freq])[None]
        pos = jnp.broadcast_to(jnp.pad(positions.astype(F32), ((0, 0), (0, head_dim - seq_dev)))[:, None, :], (batch, 8, head_dim))
        hidden_out, grad_in, ga, gb, _, _, small = block_call(hidden_in, grad_out, pos, gains, w_q, w_k, w_v, w_o, head_dim)
        grad_wq, grad_wk, grad_wv, grad_wo, dgin, dqn, dkn = widen_call(ga, gb, small)
        return hidden_out, grad_in, grad_wq, grad_wk, grad_wv, grad_wo, dgin[0], dqn[0], dkn[0]

    return jax.shard_map(shard_body, mesh=mesh,
                         in_specs=(seq_spec, seq_spec, P(None, 'sp'), replicated, replicated, replicated, replicated, replicated, replicated, replicated),
                         out_specs=(seq_spec, seq_spec, replicated, replicated, replicated, replicated, replicated, replicated, replicated),
                         check_vma=False)
```

time: 418 us -> 347 us (0.83)
  Pallas kernels: 401 us -> 335 us
  other arithmetic: 5.17 us -> 0.73 us
    pallas_call x1 -> x0, Pallas kernels: 171 us -> none  [grads_call(): pl.pallas_call(grads_kernel, in_specs=[vmem, vmem, vmem, anywhere, anywhe...]
    pallas_call x1, Pallas kernels: 216 us -> 321 us  [block_call(): pl.pallas_call(block_kernel, grid=(seqs, groups), in_specs=[anywhere, any...]
where the time goes in v4:
time: 347 us
  Pallas kernels  335 us (97%)
  local copies, waits for them, and re-layouts  10.4 us (3%)
    pallas_call x1, Pallas kernels, block_call(): pl.pallas_call(block_kernel, grid=(seqs, groups), in_specs=[anywhere, any...  321 us
    pallas_call x1, Pallas kernels, widen_call(): pl.pallas_call(widen_kernel, grid=(groups,), in_specs=[pl.BlockSpec((1, q...  14.1 us
    unnamed x4, local copies, waits for them, and re-layouts  7.08 us

profile of v4, /device:TPU:0, one launch (start us, length us, event | category | flops | bytes accessed | tf_op | source)
XLA Modules:
  0.0 346.9 jit_solution(12156351497555987707)
XLA Ops:
  0.7 2.1 concatenate.3
  2.7 0.6 broadcast_in_dim.10.gains_ref
  3.3 0.7 convert_element_type.19
  4.1 0.7 broadcast_in_dim.4.pos_hbm
  4.7 320.9 %block.1 = (bf16[32,64,1024]{2,1,0:T(8,128)(2,1)}, bf16[32,64,1024]{2,1,0:T(8,128)(2,1)}, bf16[8,256,1024]{2,1,0:T(8,128)(2,1)}, bf16[8,1024,512]{2,1,0:T(8,128)...) custom-call(bf16[32,64,1024]{2,1,0:T(8,128)(2,1)} %x_hbm.1, ...), custom_call_target="tpu_custom_call" | custom-call | flops 77309411328 | bytes 50000000 | tf_op jit(solution)/shard_map/block/pallas_call | solution.py:559
  325.7 14.1 %widen.1 = (f32[1024,2048]{1,0:T(8,128)}, f32[1024,1024]{1,0:T(8,128)}, f32[1024,1024]{1,0:T(8,128)}, f32[2048,1024]{1,0:T(8,128)}, f32[1,1024]{1,0:T(1,128)}, /*index=5*/f32[1,128]{1,0:T(1,128)}, f32[1,128]{1,0:T(1,128)}) custom-call(bf16[8,256,1024]{2,1,0:T(8,128)(2,1)} %get-tuple-element.23.ga_ref, bf16[8,1024,512]{2,1,0:T(8,128)(2,1)} %get-tuple-element.24.gb_ref, ...), custom_call_target="tpu_custom_call" | custom-call | tf_op jit(solution)/shard_map/widen/pallas_call | solution.py:627
  339.8 0.0 copy-start
  339.8 5.1 %copy.21 = bf16[32,64,1024]{2,1,0:T(8,128)(2,1)} copy(bf16[32,64,1024]{2,1,0:T(8,128)(2,1)} %get-tuple-element.42) | data formatting | bytes 8388608
  344.9 0.0 copy-done
  344.9 2.0 copy.22
  (2 shorter events, 0.0 us)
Async XLA Ops:
  339.8 5.1 %copy-start = (bf16[32,64,1024]{2,1,0:T(8,128)(2,1)S(1)}, bf16[32,64,1024]{2,1,0:T(8,128)(2,1)}, u32[]{:S(2)}) copy-start(bf16[32,64,1024]{2,1,0:T(8,128)(2,1)} %get-tuple-element.43) | copy-start | bytes 12582916

commit v5 on v4

--- a/solution.py
+++ b/solution.py
@@ -25,6 +25,17 @@
 def peer_of(me, step):
     core, x, y = me % 2, (me // 2) % 2, me // 4
     return ((y + step // 4) % 2) * 4 + ((x + (step // 2) % 2) % 2) * 2 + (core + step % 2) % 2
+
+
+X, Y, DIAG, PARTNER = 2, 4, 6, 1
+
+
+def chip_peer(me, order):
+    return peer_of(me, (1 - order // 2) * X + ((order + 1) % 2) * Y)
+
+
+def group_at(me, place):
+    return peer_of(chip_peer(me, place // 2), 1 - place % 2)
 
 
 def entry_barrier(me):
@@ -89,11 +100,16 @@
             outgoing(kind, s, step).wait_send()
 
     def weight_loads():
-        copies = [pltpu.make_async_copy(wo_hbm.at[g * q_cols:(g + 1) * q_cols], wo.at[g], weight_sem.at[3, g]) for g in range(wo.shape[0])]
-        for i, src in enumerate((wq_hbm, wk_hbm, wv_hbm)):
-            start, size = (0, q_cols, q_cols + head_dim)[i], q_cols if i == 0 else head_dim
-            copies += [pltpu.make_async_copy(src.at[:, g * size:(g + 1) * size], wqkv.at[g, :, start:start + size], weight_sem.at[i, g])
-                       for g in range(wo.shape[0])]
+        copies = []
+        for place in range(DEVICES):
+            g = group_at(me, place)
+            wide = pl.ds(pl.multiple_of(g * q_cols, q_cols), q_cols)
+            narrow = pl.ds(pl.multiple_of(g * head_dim, head_dim), head_dim)
+            parts = ((wq_hbm.at[:, wide], wqkv.at[place, :, pl.ds(0, q_cols)]),
+                     (wk_hbm.at[:, narrow], wqkv.at[place, :, pl.ds(q_cols, head_dim)]),
+                     (wv_hbm.at[:, narrow], wqkv.at[place, :, pl.ds(q_cols + head_dim, head_dim)]),
+                     (wo_hbm.at[wide], wo.at[place]))
+            copies += [pltpu.make_async_copy(src, dst, weight_sem.at[i, place]) for i, (src, dst) in enumerate(parts)]
         return copies
 
     def arrive(kind, s):
@@ -235,12 +251,14 @@
         return [pltpu.make_async_copy(o_stage.at[step % 2], o_hbm.at[g, rows], store_sem.at[0, step % 2]),
                 pltpu.make_async_copy(dqkv_stage.at[step % 2], dqkv_hbm.at[g, rows], store_sem.at[1, step % 2])]
 
-    @pl.when(step_id >= 2)
+    stored = (seqs - 1) * groups
+
+    @pl.when((step_id >= 2) & (step_id - 2 < stored))
     def _():
         for copy in stores(step_id - 2):
             copy.wait()
 
-    @pl.when(step_id >= 1)
+    @pl.when((step_id >= 1) & (step_id - 1 < stored))
     def _():
         for copy in stores(step_id - 1):
             copy.start()
@@ -290,8 +308,8 @@
             o_now[tiles[i], lane] = o_head
 
     fill = [ahead[0:2], behind[6:7], behind[7:8] + ahead[2:3], ahead[3:4]]
+    dp_all = [[dot(do_tile[i], v_now[tiles[j]], NT) for j in range(i + 1)] for i in range(blocks)]
     s_all = [scores(i) for i in range(blocks)]
-    dp_all = [[dot(do_tile[i], v_now[tiles[j]], NT) for j in range(i + 1)] for i in range(blocks)]
     dk_parts, dv_parts, dq_tile = [None] * blocks, [None] * blocks, []
     for i in range(blocks):
         p_parts, pb_parts = softmax(s_all[i])
@@ -329,22 +347,28 @@
         out_acc[...] = jnp.zeros_like(out_acc)
         dh_acc[...] = jnp.zeros_like(dh_acc)
 
-    @pl.when((seq == seqs - 1) & last_group)
+    reducer = GradientReducer(me, (ga_hbm, gb_hbm), o_hbm, dqkv_hbm, small_out, dyb, ht_ref, wo, wqkv,
+                              dgin_ref, dqn_ref, dkn_ref, small, smallb, ob, qkvb, o_now, dqkv_now, (l1a, l1b), (t_a, t_b), (l2a, l2b),
+                              load_sem, pair_send, pair_recv, turn_send, turn_recv, chip_send, chip_recv,
+                              all_send, all_recv, small_send, small_recv)
+    last_seq = seq == seqs - 1
+
+    @pl.when(last_seq & (group == 0))
+    def _():
+        start(reducer.loads(0))
+
+    @pl.when(last_seq & (group < groups - 1))
+    def _():
+        reducer.step(group)
+
+    @pl.when(last_seq & last_group)
     def _():
         o_last[...] = o_now[...]
         dqkv_last[...] = dqkv_now[...]
         run(accumulate(groups - 1))
         finish(seqs - 1)
-        for copy in stores(step_id - 1):
-            copy.wait()
-        for copy in stores(step_id):
-            copy.start()
-        for copy in stores(step_id):
-            copy.wait()
-        reduce_gradients(me, (ga_hbm, gb_hbm), o_hbm, dqkv_hbm, small_out, dyb, ht_ref, wo, wqkv,
-                         dgin_ref, dqn_ref, dkn_ref, small, smallb, ob, qkvb, (l1a, l1b), (t_a, t_b), (l2a, l2b), (out_acc, dh_acc),
-                         load_sem, pair_send, pair_recv, turn_send, turn_recv, chip_send, chip_recv,
-                         all_send, all_recv, small_send, small_recv)
+        reducer.step(groups - 1)
+        reducer.finish()
 
         def drain(s, carry):
             for step in range(1, DEVICES):
@@ -375,169 +399,159 @@
         copy.wait_recv()
 
 
-X, Y, DIAG, PARTNER = 2, 4, 6, 1
-
-
-def reduce_gradients(me, gathered, o_hbm, dqkv_hbm, small_out, dyb, ht_ref, wo, wqkv,
-                     dgin_ref, dqn_ref, dkn_ref, small, smallb, ob, qkvb, pair_in, turn_in, chip_in, acc,
-                     load_sem, pair_send, pair_recv, turn_send, turn_recv, chip_send, chip_recv,
-                     all_send, all_recv, small_send, small_recv):
-    partner = peer_of(me, PARTNER)
-    chips = 4
-    stage = (wo, wqkv)
-    sizes = [ref.shape[1] // 2 for ref in stage]
-    result = 2 * chips - 1
-
-    def half_of(i, half):
-        return pl.ds(half * sizes[i], sizes[i])
-
-    def own(i, half):
-        cols = stage[i].shape[2]
-        return acc[i].at[pl.ds(half * sizes[i], sizes[i])] if i == 0 else acc[i].at[:, pl.ds(half * cols, cols)]
-
-    small[...] = jnp.zeros_like(small)
-    lanes = dqn_ref.shape[1]
-    rows = dgin_ref.shape[1] // lanes
-    for row in range(rows):
-        small[row:row + 1] = dgin_ref[:, row * lanes:(row + 1) * lanes]
-    small[rows:rows + 1] = dqn_ref[...]
-    small[rows + 1:rows + 2] = dkn_ref[...]
-
-    def small_copy(step, arrival=False):
-        peer = peer_of(me, step)
-        return remote(small, smallb.at[peer if arrival else me], small_send.at[step], small_recv.at[step], peer)
-
-    def peer_group(order):
-        return peer_of(me, (1 - order // 2) * X + ((order + 1) % 2) * Y)
-
-    def loads(group, slot):
-        return [pltpu.make_async_copy(o_hbm.at[group], ob.at[slot], load_sem.at[0, slot]),
-                pltpu.make_async_copy(dqkv_hbm.at[group], qkvb.at[slot], load_sem.at[1, slot])]
-
-    def wait(copies):
-        for copy in copies:
+class GradientReducer:
+    def __init__(self, me, gathered, o_hbm, dqkv_hbm, small_out, dyb, ht_ref, wo, wqkv, dgin_ref, dqn_ref, dkn_ref,
+                 small, smallb, ob, qkvb, o_now, dqkv_now, pair_in, turn_in, chip_in, load_sem, pair_send, pair_recv,
+                 turn_send, turn_recv, chip_send, chip_recv, all_send, all_recv, small_send, small_recv):
+        self.__dict__.update({k: v for k, v in locals().items() if k != 'self'})
+        self.partner = peer_of(me, PARTNER)
+        self.chips = DEVICES // 2
+        self.stage = (wo, wqkv)
+        self.sizes = [ref.shape[1] // 2 for ref in self.stage]
+        self.early = ob.shape[0] - o_now.shape[0]
+
+    def slot(self, place):
+        return (place + DEVICES) % (DEVICES + 1)
+
+    def half_of(self, i, half):
+        return pl.ds(half * self.sizes[i], self.sizes[i])
+
+    def loads(self, place):
+        rows = pl.ds(0, self.early)
+        return [pltpu.make_async_copy(self.o_hbm.at[place], self.ob.at[rows], self.load_sem.at[0]),
+                pltpu.make_async_copy(self.dqkv_hbm.at[place], self.qkvb.at[rows], self.load_sem.at[1])]
+
+    def pair(self, order):
+        return [remote(self.stage[i].at[self.slot(2 * order)], self.pair_in[i].at[order % 2],
+                       self.pair_send.at[i, order], self.pair_recv.at[i, order], self.partner) for i in range(2)]
+
+    def turn(self, half):
+        return [remote(self.stage[i].at[self.slot(1), self.half_of(i, half)], self.turn_in[i].at[half],
+                       self.turn_send.at[i, half], self.turn_recv.at[i, half], peer_of(self.me, (X, Y)[half])) for i in range(2)]
+
+    def chip(self, axis, half):
+        return [remote(self.stage[i].at[self.slot(2 * axis + 3), self.half_of(i, half)], self.chip_in[i].at[axis, self.half_of(i, half)],
+                       self.chip_send.at[i, axis, half], self.chip_recv.at[i, axis, half], peer_of(self.me, (X, Y)[axis])) for i in range(2)]
+
+    def join_turn(self, axis, half):
+        wait_recv(self.turn(half))
+        for i in range(2):
+            part = self.stage[i].at[self.slot(2 * axis + 3), self.half_of(i, half)]
+            part[...] = (part[...].astype(F32) + self.turn_in[i][half].astype(F32)).astype(BF16)
+        start(self.chip(axis, half))
+
+    def step(self, place):
+        for copy in self.loads(place):
             copy.wait()
-
-    def pair(order):
-        return [remote(stage[i].at[order], pair_in[i].at[order % 2], pair_send.at[i, order], pair_recv.at[i, order], partner) for i in range(2)]
-
-    def turn(half):
-        return [remote(stage[i].at[chips, half_of(i, half)], turn_in[i].at[half], turn_send.at[i, half], turn_recv.at[i, half],
-                       peer_of(me, (X, Y)[half])) for i in range(2)]
-
-    def chip(axis, half):
-        return [remote(stage[i].at[chips + 1 + axis, half_of(i, half)], chip_in[i].at[axis, half_of(i, half)],
-                       chip_send.at[i, axis, half], chip_recv.at[i, axis, half], peer_of(me, (X, Y)[axis])) for i in range(2)]
-
-    def join_turn(axis, half):
-        wait_recv(turn(half))
-        for i in range(2):
-            part = stage[i][chips + 1 + axis, half * sizes[i]:(half + 1) * sizes[i]].astype(F32)
-            stage[i][chips + 1 + axis, half * sizes[i]:(half + 1) * sizes[i]] = (part + turn_in[i][half].astype(F32)).astype(BF16)
-        start(chip(axis, half))
-
-    start(loads(peer_of(peer_group(0), PARTNER), 0))
-    for step in range(1, DEVICES):
-        small_copy(step).start()
-
-    def products(slot):
-        tokens = dyb.shape[0] * dyb.shape[1]
-        return dot(ob[slot], dyb[...].reshape(tokens, dyb.shape[2]), TN), dot(ht_ref[...], qkvb[slot])
-
-    def body(order, carry):
-        mine = peer_group(order)
-        other = peer_of(mine, PARTNER)
-        start(loads(mine, 1))
-        wait(loads(other, 0))
-        for i, product in enumerate(products(0)):
-            stage[i][order] = product.astype(BF16)
-        start(pair(order))
-
-        @pl.when(order < chips - 1)
+        self.ob[self.early:] = self.o_now[...]
+        self.qkvb[self.early:] = self.dqkv_now[...]
+        tokens = self.ob.shape[0]
+        into = self.slot(place)
+        self.stage[0][into] = dot(self.ob[...], self.dyb[...].reshape(tokens, self.dyb.shape[2]), TN).astype(BF16)
+        self.stage[1][into] = dot(self.ht_ref[...], self.qkvb[...]).astype(BF16)
+        order = place // 2
+
+        @pl.when(place < DEVICES - 1)
         def _():
-            start(loads(peer_of(peer_group(order + 1), PARTNER), 0))
-
-        wait(loads(mine, 1))
-        for i, product in enumerate(products(1)):
-            for half in range(2):
-                own(i, half)[...] = product[half * sizes[i]:(half + 1) * sizes[i]]
-        wait_recv(pair(order))
-
-        @pl.when(order < chips - 1)
+            start(self.loads(place + 1))
+
+        @pl.when(place % 2 == 0)
         def _():
+            start(self.pair(order))
+
+        @pl.when(place % 2 == 1)
+        def _():
+            wait_recv(self.pair(order))
             for i in range(2):
                 for half in range(2):
-                    part = slice(half * sizes[i], (half + 1) * sizes[i])
-                    stage[i][chips + order, part] = (own(i, half)[...] + pair_in[i][order % 2, part].astype(F32)).astype(BF16)
-
-        @pl.when(order == 0)
+                    part = self.stage[i].at[into, self.half_of(i, half)]
+                    part[...] = (part[...].astype(F32) + self.pair_in[i][order % 2, self.half_of(i, half)].astype(F32)).astype(BF16)
+
+        @pl.when(place == 1)
         def _():
-            start(turn(0))
-            start(turn(1))
-
-        @pl.when(order == 1)
+            start(self.turn(0))
+            start(self.turn(1))
+
+        @pl.when(place == 3)
         def _():
-            start(chip(0, 0))
-
-        @pl.when(order == 2)
+            start(self.chip(0, 0))
+
+        @pl.when(place == 5)
         def _():
-            start(chip(1, 1))
-            join_turn(0, 1)
-            join_turn(1, 0)
-        return carry
-
-    lax.fori_loop(0, chips, body, 0)
-
-    def spread(half, slot, arrival=False):
+            start(self.chip(1, 1))
+            self.join_turn(0, 1)
+            self.join_turn(1, 0)
+
+    def small_copy(self, step, arrival=False):
+        peer = peer_of(self.me, step)
+        return remote(self.small, self.smallb.at[peer if arrival else self.me], self.small_send.at[step], self.small_recv.at[step], peer)
+
+    def spread(self, half, slot, arrival=False):
+        me, partner = self.me, self.partner
         x, y, diag = (peer_of(me, step) for step in (X, Y, DIAG))
         target = (x, y, (y, x)[half], partner, partner, partner, partner)[slot]
         owner = (me, me, (x, y)[half], me, x, y, diag)[slot]
         sender = (x, y, diag, partner, peer_of(partner, X), peer_of(partner, Y), peer_of(partner, DIAG))[slot]
         copies = []
         for i in range(2):
-            part = half_of(i, half)
-            src = stage[i].at[result, part] if slot in (0, 1, 3) else gathered[i].at[owner, part]
-            copies.append(remote(src, gathered[i].at[sender if arrival else owner, part],
-                                 all_send.at[i, half, slot], all_recv.at[i, half, slot], target))
+            part = self.half_of(i, half)
+            src = self.stage[i].at[self.slot(DEVICES - 1), part] if slot in (0, 1, 3) else self.gathered[i].at[owner, part]
+            copies.append(remote(src, self.gathered[i].at[sender if arrival else owner, part],
+                                 self.all_send.at[i, half, slot], self.all_recv.at[i, half, slot], target))
         return copies
 
-    for half in range(2):
-        for axis in range(2):
-            wait_recv(chip(axis, half))
-        for i in range(2):
-            part = slice(half * sizes[i], (half + 1) * sizes[i])
-            total = own(i, half)[...] + pair_in[i][(chips - 1) % 2, part].astype(F32) + chip_in[i][0, part].astype(F32) + chip_in[i][1, part].astype(F32)
-            stage[i][result, part] = total.astype(BF16)
-        for slot in ((0, 1, 3), (1, 0, 3))[half]:
-            start(spread(half, slot))
-    local = [pltpu.make_async_copy(stage[i].at[result], gathered[i].at[me], load_sem.at[i, 0]) for i in range(2)]
-    start(local)
-
-    for step in range(1, DEVICES):
-        small_copy(step, arrival=True).wait_recv()
-    smallb[me] = small[...]
-    sums = smallb[0]
-    for device in range(1, DEVICES):
-        sums = sums + smallb[device]
-    small_out[...] = sums
-
-    for half, slot, onward in ((0, 0, (2, 4)), (1, 1, (2, 5)), (1, 0, (4,)), (0, 1, (5,)), (0, 2, (6,)), (1, 2, (6,))):
-        wait_recv(spread(half, slot, arrival=True))
-        for forward in onward:
-            start(spread(half, forward))
-    wait(local)
-    for half in range(2):
-        for slot in (3, 4, 5, 6):
+    def finish(self):
+        small, smallb, spread = self.small, self.smallb, self.spread
+        small[...] = jnp.zeros_like(small)
+        lanes = self.dqn_ref.shape[1]
+        rows = self.dgin_ref.shape[1] // lanes
+        for row in range(rows):
+            small[row:row + 1] = self.dgin_ref[:, row * lanes:(row + 1) * lanes]
+        small[rows:rows + 1] = self.dqn_ref[...]
+        small[rows + 1:rows + 2] = self.dkn_ref[...]
+        for step in range(1, DEVICES):
+            self.small_copy(step).start()
+
+        result = self.slot(DEVICES - 1)
+        for half in range(2):
+            for axis in range(2):
+                wait_recv(self.chip(axis, half))
+            for i in range(2):
+                rows_half = self.half_of(i, half)
+                part = self.stage[i].at[result, rows_half]
+                total = part[...].astype(F32) + self.chip_in[i][0, rows_half].astype(F32) + self.chip_in[i][1, rows_half].astype(F32)
+                part[...] = total.astype(BF16)
+            for slot in ((0, 1, 3), (1, 0, 3))[half]:
+                start(spread(half, slot))
+        local = [pltpu.make_async_copy(self.stage[i].at[result], self.gathered[i].at[self.me], self.load_sem.at[i]) for i in range(2)]
+        start(local)
+
+        for step in range(1, DEVICES):
+            self.small_copy(step, arrival=True).wait_recv()
+        smallb[self.me] = small[...]
+        sums = smallb[0]
+        for device in range(1, DEVICES):
+            sums = sums + smallb[device]
+        self.small_out[...] = sums
+
+        for half, slot, onward in ((0, 0, (2, 4)), (1, 1, (2, 5)), (1, 0, (4,)), (0, 1, (5,)), (0, 2, (6,)), (1, 2, (6,))):
             wait_recv(spread(half, slot, arrival=True))
-        for slot in range(7):
-            wait_send(spread(half, slot))
-        wait_send(turn(half))
-        for axis in range(2):
-            wait_send(chip(axis, half))
-    for order in range(chips):
-        wait_send(pair(order))
-    for step in range(1, DEVICES):
-        small_copy(step).wait_send()
+            for forward in onward:
+                start(spread(half, forward))
+        for copy in local:
+            copy.wait()
+        for half in range(2):
+            for slot in (3, 4, 5, 6):
+                wait_recv(spread(half, slot, arrival=True))
+            for slot in range(7):
+                wait_send(spread(half, slot))
+            wait_send(self.turn(half))
+            for axis in range(2):
+                wait_send(self.chip(axis, half))
+        for order in range(self.chips):
+            wait_send(self.pair(order))
+        for step in range(1, DEVICES):
+            self.small_copy(step).wait_send()
 
 
 def block_call(x, dy, pos, gains, w_q, w_k, w_v, w_o, head_dim):
@@ -567,13 +581,13 @@
         out_shape=[
             bf(batch, piece, model), bf(batch, piece, model),
             bf(groups, q_cols, model), bf(groups, model, width),
-            bf(groups, tokens, q_cols), bf(groups, tokens, width),
+            bf(groups, tokens - seq_len, q_cols), bf(groups, tokens - seq_len, width),
             f32(16, head_dim),
         ],
         scratch_shapes=[
             vb(seqs, seq_len, model), vb(seqs, seq_len, model), vb(2, seq_len, model),
             vf(seqs, DEVICES, 8, head_dim),
-            vb(groups, model, width), vb(groups, q_cols, model),
+            vb(groups + 1, model, width), vb(groups + 1, q_cols, model),
             vb(seq_len, model), vb(model, tokens),
             vf(seq_len, head_dim), vf(seq_len, head_dim), vf(seq_len, head_dim), vf(seq_len, head_dim),
             vf(seq_len, model), vf(seq_len, model),
@@ -582,7 +596,7 @@
             vb(seq_len, q_cols), vb(seq_len, width), vb(seq_len, q_cols), vb(seq_len, width),
             vb(2, seq_len, q_cols), vb(2, seq_len, width),
             vf(1, model), vf(1, head_dim), vf(1, head_dim), vf(16, head_dim), vf(DEVICES, 16, head_dim),
-            vb(2, tokens, q_cols), vb(2, tokens, width),
+            vb(tokens, q_cols), vb(tokens, width),
             vb(2, q_cols, model), vb(2, model, width),
             vb(2, q_cols // 2, model), vb(2, model // 2, width),
             vb(2, q_cols, model), vb(2, model, width),
@@ -591,7 +605,7 @@
             pltpu.SemaphoreType.DMA((3, seqs, DEVICES)),
             pltpu.SemaphoreType.DMA((2, seqs, DEVICES)),
             pltpu.SemaphoreType.DMA((2, seqs, DEVICES)),
-            dma(2, 2), dma(2, 2), dma(2, 4), dma(2, 4), dma(2, 2), dma(2, 2), dma(2, 2, 2), dma(2, 2, 2),
+            dma(2, 2), dma(2), dma(2, 4), dma(2, 4), dma(2, 2), dma(2, 2), dma(2, 2, 2), dma(2, 2, 2),
             dma(2, 2, 7), dma(2, 2, 7), dma(DEVICES), dma(DEVICES),
         ],
         compiler_params=pltpu.CompilerParams(

time: 347 us -> 348 us (level)
  no operation moved by 1% of the time
where the time goes in v5:
time: 348 us
  Pallas kernels  336 us (97%)
  local copies, waits for them, and re-layouts  10.4 us (3%)
    pallas_call x1, Pallas kernels, block_call(): pl.pallas_call(block_kernel, grid=(seqs, groups), in_specs=[anywhere, any...  322 us
    pallas_call x1, Pallas kernels, widen_call(): pl.pallas_call(widen_kernel, grid=(groups,), in_specs=[pl.BlockSpec((1, q...  14.1 us
    unnamed x4, local copies, waits for them, and re-layouts  7.08 us

profile of v5, /device:TPU:0, one launch (start us, length us, event | category | flops | bytes accessed | tf_op | source)
XLA Modules:
  0.0 347.6 jit_solution(4380574202610337406)
XLA Ops:
  0.7 2.1 concatenate.3
  2.7 0.6 broadcast_in_dim.10.gains_ref
  3.3 0.7 convert_element_type.19
  4.1 0.7 broadcast_in_dim.4.pos_hbm
  4.7 321.7 %block.1 = (bf16[32,64,1024]{2,1,0:T(8,128)(2,1)}, bf16[32,64,1024]{2,1,0:T(8,128)(2,1)}, bf16[8,256,1024]{2,1,0:T(8,128)(2,1)}, bf16[8,1024,512]{2,1,0:T(8,128)...) custom-call(bf16[32,64,1024]{2,1,0:T(8,128)(2,1)} %x_hbm.1, ...), custom_call_target="tpu_custom_call" | custom-call | flops 77309411328 | bytes 50000000 | tf_op jit(solution)/shard_map/block/pallas_call | solution.py:573
  326.4 14.1 %widen.1 = (f32[1024,2048]{1,0:T(8,128)}, f32[1024,1024]{1,0:T(8,128)}, f32[1024,1024]{1,0:T(8,128)}, f32[2048,1024]{1,0:T(8,128)}, f32[1,1024]{1,0:T(1,128)}, /*index=5*/f32[1,128]{1,0:T(1,128)}, f32[1,128]{1,0:T(1,128)}) custom-call(bf16[8,256,1024]{2,1,0:T(8,128)(2,1)} %get-tuple-element.23.ga_ref, bf16[8,1024,512]{2,1,0:T(8,128)(2,1)} %get-tuple-element.24.gb_ref, ...), custom_call_target="tpu_custom_call" | custom-call | tf_op jit(solution)/shard_map/widen/pallas_call | solution.py:641
  340.5 0.0 copy-start
  340.5 5.1 %copy.21 = bf16[32,64,1024]{2,1,0:T(8,128)(2,1)} copy(bf16[32,64,1024]{2,1,0:T(8,128)(2,1)} %get-tuple-element.42) | data formatting | bytes 8388608
  345.6 0.0 copy-done
  345.6 2.0 copy.22
  (2 shorter events, 0.0 us)
Async XLA Ops:
  340.5 5.1 %copy-start = (bf16[32,64,1024]{2,1,0:T(8,128)(2,1)S(1)}, bf16[32,64,1024]{2,1,0:T(8,128)(2,1)}, u32[]{:S(2)}) copy-start(bf16[32,64,1024]{2,1,0:T(8,128)(2,1)} %get-tuple-element.43) | copy-start | bytes 12582916

commit v6 on v5

--- a/solution.py
+++ b/solution.py
@@ -272,8 +272,8 @@
     behind = accumulate((group + groups - 1) % groups)
     lanes = [slice(head * head_dim, (head + 1) * head_dim) for head in range(per_kv)]
     stacked = per_kv * ROW_BLOCK
-    rows_id = lax.broadcasted_iota(jnp.int32, (stacked, ROW_BLOCK), 0) % ROW_BLOCK
-    causal = rows_id >= lax.broadcasted_iota(jnp.int32, (stacked, ROW_BLOCK), 1)
+    key_id = lax.broadcasted_iota(jnp.int32, (ROW_BLOCK, stacked), 0)
+    causal = key_id <= lax.broadcasted_iota(jnp.int32, (ROW_BLOCK, stacked), 1) % ROW_BLOCK
     blocks = len(tiles)
 
     run(behind[:6])
@@ -281,49 +281,42 @@
     q_parts = [norm_rotate(q_next[:, lane], qn_ref[...]) for lane in lanes]
     q_tile = [jnp.concatenate([part[0][tile] for part in q_parts], axis=0) for tile in tiles]
     do_tile = [jnp.concatenate([do_now[tile, lane] for lane in lanes], axis=0) for tile in tiles]
-
-    def scores(i):
-        s_parts = [dot(q_tile[i], k_rot[tiles[j]], NT) for j in range(i + 1)]
-        s_parts[i] = jnp.where(causal, s_parts[i], NEG_LARGE)
-        return s_parts
-
-    def softmax(s_parts):
-        top = functools.reduce(jnp.maximum, [jnp.max(s, axis=-1, keepdims=True) for s in s_parts])
-        e_parts = [jnp.exp2((s - top) * (scale * LOG2_E)) for s in s_parts]
-        recip = 1.0 / functools.reduce(jnp.add, [jnp.sum(e, axis=-1, keepdims=True) for e in e_parts])
-        p_parts = [e * recip for e in e_parts]
-        return p_parts, [p.astype(BF16) for p in p_parts]
-
-    def softmax_back(p_parts, dp_parts):
-        delta = functools.reduce(jnp.add, [jnp.sum(p * dp, axis=-1, keepdims=True) for p, dp in zip(p_parts, dp_parts)])
-        return [(p * (dp - delta)).astype(BF16) for p, dp in zip(p_parts, dp_parts)]
-
-    def rows_sum(parts, values):
-        return functools.reduce(jnp.add, [dot(part, values[tiles[j]]) for j, part in enumerate(parts)])
+    v_cols, k_cols = v_now[...].T, k_rot.T
+    fill = [ahead[0:2], behind[6:7], behind[7:8] + ahead[2:3], ahead[3:4]]
+    dp_all = [dot(v_now[:(i + 1) * ROW_BLOCK], do_tile[i], NT) for i in range(blocks)]
+    s_all = [dot(k_rot[:(i + 1) * ROW_BLOCK], q_tile[i], NT) for i in range(blocks)]
+
+    def masked(i):
+        diagonal = jnp.where(causal, s_all[i][i * ROW_BLOCK:], NEG_LARGE)
+        return diagonal if i == 0 else jnp.concatenate([s_all[i][:i * ROW_BLOCK], diagonal], axis=0)
 
     def store_output(i, o_i):
         for head, lane in enumerate(lanes):
-            o_head = o_i[head * ROW_BLOCK:(head + 1) * ROW_BLOCK].astype(BF16)
+            o_head = o_i[head * ROW_BLOCK:(head + 1) * ROW_BLOCK]
             o_stage[slot, tiles[i], lane] = o_head
             o_now[tiles[i], lane] = o_head
 
-    fill = [ahead[0:2], behind[6:7], behind[7:8] + ahead[2:3], ahead[3:4]]
-    dp_all = [[dot(do_tile[i], v_now[tiles[j]], NT) for j in range(i + 1)] for i in range(blocks)]
-    s_all = [scores(i) for i in range(blocks)]
-    dk_parts, dv_parts, dq_tile = [None] * blocks, [None] * blocks, []
+    def add_rows(total, part):
+        keys = part.shape[0]
+        if total is None:
+            return part
+        return jnp.concatenate([total + part[:total.shape[0]], part[total.shape[0]:keys]], axis=0)
+
+    dk_all, dv_all, dq_tile = None, None, []
     for i in range(blocks):
-        p_parts, pb_parts = softmax(s_all[i])
+        keys = (i + 1) * ROW_BLOCK
+        s = masked(i)
+        e = jnp.exp2((s - jnp.max(s, axis=0, keepdims=True)) * (scale * LOG2_E))
+        p = e * (1.0 / jnp.sum(e, axis=0, keepdims=True))
+        p_bf16 = p.astype(BF16)
         run(fill[2 * i])
-        store_output(i, rows_sum(pb_parts, v_now))
-        for j in range(i + 1):
-            dv_j = dot(pb_parts[j], do_tile[i], TN)
-            dv_parts[j] = dv_j if dv_parts[j] is None else dv_parts[j] + dv_j
-        ds_parts = softmax_back(p_parts, dp_all[i])
+        store_output(i, dot(v_cols[:, :keys], p_bf16).astype(BF16).T)
+        dv_all = add_rows(dv_all, dot(p_bf16, do_tile[i]))
+        delta = jnp.sum(p * dp_all[i], axis=0, keepdims=True)
+        ds = (p * (dp_all[i] - delta)).astype(BF16)
         run(fill[2 * i + 1])
-        dq_tile.append(rows_sum(ds_parts, k_rot))
-        for j in range(i + 1):
-            dk_j = dot(ds_parts[j], q_tile[i], TN)
-            dk_parts[j] = dk_j if dk_parts[j] is None else dk_parts[j] + dk_j
+        dq_tile.append(dot(k_cols[:, :keys], ds).T)
+        dk_all = add_rows(dk_all, dot(ds, q_tile[i]))
     run(ahead[4:])
     for head, lane in enumerate(lanes):
         dq_head = jnp.concatenate([dq[head * ROW_BLOCK:(head + 1) * ROW_BLOCK] for dq in dq_tile], axis=0)
@@ -332,12 +325,12 @@
         dq_head = dq_head.astype(BF16)
         dqkv_stage[slot, :, lane] = dq_head
         dqkv_now[:, lane] = dq_head
-    dk_head, d_gain = norm_rotate_back(jnp.concatenate(dk_parts, axis=0) * scale, k_unit, k_inv, kn_ref[...])
+    dk_head, d_gain = norm_rotate_back(dk_all * scale, k_unit, k_inv, kn_ref[...])
     dkn_ref[...] += d_gain
     dk_head = dk_head.astype(BF16)
     dqkv_stage[slot, :, q_cols:q_cols + head_dim] = dk_head
     dqkv_now[:, q_cols:q_cols + head_dim] = dk_head
-    dv_head = jnp.concatenate(dv_parts, axis=0).astype(BF16)
+    dv_head = dv_all.astype(BF16)
     dqkv_stage[slot, :, q_cols + head_dim:] = dv_head
     dqkv_now[:, q_cols + head_dim:] = dv_head
 

time: 348 us -> 325 us (0.934)
  Pallas kernels: 336 us -> 313 us
    pallas_call x1, Pallas kernels: 322 us -> 299 us  [block_call(): pl.pallas_call(block_kernel, grid=(seqs, groups), in_specs=[anywhere, any...]
where the time goes in v6:
time: 325 us
  Pallas kernels  313 us (96%)
  local copies, waits for them, and re-layouts  10.4 us (3%)
    pallas_call x1, Pallas kernels, block_call(): pl.pallas_call(block_kernel, grid=(seqs, groups), in_specs=[anywhere, any...  299 us
    pallas_call x1, Pallas kernels, widen_call(): pl.pallas_call(widen_kernel, grid=(groups,), in_specs=[pl.BlockSpec((1, q...  14.1 us
    unnamed x4, local copies, waits for them, and re-layouts  7.08 us

profile of v6, /device:TPU:0, one launch (start us, length us, event | category | flops | bytes accessed | tf_op | source)
XLA Modules:
  0.0 324.6 jit_solution(4371417204083375944)
XLA Ops:
  0.7 2.1 concatenate.3
  2.7 0.6 broadcast_in_dim.10.gains_ref
  3.3 0.7 convert_element_type.19
  4.1 0.7 broadcast_in_dim.4.pos_hbm
  4.7 298.6 %block.1 = (bf16[32,64,1024]{2,1,0:T(8,128)(2,1)}, bf16[32,64,1024]{2,1,0:T(8,128)(2,1)}, bf16[8,256,1024]{2,1,0:T(8,128)(2,1)}, bf16[8,1024,512]{2,1,0:T(8,128)...) custom-call(bf16[32,64,1024]{2,1,0:T(8,128)(2,1)} %x_hbm.1, ...), custom_call_target="tpu_custom_call" | custom-call | flops 77309411328 | bytes 50000000 | tf_op jit(solution)/shard_map/block/pallas_call | solution.py:566
  303.4 14.1 %widen.1 = (f32[1024,2048]{1,0:T(8,128)}, f32[1024,1024]{1,0:T(8,128)}, f32[1024,1024]{1,0:T(8,128)}, f32[2048,1024]{1,0:T(8,128)}, f32[1,1024]{1,0:T(1,128)}, /*index=5*/f32[1,128]{1,0:T(1,128)}, f32[1,128]{1,0:T(1,128)}) custom-call(bf16[8,256,1024]{2,1,0:T(8,128)(2,1)} %get-tuple-element.23.ga_ref, bf16[8,1024,512]{2,1,0:T(8,128)(2,1)} %get-tuple-element.24.gb_ref, ...), custom_call_target="tpu_custom_call" | custom-call | tf_op jit(solution)/shard_map/widen/pallas_call | solution.py:634
  317.5 0.0 copy-start
  317.5 5.1 %copy.21 = bf16[32,64,1024]{2,1,0:T(8,128)(2,1)} copy(bf16[32,64,1024]{2,1,0:T(8,128)(2,1)} %get-tuple-element.42) | data formatting | bytes 8388608
  322.6 0.0 copy-done
  322.6 2.0 copy.22
  (2 shorter events, 0.0 us)
Async XLA Ops:
  317.5 5.1 %copy-start = (bf16[32,64,1024]{2,1,0:T(8,128)(2,1)S(1)}, bf16[32,64,1024]{2,1,0:T(8,128)(2,1)}, u32[]{:S(2)}) copy-start(bf16[32,64,1024]{2,1,0:T(8,128)(2,1)} %get-tuple-element.43) | copy-start | bytes 12582916

commit v7 on v6

--- a/solution.py
+++ b/solution.py
@@ -50,7 +50,7 @@
                                         device_id=(device,), device_id_type=pl.DeviceIdType.MESH)
 
 
-def block_kernel(x_hbm, dy_hbm, pos_hbm, wq_hbm, wk_hbm, wv_hbm, wo_hbm, gains_ref,
+def block_kernel(x_hbm, dy_hbm, pos_hbm, wq_hbm, wk_hbm, wv_hbm, wo_hbm, gin_ref, qn_ref, kn_ref, freq_ref,
                  out_hbm, gi_hbm, ga_hbm, gb_hbm, o_hbm, dqkv_hbm, small_out,
                  xb, dyb, gib, posb, wqkv, wo, h_ref, ht_ref, rope_cos, rope_sin, next_cos, next_sin, out_acc, dh_acc,
                  q_next, k_next, v_next, do_next, v_now, do_now, o_now, dqkv_now, o_last, dqkv_last, o_stage, dqkv_stage,
@@ -61,8 +61,7 @@
     seqs, groups = pl.num_programs(0), pl.num_programs(1)
     me = lax.axis_index('sp')
     head_dim, model = dqn_ref.shape[1], dgin_ref.shape[1]
-    gin_ref = gains_ref.at[:, pl.ds(0, model)]
-    qn_ref, kn_ref, freq_ref = (gains_ref.at[:, pl.ds(model + i * head_dim, head_dim)] for i in range(3))
+    q_gain, k_gain, in_gain = (ref[...].astype(F32) for ref in (qn_ref, kn_ref, gin_ref))
     q_cols = o_now.shape[1]
     per_kv = q_cols // head_dim
     seq_len = xb.shape[1]
@@ -142,8 +141,7 @@
         arrive(0, s)
         x = xb[s].astype(F32)
         inv = lax.rsqrt(jnp.mean(x * x, axis=-1, keepdims=True) + EPSILON)
-        h_ref[...] = (x * inv * gin_ref[...]).astype(BF16)
-        arrive(1, s)
+        h_ref[...] = (x * inv * in_gain).astype(BF16)
 
     def project(s, g):
         def q_rows(rows):
@@ -180,7 +178,7 @@
         xb[s] = (x + out_acc[...]).astype(BF16)
         d_norm = dh_acc[...]
         dgin_ref[...] += jnp.sum(d_norm * unit, axis=0, keepdims=True)
-        d_unit = d_norm * gin_ref[...]
+        d_unit = d_norm * in_gain
         grad = inv * (d_unit - unit * jnp.mean(d_unit * unit, axis=-1, keepdims=True))
 
         @pl.when(s >= 2)
@@ -215,7 +213,10 @@
         for copy in weight_loads():
             copy.wait()
         prepare(0)
-        run(project(0, 0))
+        first = project(0, 0)
+        run(first[:4])
+        arrive(1, 0)
+        run(first[4:])
 
     @pl.when(group == 0)
     def _():
@@ -228,6 +229,7 @@
     @pl.when(last_group & (seq < seqs - 1))
     def _():
         prepare(seq + 1)
+        arrive(1, seq + 1)
 
     cos, sin = rope_cos[...], rope_sin[...]
 
@@ -277,8 +279,8 @@
     blocks = len(tiles)
 
     run(behind[:6])
-    k_rot, k_unit, k_inv = norm_rotate(k_next[...], kn_ref[...])
-    q_parts = [norm_rotate(q_next[:, lane], qn_ref[...]) for lane in lanes]
+    k_rot, k_unit, k_inv = norm_rotate(k_next[...], k_gain)
+    q_parts = [norm_rotate(q_next[:, lane], q_gain) for lane in lanes]
     q_tile = [jnp.concatenate([part[0][tile] for part in q_parts], axis=0) for tile in tiles]
     do_tile = [jnp.concatenate([do_now[tile, lane] for lane in lanes], axis=0) for tile in tiles]
     v_cols, k_cols = v_now[...].T, k_rot.T
@@ -320,12 +322,12 @@
     run(ahead[4:])
     for head, lane in enumerate(lanes):
         dq_head = jnp.concatenate([dq[head * ROW_BLOCK:(head + 1) * ROW_BLOCK] for dq in dq_tile], axis=0)
-        dq_head, d_gain = norm_rotate_back(dq_head * scale, q_parts[head][1], q_parts[head][2], qn_ref[...])
+        dq_head, d_gain = norm_rotate_back(dq_head * scale, q_parts[head][1], q_parts[head][2], q_gain)
         dqn_ref[...] += d_gain
         dq_head = dq_head.astype(BF16)
         dqkv_stage[slot, :, lane] = dq_head
         dqkv_now[:, lane] = dq_head
-    dk_head, d_gain = norm_rotate_back(dk_all * scale, k_unit, k_inv, kn_ref[...])
+    dk_head, d_gain = norm_rotate_back(dk_all * scale, k_unit, k_inv, k_gain)
     dkn_ref[...] += d_gain
     dk_head = dk_head.astype(BF16)
     dqkv_stage[slot, :, q_cols:q_cols + head_dim] = dk_head
@@ -568,8 +570,7 @@
         grid=(seqs, groups),
         in_specs=[
             anywhere, anywhere, anywhere, anywhere, anywhere, anywhere, anywhere,
-            pl.BlockSpec(gains.shape, fixed),
-        ],
+        ] + [pl.BlockSpec(t.shape, fixed) for t in gains],
         out_specs=[anywhere] * 6 + [pl.BlockSpec((16, head_dim), fixed)],
         out_shape=[
             bf(batch, piece, model), bf(batch, piece, model),
@@ -606,10 +607,10 @@
             collective_id=0, has_side_effects=True),
         cost_estimate=pl.CostEstimate(flops=flops, bytes_accessed=50_000_000, transcendentals=tokens * seq_len * 8),
         name="block",
-    )(x, dy, pos, w_q, w_k, w_v, w_o, gains)
-
-
-def widen_kernel(ga_ref, gb_ref, small_ref, wq_ref, wk_ref, wv_ref, wo_ref, dgin_ref, dqn_ref, dkn_ref):
+    )(x, dy, pos, w_q, w_k, w_v, w_o, *gains)
+
+
+def widen_kernel(ga_ref, gb_ref, small_ref, out_in, gi_in, wq_ref, wk_ref, wv_ref, wo_ref, dgin_ref, dqn_ref, dkn_ref, out_ref, gi_ref):
     @pl.when(pl.program_id(0) == 0)
     def _():
         lanes = small_ref.shape[1]
@@ -624,27 +625,35 @@
     wq_ref[...] = gb_ref[0, :, :q_cols].astype(F32)
     wk_ref[...] = gb_ref[0, :, q_cols:q_cols + head_dim].astype(F32)
     wv_ref[...] = gb_ref[0, :, q_cols + head_dim:].astype(F32)
-
-
-def widen_call(ga, gb, small):
+    out_ref[...] = out_in[...]
+    gi_ref[...] = gi_in[...]
+
+
+def widen_call(ga, gb, small, out, gi):
     groups, q_cols, model = ga.shape
-    head_dim = (gb.shape[2] - q_cols) // 2
+    width = gb.shape[2]
+    head_dim = (width - q_cols) // 2
+    parts = 2
+    batch, piece, _ = out.shape
     f32 = lambda *shape: jax.ShapeDtypeStruct(shape, F32)
-    across = lambda g: (0, g)
+    across = lambda i: (i % parts, i // parts)
+    fixed = lambda i: (0, 0)
+    act = pl.BlockSpec((batch // (groups * parts), piece, model), lambda i: (i, 0, 0))
     return pl.pallas_call(
         widen_kernel,
-        grid=(groups,),
-        in_specs=[pl.BlockSpec((1, q_cols, model), lambda g: (g, 0, 0)),
-                  pl.BlockSpec((1, model, gb.shape[2]), lambda g: (g, 0, 0)),
-                  pl.BlockSpec(small.shape, lambda g: (0, 0))],
-        out_specs=[pl.BlockSpec((model, q_cols), across), pl.BlockSpec((model, head_dim), across),
-                   pl.BlockSpec((model, head_dim), across), pl.BlockSpec((q_cols, model), lambda g: (g, 0))]
-        + [pl.BlockSpec((1, n), lambda g: (0, 0)) for n in (model, head_dim, head_dim)],
+        grid=(groups * parts,),
+        in_specs=[pl.BlockSpec((1, q_cols // parts, model), lambda i: (i // parts, i % parts, 0)),
+                  pl.BlockSpec((1, model // parts, width), lambda i: (i // parts, i % parts, 0)),
+                  pl.BlockSpec(small.shape, fixed), act, act],
+        out_specs=[pl.BlockSpec((model // parts, q_cols), across), pl.BlockSpec((model // parts, head_dim), across),
+                   pl.BlockSpec((model // parts, head_dim), across), pl.BlockSpec((q_cols // parts, model), lambda i: (i, 0))]
+        + [pl.BlockSpec((1, n), fixed) for n in (model, head_dim, head_dim)] + [act, act],
         out_shape=[f32(model, groups * q_cols), f32(model, groups * head_dim), f32(model, groups * head_dim),
-                   f32(groups * q_cols, model), f32(1, model), f32(1, head_dim), f32(1, head_dim)],
+                   f32(groups * q_cols, model), f32(1, model), f32(1, head_dim), f32(1, head_dim),
+                   jax.ShapeDtypeStruct(out.shape, out.dtype), jax.ShapeDtypeStruct(gi.shape, gi.dtype)],
         compiler_params=pltpu.CompilerParams(dimension_semantics=("arbitrary",)),
         name="widen",
-    )(ga, gb, small)
+    )(ga, gb, small, out, gi)
 
 
 def solution(mesh):
@@ -656,10 +665,10 @@
         head_dim = q_norm.shape[0]
         exponents = jnp.arange(0, head_dim, 2).astype(F32) / head_dim
         inv_freq = jnp.power(ROPE_THETA, -exponents)
-        gains = jnp.concatenate([g_in.astype(F32), q_norm.astype(F32), k_norm.astype(F32), inv_freq, inv_freq])[None]
+        gains = (g_in[None], q_norm[None], k_norm[None], jnp.concatenate([inv_freq, inv_freq])[None])
         pos = jnp.broadcast_to(jnp.pad(positions.astype(F32), ((0, 0), (0, head_dim - seq_dev)))[:, None, :], (batch, 8, head_dim))
         hidden_out, grad_in, ga, gb, _, _, small = block_call(hidden_in, grad_out, pos, gains, w_q, w_k, w_v, w_o, head_dim)
-        grad_wq, grad_wk, grad_wv, grad_wo, dgin, dqn, dkn = widen_call(ga, gb, small)
+        grad_wq, grad_wk, grad_wv, grad_wo, dgin, dqn, dkn, hidden_out, grad_in = widen_call(ga, gb, small, hidden_out, grad_in)
         return hidden_out, grad_in, grad_wq, grad_wk, grad_wv, grad_wo, dgin[0], dqn[0], dkn[0]
 
     return jax.shard_map(shard_body, mesh=mesh,

time: 325 us -> 324 us (level)
  local copies, waits for them, and re-layouts: 10.4 us -> 1.95 us
  Pallas kernels: 313 us -> 320 us
    pallas_call x1, Pallas kernels: 14.1 us -> 21.3 us  [widen_call(): pl.pallas_call(widen_kernel, grid=(groups * parts,), in_specs=[pl.BlockSp...]
    unnamed x4 -> x0, local copies, waits for them, and re-layouts: 7.08 us -> none
where the time goes in v7:
time: 324 us
  Pallas kernels  320 us (99%)
    pallas_call x1, Pallas kernels, block_call(): pl.pallas_call(block_kernel, grid=(seqs, groups), in_specs=[anywhere, any...  298 us
    pallas_call x1, Pallas kernels, widen_call(): pl.pallas_call(widen_kernel, grid=(groups * parts,), in_specs=[pl.BlockSp...  21.3 us

profile of v7, /device:TPU:0, one launch (start us, length us, event | category | flops | bytes accessed | tf_op | source)
XLA Modules:
  0.0 323.6 jit_solution(3492531509739434211)
XLA Ops:
  0.7 0.6 maximum_bitcast_fusion.freq_ref
  1.2 1.3 broadcast_in_dim.19.gin_ref
  2.5 0.7 convert_element_type.10
  3.2 0.7 broadcast_in_dim.18.pos_hbm
  3.9 298.3 %block.1 = (bf16[32,64,1024]{2,1,0:T(8,128)(2,1)}, bf16[32,64,1024]{2,1,0:T(8,128)(2,1)}, bf16[8,256,1024]{2,1,0:T(8,128)(2,1)}, bf16[8,1024,512]{2,1,0:T(8,128)...) custom-call(bf16[32,64,1024]{2,1,0:T(8,128)(2,1)} %x_hbm.1, ...), custom_call_target="tpu_custom_call" | custom-call | flops 77309411328 | bytes 50000000 | tf_op jit(solution)/shard_map/block/pallas_call | solution.py:568
  302.3 21.3 %widen.1 = (f32[1024,2048]{1,0:T(8,128)}, f32[1024,1024]{1,0:T(8,128)}, f32[1024,1024]{1,0:T(8,128)}, f32[2048,1024]{1,0:T(8,128)}, f32[1,1024]{1,0:T(1,128)}, /...) custom-call(bf16[8,256,1024]{2,1,0:T(8,128)(2,1)} %get-tuple-element.23.ga_re, ...), custom_call_target="tpu_custom_call" | custom-call | tf_op jit(solution)/shard_map/widen/pallas_call | solution.py:642
  (2 shorter events, 0.0 us)

commit v8 on v7

--- a/solution.py
+++ b/solution.py
@@ -10,15 +10,14 @@
 ROPE_THETA = 1000000.0
 NEG_LARGE = -1e30
 LOG2_E = 1.4426950408889634
-NT = (((1,), (1,)), ((), ()))
-TN = (((0,), (0,)), ((), ()))
+NN, NT, TN = ((((a,), (b,)), ((), ())) for a, b in ((1, 0), (1, 1), (0, 0)))
 ROW_BLOCK = 256
 DEVICES = 8
 BF16 = jnp.bfloat16
 F32 = jnp.float32
 
 
-def dot(a, b, dims=(((1,), (0,)), ((), ()))):
+def dot(a, b, dims=NN):
     return lax.dot_general(a, b, dims, preferred_element_type=F32)
 
 
@@ -28,6 +27,7 @@
 
 
 X, Y, DIAG, PARTNER = 2, 4, 6, 1
+SEND_ORDER = (2, 4, 6, 3, 5, 7, 1, 0)
 
 
 def chip_peer(me, order):
@@ -187,7 +187,7 @@
 
         gib[s % 2] = (dyb[s].astype(F32) + grad).astype(BF16)
         for kind in range(2):
-            for step in (2, 4, 6, 3, 5, 7, 1, 0):
+            for step in SEND_ORDER:
                 outgoing(kind, s, step).start()
 
     @pl.when((seq == 0) & (group == 0))
@@ -196,7 +196,7 @@
 
         def send_all(s, carry):
             for kind in (2, 0, 1):
-                for step in (2, 4, 6, 3, 5, 7, 1, 0):
+                for step in SEND_ORDER:
                     incoming(kind, s, step).start()
             return carry
 
@@ -565,6 +565,7 @@
     vb = lambda *shape: pltpu.VMEM(shape, BF16)
     vf = lambda *shape: pltpu.VMEM(shape, F32)
     dma = lambda *shape: pltpu.SemaphoreType.DMA(shape)
+    twice = lambda shape: [shape] * 2
     return pl.pallas_call(
         block_kernel,
         grid=(seqs, groups),
@@ -594,13 +595,9 @@
             vb(2, q_cols, model), vb(2, model, width),
             vb(2, q_cols // 2, model), vb(2, model // 2, width),
             vb(2, q_cols, model), vb(2, model, width),
-            pltpu.SemaphoreType.DMA((4, groups)),
-            pltpu.SemaphoreType.DMA((3, seqs, DEVICES)),
-            pltpu.SemaphoreType.DMA((3, seqs, DEVICES)),
-            pltpu.SemaphoreType.DMA((2, seqs, DEVICES)),
-            pltpu.SemaphoreType.DMA((2, seqs, DEVICES)),
-            dma(2, 2), dma(2), dma(2, 4), dma(2, 4), dma(2, 2), dma(2, 2), dma(2, 2, 2), dma(2, 2, 2),
-            dma(2, 2, 7), dma(2, 2, 7), dma(DEVICES), dma(DEVICES),
+            dma(4, groups), *twice(dma(3, seqs, DEVICES)), *twice(dma(2, seqs, DEVICES)),
+            dma(2, 2), dma(2), *twice(dma(2, DEVICES // 2)), *twice(dma(2, 2)), *twice(dma(2, 2, 2)),
+            *twice(dma(2, 2, DEVICES)), *twice(dma(DEVICES)),
         ],
         compiler_params=pltpu.CompilerParams(
             dimension_semantics=("arbitrary", "arbitrary"), vmem_limit_bytes=67_000_000,

time: 324 us -> 324 us (level)
  no operation moved by 1% of the time
where the time goes in v8:
time: 324 us
  Pallas kernels  320 us (99%)
    pallas_call x1, Pallas kernels, block_call(): pl.pallas_call(block_kernel, grid=(seqs, groups), in_specs=[anywhere, any...  298 us
    pallas_call x1, Pallas kernels, widen_call(): pl.pallas_call(widen_kernel, grid=(groups * parts,), in_specs=[pl.BlockSp...  21.3 us

profile of v8, /device:TPU:0, one launch (start us, length us, event | category | flops | bytes accessed | tf_op | source)
XLA Modules:
  0.0 323.7 jit_solution(66227751143165926)
XLA Ops:
  0.7 0.6 maximum_bitcast_fusion.freq_ref
  1.2 1.3 broadcast_in_dim.19.gin_ref
  2.5 0.7 convert_element_type.10
  3.2 0.7 broadcast_in_dim.18.pos_hbm
  3.9 298.4 %block.1 = (bf16[32,64,1024]{2,1,0:T(8,128)(2,1)}, bf16[32,64,1024]{2,1,0:T(8,128)(2,1)}, bf16[8,256,1024]{2,1,0:T(8,128)(2,1)}, bf16[8,1024,512]{2,1,0:T(8,128)...) custom-call(bf16[32,64,1024]{2,1,0:T(8,128)(2,1)} %x_hbm.1, ...), custom_call_target="tpu_custom_call" | custom-call | flops 77309411328 | bytes 50000000 | tf_op jit(solution)/shard_map/block/pallas_call | solution.py:569
  302.3 21.3 %widen.1 = (f32[1024,2048]{1,0:T(8,128)}, f32[1024,1024]{1,0:T(8,128)}, f32[1024,1024]{1,0:T(8,128)}, f32[2048,1024]{1,0:T(8,128)}, f32[1,1024]{1,0:T(1,128)}, /...) custom-call(bf16[8,256,1024]{2,1,0:T(8,128)(2,1)} %get-tuple-element.23.ga_re, ...), custom_call_target="tpu_custom_call" | custom-call | tf_op jit(solution)/shard_map/widen/pallas_call | solution.py:639
  (2 shorter events, 0.0 us)
